TPU v7x, 32 devices: a whole 2x2x4 slice. The times are simulated.
32 devices in a mesh: dp: 8 (over y, x, core), tensor: 4 (over z).
Axes of the slice: x: 2, y: 2, z: 4, core: 2. Of those that a mesh axis runs over, the one named last changes fastest.
Arguments:
- tokens: bfloat16 [16, 320, 1536], P('dp', 'tensor'), may hold values from -6 to 6
- cotangent: bfloat16 [16, 320, 1536], P('dp', 'tensor'), may hold values from -6 to 6
- order: int32 [16, 320], P('dp'), may hold values from 0 to 319, each once within a row
- lengths: int32 [16, 3], P('dp'), may hold values from 1 to 256, 320 in all within a row
- gain_attn: bfloat16 [1536], P('dp'), may hold values from 0.5 to 1.5
- w_query: bfloat16 [1536, 1536], P('dp', 'tensor'), may hold values from -0.15625 to 0.15625
- w_key: bfloat16 [1536, 768], P('dp', 'tensor'), may hold values from -0.15625 to 0.15625
- w_value: bfloat16 [1536, 768], P('dp', 'tensor'), may hold values from -0.15625 to 0.15625
- w_out: bfloat16 [1536, 1536], P('tensor', 'dp'), may hold values from -1.5 to 1.5
- gain_ffn: bfloat16 [1536], P('dp'), may hold values from 0.5 to 1.5
- w_gate: bfloat16 [1536, 4096], P('dp', 'tensor'), may hold values from -0.15625 to 0.15625
- w_up: bfloat16 [1536, 4096], P('dp', 'tensor'), may hold values from -0.15625 to 0.15625
- w_down: bfloat16 [4096, 1536], P('tensor', 'dp'), may hold values from -0.09375 to 0.09375
Outputs:
- output: bfloat16 [16, 320, 1536], P('dp', 'tensor')
- grad_tokens: float32 [16, 320, 1536], P('dp', 'tensor')
- grad_gain_attn: float32 [1536], P('dp')
- grad_query: float32 [1536, 1536], P('dp', 'tensor')
- grad_key: float32 [1536, 768], P('dp', 'tensor')
- grad_value: float32 [1536, 768], P('dp', 'tensor')
- grad_out: float32 [1536, 1536], P('tensor', 'dp')
- grad_gain_ffn: float32 [1536], P('dp')
- grad_gate: float32 [1536, 4096], P('dp', 'tensor')
- grad_up: float32 [1536, 4096], P('dp', 'tensor')
- grad_down: float32 [4096, 1536], P('tensor', 'dp')
Inputs may be any that keep to these rules, and one draw needn't show every extreme that they name: `order`: each row is a permutation of 0 to 319. `lengths`: each row sums to 320; its largest entry is 256; the last document of each stream is padding.
All inputs are finite; a program needn't handle non-finite values.
Results may differ from a plain program's by a relative error of at most 0.012.
Values may be sent and summed in bfloat16 or wider, within the bound.
A program may use at most 128 MiB of HBM per device.

v0:
```python
import jax
import jax.numpy as jnp
from jax import lax
from jax.sharding import PartitionSpec as P

HEAD = 96


eps = 1e-05
rope_base = 100000.0


def rotate(field, cosine, sine):
    half = field.shape[-1] // 2
    first = field[..., :half]
    second = field[..., half:]
    return jnp.concatenate(
        [first * cosine - second * sine, second * cosine + first * sine], axis=-1
    )


def rotate_back(field, cosine, sine):
    half = field.shape[-1] // 2
    first = field[..., :half]
    second = field[..., half:]
    return jnp.concatenate(
        [first * cosine + second * sine, second * cosine - first * sine], axis=-1
    )


def layout(order, lengths):
    starts = jnp.cumsum(lengths, dtype=jnp.int32) - lengths
    docs = jnp.sum((order[:, None] >= starts[None, 1:]).astype(jnp.int32), axis=1, dtype=jnp.int32)
    onehot = docs[:, None] == jnp.arange(lengths.shape[0], dtype=jnp.int32)[None, :]
    first = jnp.sum(jnp.where(onehot, starts[None, :], 0), axis=1, dtype=jnp.int32)
    positions = (order - first).astype(jnp.float32)
    mask = (docs[:, None] == docs[None, :]) & (order[None, :] <= order[:, None])
    real = (docs < lengths.shape[0] - 1).astype(jnp.float32)
    return (positions, mask, real)


def norm_forward(rows, gain):
    scale = lax.rsqrt(jnp.mean(rows * rows, axis=-1, keepdims=True) + eps)
    unit = rows * scale
    return (unit, scale, (unit * gain).astype(jnp.bfloat16))


def norm_backward(grad, unit, scale, gain):
    inner = grad * gain
    return scale * (inner - unit * jnp.mean(inner * unit, axis=-1, keepdims=True))


def contract_rows(left, right):
    return lax.dot_general(
        left, right, (((0,), (0,)), ((), ())), preferred_element_type=jnp.float32
    )


def times_transpose(left, right):
    return lax.dot_general(
        left, right, (((1,), (1,)), ((), ())), preferred_element_type=jnp.float32
    )


def attn_weights(gain_attn, w_query, w_key, w_value, w_out):
    return (
        lax.all_gather(gain_attn, "dp", axis=0, tiled=True),
        lax.all_gather(w_query, "dp", axis=0, tiled=True),
        lax.all_gather(w_key, "dp", axis=0, tiled=True),
        lax.all_gather(w_value, "dp", axis=0, tiled=True),
        lax.all_gather(w_out, "dp", axis=1, tiled=True),
    )


def mlp_weights(gain_ffn, w_gate, w_up, w_down):
    return (
        lax.all_gather(gain_ffn, "dp", axis=0, tiled=True),
        lax.all_gather(w_gate, "dp", axis=0, tiled=True),
        lax.all_gather(w_up, "dp", axis=0, tiled=True),
        lax.all_gather(w_down, "dp", axis=1, tiled=True),
    )


def gather_rows(normed):
    return lax.all_gather(normed, "tensor", axis=0, tiled=True)


def gather_grads(grad_rows):
    return lax.all_gather(grad_rows, "tensor", axis=0, tiled=True)


def scatter_rows(left, right, rows):

    def term(start, size):
        return jnp.dot(left, right, preferred_element_type=jnp.float32)

    return lax.psum_scatter(
        term(jnp.int32(0), rows * lax.axis_size("tensor")),
        "tensor",
        scatter_dimension=0,
        tiled=True,
    )


def scatter_grads(pairs, rows):

    def term(start, size):
        total = None
        for left, right in pairs:
            piece = times_transpose(left, right)
            total = piece if total is None else total + piece
        return total

    return lax.psum_scatter(
        term(jnp.int32(0), rows * lax.axis_size("tensor")),
        "tensor",
        scatter_dimension=0,
        tiled=True,
    )


def reduce_attn(terms):
    return (
        lax.psum_scatter(terms[0], "dp", scatter_dimension=0, tiled=True),
        lax.psum_scatter(terms[1], "dp", scatter_dimension=0, tiled=True),
        lax.psum_scatter(terms[2], "dp", scatter_dimension=0, tiled=True),
        lax.psum_scatter(terms[3], "dp", scatter_dimension=0, tiled=True),
        lax.psum_scatter(terms[4], "dp", scatter_dimension=1, tiled=True),
    )


def reduce_mlp(terms):
    return (
        lax.psum_scatter(terms[0], "dp", scatter_dimension=0, tiled=True),
        lax.psum_scatter(terms[1], "dp", scatter_dimension=0, tiled=True),
        lax.psum_scatter(terms[2], "dp", scatter_dimension=0, tiled=True),
        lax.psum_scatter(terms[3], "dp", scatter_dimension=1, tiled=True),
    )


def local(
    tokens,
    cotangent,
    order,
    lengths,
    gain_attn,
    w_query,
    w_key,
    w_value,
    w_out,
    gain_ffn,
    w_gate,
    w_up,
    w_down,
):
    micro = tokens.shape[0]
    rows = tokens.shape[1]
    seq = rows * lax.axis_size("tensor")
    local_heads = w_query.shape[1] // HEAD
    local_kv = w_key.shape[1] // HEAD
    group = local_heads // local_kv
    first_row = lax.axis_index("tensor") * rows
    freqs = rope_base ** (-2.0 * jnp.arange(HEAD // 2, dtype=jnp.float32) / HEAD)
    head_scale = HEAD ** (-0.5)
    outputs = []
    input_grads = []
    attn_total = None
    mlp_total = None
    for step in range(micro):
        gain1, wq, wk, wv, wo = attn_weights(gain_attn, w_query, w_key, w_value, w_out)
        gain1 = gain1.astype(jnp.float32)
        stream = tokens[step].astype(jnp.float32)
        positions, mask, real = layout(order[step], lengths[step])
        angles = positions[:, None] * freqs[None, :]
        cosine = jnp.cos(angles)[:, None, :]
        sine = jnp.sin(angles)[:, None, :]
        real_rows = lax.dynamic_slice_in_dim(real, first_row, rows, 0)[:, None]
        unit1, scale1, normed1 = norm_forward(stream, gain1)
        full1 = gather_rows(normed1)
        query = jnp.dot(full1, wq, preferred_element_type=jnp.float32).reshape(
            seq, local_heads, HEAD
        )
        query = (
            (rotate(query, cosine, sine) * head_scale)
            .astype(jnp.bfloat16)
            .reshape(seq, local_kv, group, HEAD)
        )
        keys = jnp.dot(full1, wk, preferred_element_type=jnp.float32).reshape(seq, local_kv, HEAD)
        keys = rotate(keys, cosine, sine).astype(jnp.bfloat16)
        values = (
            jnp.dot(full1, wv, preferred_element_type=jnp.float32)
            .astype(jnp.bfloat16)
            .reshape(seq, local_kv, HEAD)
        )
        scores = jnp.einsum("qkgd,skd->kgqs", query, keys, preferred_element_type=jnp.float32)
        scores = jnp.where(mask, scores, -1e30)
        peak = jnp.max(scores, axis=-1, keepdims=True)
        expon = jnp.exp(scores - peak)
        total = jnp.sum(expon, axis=-1, keepdims=True)
        lse = peak + jnp.log(total)
        probs_low = (expon / total).astype(jnp.bfloat16)
        mixed = jnp.einsum("kgqs,skd->qkgd", probs_low, values, preferred_element_type=jnp.float32)
        mixed = mixed.reshape(seq, local_heads * HEAD).astype(jnp.bfloat16)
        branch = scatter_rows(mixed, wo, rows)
        resid = stream + branch
        mlp_set = mlp_weights(gain_ffn, w_gate, w_up, w_down)
        gain2 = mlp_set[0].astype(jnp.float32)
        unit2, scale2, normed2 = norm_forward(resid, gain2)
        full2 = gather_rows(normed2)
        gate = jnp.dot(full2, mlp_set[1], preferred_element_type=jnp.float32)
        upper = jnp.dot(full2, mlp_set[2], preferred_element_type=jnp.float32)
        sigma = jax.nn.sigmoid(gate)
        hidden = (gate * sigma * upper).astype(jnp.bfloat16)
        ffn = scatter_rows(hidden, mlp_set[3], rows)
        outputs.append(((resid + ffn) * real_rows).astype(jnp.bfloat16))
        mlp_set = mlp_weights(gain_ffn, w_gate, w_up, w_down)
        gain2 = mlp_set[0].astype(jnp.float32)
        grad_out_rows = cotangent[step].astype(jnp.float32) * real_rows
        full_grad = gather_grads(grad_out_rows.astype(jnp.bfloat16))
        grad_hidden = times_transpose(full_grad, mlp_set[3])
        term_down = contract_rows(hidden, full_grad)
        grad_gate = (grad_hidden * upper * sigma * (1.0 + gate * (1.0 - sigma))).astype(
            jnp.bfloat16
        )
        grad_up = (grad_hidden * gate * sigma).astype(jnp.bfloat16)
        term_gate = contract_rows(full2, grad_gate)
        term_up = contract_rows(full2, grad_up)
        grad_norm2 = scatter_grads(((grad_gate, mlp_set[1]), (grad_up, mlp_set[2])), rows)
        term_gain2 = jnp.sum(grad_norm2 * unit2, axis=0)
        grad_resid = grad_out_rows + norm_backward(grad_norm2, unit2, scale2, gain2)
        attn_set = attn_weights(gain_attn, w_query, w_key, w_value, w_out)
        gain1 = attn_set[0].astype(jnp.float32)
        full_resid = gather_grads(grad_resid.astype(jnp.bfloat16))
        grad_mixed = times_transpose(full_resid, attn_set[4]).astype(jnp.bfloat16)
        term_out = contract_rows(mixed, full_resid)
        scores = jnp.einsum("qkgd,skd->kgqs", query, keys, preferred_element_type=jnp.float32)
        probs = jnp.where(mask, jnp.exp(scores - lse), 0.0)
        grad_heads = grad_mixed.reshape(seq, local_kv, group, HEAD)
        grad_probs = jnp.einsum(
            "qkgd,skd->kgqs", grad_heads, values, preferred_element_type=jnp.float32
        )
        grad_values = jnp.einsum(
            "kgqs,qkgd->skd",
            probs.astype(jnp.bfloat16),
            grad_heads,
            preferred_element_type=jnp.float32,
        )
        grad_scores = (
            probs * (grad_probs - jnp.sum(probs * grad_probs, axis=-1, keepdims=True))
        ).astype(jnp.bfloat16)
        grad_query = jnp.einsum(
            "kgqs,skd->qkgd", grad_scores, keys, preferred_element_type=jnp.float32
        )
        grad_keys = jnp.einsum(
            "kgqs,qkgd->skd", grad_scores, query, preferred_element_type=jnp.float32
        )
        grad_query = rotate_back(
            grad_query.reshape(seq, local_heads, HEAD) * head_scale, cosine, sine
        )
        grad_query = grad_query.reshape(seq, local_heads * HEAD).astype(jnp.bfloat16)
        grad_keys = (
            rotate_back(grad_keys, cosine, sine).reshape(seq, local_kv * HEAD).astype(jnp.bfloat16)
        )
        grad_values = grad_values.reshape(seq, local_kv * HEAD).astype(jnp.bfloat16)
        term_query = contract_rows(full1, grad_query)
        term_key = contract_rows(full1, grad_keys)
        term_value = contract_rows(full1, grad_values)
        grad_norm1 = scatter_grads(
            ((grad_query, attn_set[1]), (grad_keys, attn_set[2]), (grad_values, attn_set[3])), rows
        )
        term_gain1 = jnp.sum(grad_norm1 * unit1, axis=0)
        input_grads.append(grad_resid + norm_backward(grad_norm1, unit1, scale1, gain1))
        attn_terms = (term_gain1, term_query, term_key, term_value, term_out)
        mlp_terms = (term_gain2, term_gate, term_up, term_down)
        if step == 0:
            attn_total = attn_terms
            mlp_total = mlp_terms
        else:
            attn_total = jax.tree.map(jnp.add, attn_total, attn_terms)
            mlp_total = jax.tree.map(jnp.add, mlp_total, mlp_terms)
    attn_final = reduce_attn(attn_total)
    mlp_final = reduce_mlp(mlp_total)
    gain_one, gain_two = lax.psum((attn_final[0], mlp_final[0]), "tensor")
    output = jnp.stack(outputs, axis=0)
    grad_tokens = jnp.stack(input_grads, axis=0)
    return (
        output,
        grad_tokens,
        gain_one,
        attn_final[1],
        attn_final[2],
        attn_final[3],
        attn_final[4],
        gain_two,
        mlp_final[1],
        mlp_final[2],
        mlp_final[3],
    )


def solution(mesh):
    return jax.shard_map(
        local,
        mesh=mesh,
        in_specs=(
            P("dp", "tensor", None),
            P("dp", "tensor", None),
            P("dp", None),
            P("dp", None),
            P("dp"),
            P("dp", "tensor"),
            P("dp", "tensor"),
            P("dp", "tensor"),
            P("tensor", "dp"),
            P("dp"),
            P("dp", "tensor"),
            P("dp", "tensor"),
            P("tensor", "dp"),
        ),
        out_specs=(
            P("dp", "tensor", None),
            P("dp", "tensor", None),
            P("dp"),
            P("dp", "tensor"),
            P("dp", "tensor"),
            P("dp", "tensor"),
            P("tensor", "dp"),
            P("dp"),
            P("dp", "tensor"),
            P("dp", "tensor"),
            P("tensor", "dp"),
        ),
        check_vma=False,
    )
```

profile of v0, /device:TPU:0, one launch (start us, length us, event | category | flops | bytes accessed | tf_op | source)
XLA Modules:
  0.0 1036.9 jit_solution(287252882085585098)
XLA Ops:
  16.5 16.1 %all-reduce.6 = (bf16[1536]{0:T(1024)(128)(2,1)S(1)}, bf16[1536]{0:T(1024)(128)(2,1)}) all-reduce(bf16[1536]{0:T(1024)(128)(2,1)S(1)} %dynamic-update-slice, bf16[1536]{0:T(1024)(128)(2,1)S(1)} %dynamic-update-slice.1), channel_id=1, replica_groups=mesh['dp'=8,'tensor'=4] {'dp'}, use_global_device_ids=true, to_apply=%add | all-reduce | flops 3072 | bytes 12288
  34.6 9.8 all_gather.37
  45.3 22.3 %all_gather.89 = bf16[320,1536]{1,0:T(8,128)(2,1)S(1)} all-gather(bf16[80,1536]{1,0:T(8,128)(2,1)S(1)} %get-tuple-element.58), channel_id=1, replica_groups=mesh['dp'=8,'tensor'=4] {'tensor'}, dimensions={0}, use_global_device_ids=true | all-gather | bytes 1228800 | tf_op jit(solution)/shard_map/all_gather | solution.py:85
  69.4 10.0 all_gather.36
  89.7 36.3 %all_gather.35 = bf16[320,1536]{1,0:T(8,128)(2,1)S(1)} all-gather(bf16[80,1536]{1,0:T(8,128)(2,1)} %get-tuple-element.57), channel_id=1, replica_groups=mesh['dp'=8,'tensor'=4] {'tensor'}, dimensions={0}, use_global_device_ids=true | all-gather | bytes 1228800 | tf_op jit(solution)/shard_map/all_gather | solution.py:85
  138.2 26.7 %all_gather.91 = bf16[320,1536]{1,0:T(8,128)(2,1)} all-gather(bf16[80,1536]{1,0:T(8,128)(2,1)S(1)} %get-tuple-element.61), channel_id=1, replica_groups=mesh['dp'=8,'tensor'=4] {'tensor'}, dimensions={0}, use_global_device_ids=true | all-gather | bytes 1228800 | tf_op jit(solution)/shard_map/all_gather | solution.py:89
  165.0 26.6 %reduce-scatter.16.cloned.1.call-done = f32[80,1536]{1,0:T(8,128)} async-done(((f32[320,1536]{1,0:T(8,128)}), f32[80,1536]{1,0:T(8,128)}) %reduce-scatter.16.cloned.1.call-update) | async-done | bytes 491536 | tf_op jit(solution)/shard_map/reduce_scatter | solution.py:97
  195.4 22.5 %all_gather.41 = bf16[320,1536]{1,0:T(8,128)(2,1)} all-gather(bf16[80,1536]{1,0:T(8,128)(2,1)S(1)} %multiply_convert_fusion.9), channel_id=1, replica_groups=mesh['dp'=8,'tensor'=4] {'tensor'}, dimensions={0}, use_global_device_ids=true | all-gather | bytes 1228800 | tf_op jit(solution)/shard_map/all_gather | solution.py:85
  217.9 7.9 all-gather.12.cloned.1.call-done
  230.2 29.5 %all-gather.10.cloned.1.call-done = bf16[1536,1024]{1,0:T(8,128)(2,1)} async-done(((bf16[192,1024]{1,0:T(8,128)(2,1)}), bf16[1536,1024]{1,0:T(8,128)(2,1)}) %all-gather.10.cloned.1.call-update) | async-done | bytes 3145744 | tf_op jit(solution)/shard_map/all_gather | solution.py:78
  264.2 29.6 %all-gather.14.cloned.1.call-done = bf16[1024,1536]{0,1:T(8,128)(2,1)} async-done(((bf16[1024,192]{0,1:T(8,128)(2,1)}), bf16[1024,1536]{0,1:T(8,128)(2,1)}) %all-gather.14.cloned.1.call-update) | async-done | bytes 3145744 | tf_op jit(solution)/shard_map/all_gather | solution.py:80
  293.8 5.5 multiply_convert_fusion.2
  304.4 35.7 %all_gather.93 = bf16[320,1536]{1,0:T(8,128)(2,1)} all-gather(bf16[80,1536]{1,0:T(8,128)(2,1)} %get-tuple-element.62), channel_id=1, replica_groups=mesh['dp'=8,'tensor'=4] {'tensor'}, dimensions={0}, use_global_device_ids=true | all-gather | bytes 1228800 | tf_op jit(solution)/shard_map/all_gather | solution.py:89
  341.2 17.6 %reduce-scatter.24.cloned.1.call-done = f32[80,1536]{1,0:T(8,128)} async-done(((f32[320,1536]{1,0:T(8,128)}), f32[80,1536]{1,0:T(8,128)}) %reduce-scatter.24.cloned.1.call-update) | async-done | bytes 491536 | tf_op jit(solution)/shard_map/reduce_scatter | solution.py:114
  361.0 21.8 %all_gather.90 = bf16[320,1536]{1,0:T(8,128)(2,1)S(1)} all-gather(bf16[80,1536]{1,0:T(8,128)(2,1)S(1)} %get-tuple-element.73), channel_id=1, replica_groups=mesh['dp'=8,'tensor'=4] {'tensor'}, dimensions={0}, use_global_device_ids=true | all-gather | bytes 1228800 | tf_op jit(solution)/shard_map/all_gather | solution.py:85
  396.1 4.6 fusion.94
  400.8 4.8 fusion.100
  408.2 28.6 %reduce-scatter.28.cloned.1.call-done = f32[80,1536]{1,0:T(8,128)} async-done(((f32[320,1536]{1,0:T(8,128)}), f32[80,1536]{1,0:T(8,128)}) %reduce-scatter.28.cloned.1.call-update) | async-done | bytes 491536 | tf_op jit(solution)/shard_map/reduce_scatter | solution.py:114
  439.2 40.4 %reduce-scatter.18.cloned.1.call-done = f32[80,1536]{1,0:T(8,128)} async-done(((f32[320,1536]{1,0:T(8,128)}), f32[80,1536]{1,0:T(8,128)}) %reduce-scatter.18.cloned.1.call-update) | async-done | bytes 491536 | tf_op jit(solution)/shard_map/reduce_scatter | solution.py:97
  479.7 43.1 %reduce-scatter.22.cloned.1.call-done = f32[80,1536]{1,0:T(8,128)} async-done(((f32[320,1536]{1,0:T(8,128)}), f32[80,1536]{1,0:T(8,128)}) %reduce-scatter.22.cloned.1.call-update) | async-done | bytes 491536 | tf_op jit(solution)/shard_map/reduce_scatter | solution.py:97
  526.4 20.4 %all_gather.94 = bf16[320,1536]{1,0:T(8,128)(2,1)S(1)} all-gather(bf16[80,1536]{1,0:T(8,128)(2,1)S(1)} %get-tuple-element.55), channel_id=1, replica_groups=mesh['dp'=8,'tensor'=4] {'tensor'}, dimensions={0}, use_global_device_ids=true | all-gather | bytes 1228800 | tf_op jit(solution)/shard_map/all_gather | solution.py:89
  560.8 33.4 %all_gather.92 = bf16[320,1536]{1,0:T(8,128)(2,1)S(1)} all-gather(bf16[80,1536]{1,0:T(8,128)(2,1)} %get-tuple-element.31), channel_id=1, replica_groups=mesh['dp'=8,'tensor'=4] {'tensor'}, dimensions={0}, use_global_device_ids=true | all-gather | bytes 1228800 | tf_op jit(solution)/shard_map/all_gather | solution.py:89
  635.5 4.6 convolution_add_fusion.1
  649.5 7.5 reduce-scatter.26.cloned.1.call-done
  658.6 23.6 %all-reduce.4 = (f32[1536]{0:T(1024)S(1)}, f32[1536]{0:T(1024)S(1)}) all-reduce(f32[1536]{0:T(1024)S(1)} %add.228, f32[1536]{0:T(1024)S(1)} %add.233), channel_id=10, replica_groups=mesh['dp'=8,'tensor'=4] {'dp'}, use_global_device_ids=true, to_apply=%region_30.31.clone | all-reduce | flops 3072 | bytes 24576
  682.4 10.6 %all-reduce.5 = (f32[192]{0:T(256)}, f32[192]{0:T(256)}) all-reduce(f32[192]{0:T(256)S(1)} %dynamic-slice.3, f32[192]{0:T(256)S(1)} %dynamic-slice.5), channel_id=1, replica_groups=mesh['dp'=8,'tensor'=4] {'tensor'}, use_global_device_ids=true, to_apply=%region_31.32 | all-reduce | flops 384 | bytes 3072 | tf_op jit(solution)/shard_map/psum | solution.py:283
  698.2 42.1 %reduce-scatter.36.cloned.1.call-done = f32[192,192]{1,0:T(8,128)} async-done(((f32[1536,192]{1,0:T(8,128)}), f32[192,192]{1,0:T(8,128)}) %reduce-scatter.36.cloned.1.call-update) | async-done | bytes 147472 | tf_op jit(solution)/shard_map/reduce_scatter | solution.py:127
  740.3 46.1 %reduce-scatter.38.cloned.1.call-done = f32[384,192]{0,1:T(8,128)} async-done(((f32[384,1536]{0,1:T(8,128)}), f32[384,192]{0,1:T(8,128)}) %reduce-scatter.38.cloned.1.call-update) | async-done | bytes 294928 | tf_op jit(solution)/shard_map/reduce_scatter | solution.py:128
  786.4 46.1 %reduce-scatter.32.cloned.1.call-done = f32[192,384]{1,0:T(8,128)} async-done(((f32[1536,384]{1,0:T(8,128)}), f32[192,384]{1,0:T(8,128)}) %reduce-scatter.32.cloned.1.call-update) | async-done | bytes 294928 | tf_op jit(solution)/shard_map/reduce_scatter | solution.py:125
  832.6 65.6 %reduce-scatter.44.cloned.1.call-done = f32[1024,192]{0,1:T(8,128)} async-done(((f32[1024,1536]{0,1:T(8,128)}), f32[1024,192]{0,1:T(8,128)}) %reduce-scatter.44.cloned.1.call-update) | async-done | bytes 786448 | tf_op jit(solution)/shard_map/reduce_scatter | solution.py:137
  898.2 65.7 %reduce-scatter.42.cloned.1.call-done = f32[192,1024]{1,0:T(8,128)} async-done(((f32[1536,1024]{1,0:T(8,128)}), f32[192,1024]{1,0:T(8,128)}) %reduce-scatter.42.cloned.1.call-update) | async-done | bytes 786448 | tf_op jit(solution)/shard_map/reduce_scatter | solution.py:136
  963.9 65.6 %reduce-scatter.40.cloned.1.call-done = f32[192,1024]{1,0:T(8,128)} async-done(((f32[1536,1024]{1,0:T(8,128)}), f32[192,1024]{1,0:T(8,128)}) %reduce-scatter.40.cloned.1.call-update) | async-done | bytes 786448 | tf_op jit(solution)/shard_map/reduce_scatter | solution.py:135
  (381 shorter events, 148.1 us)
Async XLA Ops:
  7.2 37.2 %copy-start.5 = (bf16[2,80,1536]{2,1,0:T(8,128)(2,1)S(1)}, bf16[2,80,1536]{2,1,0:T(8,128)(2,1)}, u32[]{:S(2)}) copy-start(bf16[2,80,1536]{2,1,0:T(8,128)(2,1)} %param.13) | copy-start | bytes 1474564
  7.2 74.2 %all-gather.6.cloned.1.call-start = ((), (), s32[]{:S(2)}) async-start(), calls=%async_computation.15 | async-start | bytes 1327104 | tf_op jit(solution)/shard_map/all_gather | solution.py:68
  7.9 78.3 %all-gather.8.cloned.1.call-start = ((), (), s32[]{:S(2)}) async-start(), calls=%async_computation.16 | async-start | bytes 1327104 | tf_op jit(solution)/shard_map/all_gather | solution.py:71
  8.7 156.3 %reduce-scatter.20.cloned.1.call-start = ((), (), s32[]{:S(2)}) async-start(), calls=%async_computation.22 | async-start | bytes 2457600 | tf_op jit(solution)/shard_map/reduce_scatter | solution.py:97
  33.4 11.8 %copy-start.88 = (s32[320]{0:T(512)}, s32[320]{0:T(512)S(1)}, u32[]{:S(2)}) copy-start(s32[320]{0:T(512)S(1)} %fusion.64) | copy-start | bytes 3844
  34.5 50.1 %copy-start.23 = (pred[320,320]{0,1:T(8,128)(4,1)}, pred[320,320]{0,1:T(8,128)(4,1)S(1)}, u32[]{:S(2)}) copy-start(pred[320,320]{0,1:T(8,128)(4,1)S(1)} %get-tuple-element.98) | copy-start | bytes 307204
  45.2 24.2 %copy-start.84 = (bf16[192,192]{1,0:T(8,128)(2,1)S(1)}, bf16[192,192]{1,0:T(8,128)(2,1)}, u32[]{:S(2)}) copy-start(bf16[192,192]{1,0:T(8,128)(2,1)} %param.20) | copy-start | bytes 221188
  69.4 14.1 %copy-start.43 = (f32[320,48]{0,1:T(8,128)}, f32[320,48]{0,1:T(8,128)S(1)}, u32[]{:S(2)}) copy-start(f32[320,48]{0,1:T(8,128)S(1)} %get-tuple-element.86) | copy-start | bytes 184324
  69.4 14.1 %copy-start.45 = (f32[320,48]{0,1:T(8,128)}, f32[320,48]{0,1:T(8,128)S(1)}, u32[]{:S(2)}) copy-start(f32[320,48]{0,1:T(8,128)S(1)} %get-tuple-element.87) | copy-start | bytes 184324
  89.7 101.9 %reduce-scatter.16.cloned.1.call-start = ((), (), s32[]{:S(2)}) async-start(), calls=%async_computation.17 | async-start | bytes 2457600 | tf_op jit(solution)/shard_map/reduce_scatter | solution.py:97
  89.7 36.9 %copy-start.39 = (f32[320,48]{0,1:T(8,128)S(1)}, f32[320,48]{0,1:T(8,128)}, u32[]{:S(2)}) copy-start(f32[320,48]{0,1:T(8,128)} %get-tuple-element.74) | copy-start | bytes 184324
  89.7 36.9 %copy-start.41 = (f32[320,48]{0,1:T(8,128)S(1)}, f32[320,48]{0,1:T(8,128)}, u32[]{:S(2)}) copy-start(f32[320,48]{0,1:T(8,128)} %get-tuple-element.75) | copy-start | bytes 184324
  133.5 92.3 %all-gather.12.cloned.1.call-start = ((), (), s32[]{:S(2)}) async-start(), calls=%async_computation.19 | async-start | bytes 3538944 | tf_op jit(solution)/shard_map/all_gather | solution.py:79
  134.1 125.7 %all-gather.10.cloned.1.call-start = ((), (), s32[]{:S(2)}) async-start(), calls=%async_computation.18 | async-start | bytes 3538944 | tf_op jit(solution)/shard_map/all_gather | solution.py:78
  134.7 159.2 %all-gather.14.cloned.1.call-start = ((), (), s32[]{:S(2)}) async-start(), calls=%async_computation.20 | async-start | bytes 3538944 | tf_op jit(solution)/shard_map/all_gather | solution.py:80
  135.4 223.4 %reduce-scatter.24.cloned.1.call-start = ((), (), s32[]{:S(2)}) async-start(), calls=%async_computation.24 | async-start | bytes 2457600 | tf_op jit(solution)/shard_map/reduce_scatter | solution.py:114
  304.3 132.5 %reduce-scatter.28.cloned.1.call-start = ((), (), s32[]{:S(2)}) async-start(), calls=%async_computation.26 | async-start | bytes 2457600 | tf_op jit(solution)/shard_map/reduce_scatter | solution.py:114
  396.1 83.6 %reduce-scatter.18.cloned.1.call-start = ((), (), s32[]{:S(2)}) async-start(), calls=%async_computation.21 | async-start | bytes 2457600 | tf_op jit(solution)/shard_map/reduce_scatter | solution.py:97
  400.8 122.0 %reduce-scatter.22.cloned.1.call-start = ((), (), s32[]{:S(2)}) async-start(), calls=%async_computation.23 | async-start | bytes 2457600 | tf_op jit(solution)/shard_map/reduce_scatter | solution.py:97
  405.6 243.8 %reduce-scatter.30.cloned.1.call-start = ((), (), s32[]{:S(2)}) async-start(), calls=%async_computation.27 | async-start | bytes 2457600 | tf_op jit(solution)/shard_map/reduce_scatter | solution.py:114
  522.7 25.1 %copy-start.14 = (bf16[384,1536]{0,1:T(8,128)(2,1)S(1)}, bf16[384,1536]{0,1:T(8,128)(2,1)}, u32[]{:S(2)}) copy-start(bf16[384,1536]{0,1:T(8,128)(2,1)} %all-gather.8.cloned.1.call-done) | copy-start | bytes 3538948
  526.4 24.6 %copy-start.85 = (f32[2,2,320]{2,1,0:T(2,128)S(1)}, f32[2,2,320]{2,1,0:T(2,128)}, u32[]{:S(2)}) copy-start(f32[2,2,320]{2,1,0:T(2,128)} %log_add_fusion) | copy-start | bytes 15364
  560.1 96.9 %reduce-scatter.26.cloned.1.call-start = ((), (), s32[]{:S(2)}) async-start(), calls=%async_computation.25 | async-start | bytes 2457600 | tf_op jit(solution)/shard_map/reduce_scatter | solution.py:114
  609.1 89.1 %reduce-scatter.34.cloned.1.call-start = ((), (), s32[]{:S(2)}) async-start(), calls=%async_computation.29 | async-start | bytes 1769472 | tf_op jit(solution)/shard_map/reduce_scatter | solution.py:126
  612.5 127.8 %reduce-scatter.36.cloned.1.call-start = ((), (), s32[]{:S(2)}) async-start(), calls=%async_computation.30 | async-start | bytes 1769472 | tf_op jit(solution)/shard_map/reduce_scatter | solution.py:127
  615.2 171.2 %reduce-scatter.38.cloned.1.call-start = ((), (), s32[]{:S(2)}) async-start(), calls=%async_computation.31 | async-start | bytes 2654208 | tf_op jit(solution)/shard_map/reduce_scatter | solution.py:128
  620.2 212.4 %reduce-scatter.32.cloned.1.call-start = ((), (), s32[]{:S(2)}) async-start(), calls=%async_computation.28 | async-start | bytes 2654208 | tf_op jit(solution)/shard_map/reduce_scatter | solution.py:125
  624.6 273.6 %reduce-scatter.44.cloned.1.call-start = ((), (), s32[]{:S(2)}) async-start(), calls=%async_computation.34 | async-start | bytes 7077888 | tf_op jit(solution)/shard_map/reduce_scatter | solution.py:137
  632.3 331.6 %reduce-scatter.42.cloned.1.call-start = ((), (), s32[]{:S(2)}) async-start(), calls=%async_computation.33 | async-start | bytes 7077888 | tf_op jit(solution)/shard_map/reduce_scatter | solution.py:136
  640.1 389.4 %reduce-scatter.40.cloned.1.call-start = ((), (), s32[]{:S(2)}) async-start(), calls=%async_computation.32 | async-start | bytes 7077888 | tf_op jit(solution)/shard_map/reduce_scatter | solution.py:135
  647.6 45.4 %copy-start.37 = (f32[80,1536]{1,0:T(8,128)S(1)}, f32[80,1536]{1,0:T(8,128)}, u32[]{:S(2)}) copy-start(f32[80,1536]{1,0:T(8,128)} %get-tuple-element.32) | copy-start | bytes 1474564
  647.6 45.4 %copy-start.38 = (f32[80,1536]{1,0:T(8,128)S(1)}, f32[80,1536]{1,0:T(8,128)}, u32[]{:S(2)}) copy-start(f32[80,1536]{1,0:T(8,128)} %get-tuple-element.56) | copy-start | bytes 1474564
  (96 other events, 199.4 us)
Sparse Core Ops, SparseCore 0:
  9.9 26.7 all-gather.5
  38.6 23.9 all-gather.7
  89.8 53.7 reduce-scatter.19
  145.8 45.7 reduce-scatter.15
  193.3 32.4 all-gather.11
  227.5 32.1 all-gather.9
  261.6 32.1 all-gather.13
  304.4 54.3 reduce-scatter.23
  396.2 40.5 reduce-scatter.27
  439.0 40.6 reduce-scatter.17
  482.0 40.6 reduce-scatter.21
  560.2 51.7 reduce-scatter.29
  614.3 42.6 reduce-scatter.25
  660.7 37.4 reduce-scatter.33
  701.9 38.3 reduce-scatter.35
  744.1 42.3 reduce-scatter.37
  790.2 42.3 reduce-scatter.31
  836.4 61.7 reduce-scatter.43
  902.1 61.7 reduce-scatter.41
  967.7 61.7 reduce-scatter.39
where the time goes:
time: 1040 us
  waiting for transfers between devices  568 us (55%)
  blocking collectives  289 us (28%)
  matrix products  102 us (10%)
  other arithmetic  32.7 us (3%)
  local copies, waits for them, and re-layouts  25.6 us (2%)
  between operations  17.6 us (2%)
    all_gather x4, blocking collectives, gather_grads(): return lax.all_gather(grad_rows, 'tensor', axis=0, tiled=True)  116 us
    reduce_scatter x4, waiting for transfers between devices, scatter_rows(): lax.psum_scatter(term(jnp.int32(0), rows * lax.axis_size('tensor')), 'ten...  110 us
    all_gather x4, blocking collectives, gather_rows(): return lax.all_gather(normed, 'tensor', axis=0, tiled=True)  103 us
    reduce_scatter x1, waiting for transfers between devices, reduce_mlp(): lax.psum_scatter(terms[2], 'dp', scatter_dimension=0, tiled=True)  65.7 us
    reduce_scatter x1, waiting for transfers between devices, reduce_mlp(): lax.psum_scatter(terms[3], 'dp', scatter_dimension=1, tiled=True)  65.6 us
    reduce_scatter x1, waiting for transfers between devices, reduce_mlp(): lax.psum_scatter(terms[1], 'dp', scatter_dimension=0, tiled=True)  65.6 us
    reduce_scatter x4, waiting for transfers between devices, scatter_grads(): lax.psum_scatter(term(jnp.int32(0), rows * lax.axis_size('tensor')), 'ten...  53.8 us
    reduce_scatter x1, waiting for transfers between devices, reduce_attn(): lax.psum_scatter(terms[4], 'dp', scatter_dimension=1, tiled=True)  46.1 us
  transfers between devices with their start and end apart: 20, of which 16 were waited for; matrix products, arithmetic and copies ran while one was open for 10% of the time, Pallas kernels for 0%

commit v1 on v0

v1 whole, which is shorter than its diff:
```python
import jax
import jax.numpy as jnp
from jax import lax
from jax.sharding import PartitionSpec as P

HEAD = 96


eps = 1e-05
rope_base = 100000.0


def rotate(field, cosine, sine):
    half = field.shape[-1] // 2
    first = field[..., :half]
    second = field[..., half:]
    return jnp.concatenate(
        [first * cosine - second * sine, second * cosine + first * sine], axis=-1
    )


def rotate_back(field, cosine, sine):
    half = field.shape[-1] // 2
    first = field[..., :half]
    second = field[..., half:]
    return jnp.concatenate(
        [first * cosine + second * sine, second * cosine - first * sine], axis=-1
    )


def layout(order, lengths):
    starts = jnp.cumsum(lengths, dtype=jnp.int32) - lengths
    docs = jnp.sum((order[:, None] >= starts[None, 1:]).astype(jnp.int32), axis=1, dtype=jnp.int32)
    onehot = docs[:, None] == jnp.arange(lengths.shape[0], dtype=jnp.int32)[None, :]
    first = jnp.sum(jnp.where(onehot, starts[None, :], 0), axis=1, dtype=jnp.int32)
    positions = (order - first).astype(jnp.float32)
    mask = (docs[:, None] == docs[None, :]) & (order[None, :] <= order[:, None])
    real = (docs < lengths.shape[0] - 1).astype(jnp.float32)
    return (positions, mask, real)


def norm_forward(rows, gain):
    scale = lax.rsqrt(jnp.mean(rows * rows, axis=-1, keepdims=True) + eps)
    unit = rows * scale
    return (unit, scale, (unit * gain).astype(jnp.bfloat16))


def norm_backward(grad, unit, scale, gain):
    inner = grad * gain
    return scale * (inner - unit * jnp.mean(inner * unit, axis=-1, keepdims=True))


def contract_rows(left, right):
    return lax.dot_general(
        left, right, (((0,), (0,)), ((), ())), preferred_element_type=jnp.float32
    )


def times_transpose(left, right):
    return lax.dot_general(
        left, right, (((1,), (1,)), ((), ())), preferred_element_type=jnp.float32
    )


def gather_weights(gain_attn, w_query, w_key, w_value, w_out, gain_ffn, w_gate, w_up, w_down):
    gains = lax.all_gather(jnp.stack([gain_attn, gain_ffn], axis=0), "dp", axis=1, tiled=True)
    attn = lax.all_gather(
        jnp.concatenate([w_query, w_key, w_value, w_out.T], axis=1), "dp", axis=0, tiled=True
    )
    gate_up = lax.all_gather(jnp.concatenate([w_gate, w_up], axis=1), "dp", axis=0, tiled=True)
    down = lax.all_gather(w_down.T, "dp", axis=0, tiled=True)
    return gains, attn, gate_up, down


def gather_rows(rows):
    return lax.all_gather(rows, "tensor", axis=1, tiled=True)


def scatter_rows(partial):
    low = partial.astype(jnp.bfloat16)
    return lax.psum_scatter(low, "tensor", scatter_dimension=1, tiled=True).astype(jnp.float32)


def reduce_weights(term):
    low = term.astype(jnp.bfloat16)
    return lax.psum_scatter(low, "dp", scatter_dimension=0, tiled=True).astype(jnp.float32)


def local(
    tokens,
    cotangent,
    order,
    lengths,
    gain_attn,
    w_query,
    w_key,
    w_value,
    w_out,
    gain_ffn,
    w_gate,
    w_up,
    w_down,
):
    micro, rows, width = tokens.shape
    seq = rows * lax.axis_size("tensor")
    q_cols, k_cols, ff_cols = w_query.shape[1], w_key.shape[1], w_gate.shape[1]
    local_heads, local_kv = q_cols // HEAD, k_cols // HEAD
    group = local_heads // local_kv
    first_row = lax.axis_index("tensor") * rows
    freqs = rope_base ** (-2.0 * jnp.arange(HEAD // 2, dtype=jnp.float32) / HEAD)
    head_scale = HEAD ** (-0.5)

    gains, attn, gate_up, down = gather_weights(
        gain_attn, w_query, w_key, w_value, w_out, gain_ffn, w_gate, w_up, w_down
    )
    gain1, gain2 = gains[0].astype(jnp.float32), gains[1].astype(jnp.float32)
    in_cols = q_cols + 2 * k_cols
    w_in, w_out_t = attn[:, :in_cols], attn[:, in_cols:]

    positions, mask, real = jax.vmap(layout)(order, lengths)
    angles = positions[:, :, None] * freqs
    cosine, sine = jnp.cos(angles)[:, :, None, :], jnp.sin(angles)[:, :, None, :]
    mask = mask[:, None, None]
    real_rows = lax.dynamic_slice_in_dim(real, first_row, rows, 1)[:, :, None]

    stream = tokens.astype(jnp.float32)
    unit1, scale1, normed1 = norm_forward(stream, gain1)
    full1 = gather_rows(normed1)
    grad_out_rows = cotangent.astype(jnp.float32) * real_rows
    full_grad = gather_rows(grad_out_rows.astype(jnp.bfloat16))
    flat1 = full1.reshape(micro * seq, width)
    flat_grad = full_grad.reshape(micro * seq, width)

    mixed_in = jnp.dot(flat1, w_in, preferred_element_type=jnp.float32).reshape(micro, seq, in_cols)
    query = mixed_in[..., :q_cols].reshape(micro, seq, local_heads, HEAD)
    keys = mixed_in[..., q_cols : q_cols + k_cols].reshape(micro, seq, local_kv, HEAD)
    values = mixed_in[..., q_cols + k_cols :].reshape(micro, seq, local_kv, HEAD).astype(jnp.bfloat16)
    query = (rotate(query, cosine, sine) * head_scale).astype(jnp.bfloat16)
    query = query.reshape(micro, seq, local_kv, group, HEAD)
    keys = rotate(keys, cosine, sine).astype(jnp.bfloat16)
    scores = jnp.einsum("bqkgd,bskd->bkgqs", query, keys, preferred_element_type=jnp.float32)
    scores = jnp.where(mask, scores, -1e30)
    peak = jnp.max(scores, axis=-1, keepdims=True)
    expon = jnp.exp(scores - peak)
    total = jnp.sum(expon, axis=-1, keepdims=True)
    probs = expon / total
    probs_low = probs.astype(jnp.bfloat16)
    mixed = jnp.einsum("bkgqs,bskd->bqkgd", probs_low, values, preferred_element_type=jnp.float32)
    mixed = mixed.reshape(micro * seq, q_cols).astype(jnp.bfloat16)
    branch = scatter_rows(times_transpose(mixed, w_out_t).reshape(micro, seq, width))
    resid = stream + branch
    unit2, scale2, normed2 = norm_forward(resid, gain2)
    full2 = gather_rows(normed2).reshape(micro * seq, width)

    both = jnp.dot(full2, gate_up, preferred_element_type=jnp.float32)
    gate, upper = both[:, :ff_cols], both[:, ff_cols:]
    sigma = jax.nn.sigmoid(gate)
    hidden = (gate * sigma * upper).astype(jnp.bfloat16)
    ffn = scatter_rows(times_transpose(hidden, down).reshape(micro, seq, width))
    output = ((resid + ffn) * real_rows).astype(jnp.bfloat16)

    grad_hidden = jnp.dot(flat_grad, down, preferred_element_type=jnp.float32)
    grad_gate = (grad_hidden * upper * sigma * (1.0 + gate * (1.0 - sigma))).astype(jnp.bfloat16)
    grad_up = (grad_hidden * gate * sigma).astype(jnp.bfloat16)
    grad_both = jnp.concatenate([grad_gate, grad_up], axis=1)
    grad_norm2 = scatter_rows(times_transpose(grad_both, gate_up).reshape(micro, seq, width))
    final_down = reduce_weights(contract_rows(flat_grad, hidden))
    final_gate = reduce_weights(contract_rows(full2, grad_gate))
    final_up = reduce_weights(contract_rows(full2, grad_up))
    term_gain2 = jnp.sum(grad_norm2 * unit2, axis=(0, 1))
    grad_resid = grad_out_rows + norm_backward(grad_norm2, unit2, scale2, gain2)

    full_resid = gather_rows(grad_resid.astype(jnp.bfloat16)).reshape(micro * seq, width)
    grad_mixed = jnp.dot(full_resid, w_out_t, preferred_element_type=jnp.float32).astype(jnp.bfloat16)
    final_out = reduce_weights(contract_rows(full_resid, mixed))
    grad_heads = grad_mixed.reshape(micro, seq, local_kv, group, HEAD)
    grad_probs = jnp.einsum(
        "bqkgd,bskd->bkgqs", grad_heads, values, preferred_element_type=jnp.float32
    )
    grad_values = jnp.einsum(
        "bkgqs,bqkgd->bskd", probs_low, grad_heads, preferred_element_type=jnp.float32
    )
    grad_scores = (
        probs * (grad_probs - jnp.sum(probs * grad_probs, axis=-1, keepdims=True))
    ).astype(jnp.bfloat16)
    grad_query = jnp.einsum(
        "bkgqs,bskd->bqkgd", grad_scores, keys, preferred_element_type=jnp.float32
    ).reshape(micro, seq, local_heads, HEAD)
    grad_keys = jnp.einsum(
        "bkgqs,bqkgd->bskd", grad_scores, query, preferred_element_type=jnp.float32
    )
    grad_query = rotate_back(grad_query * head_scale, cosine, sine).reshape(micro * seq, q_cols)
    grad_keys = rotate_back(grad_keys, cosine, sine).reshape(micro * seq, k_cols)
    grad_values = grad_values.reshape(micro * seq, k_cols)
    grad_in = jnp.concatenate(
        [grad_query.astype(jnp.bfloat16), grad_keys.astype(jnp.bfloat16), grad_values.astype(jnp.bfloat16)],
        axis=1,
    )
    grad_norm1 = scatter_rows(times_transpose(grad_in, w_in).reshape(micro, seq, width))
    final_in = reduce_weights(contract_rows(flat1, grad_in))
    term_gain1 = jnp.sum(grad_norm1 * unit1, axis=(0, 1))
    grad_tokens = grad_resid + norm_backward(grad_norm1, unit1, scale1, gain1)

    gain_terms = lax.psum(jnp.stack([term_gain1, term_gain2], axis=0), ("dp", "tensor"))
    own = gain_attn.shape[0]
    gain_own = lax.dynamic_slice_in_dim(gain_terms, lax.axis_index("dp") * own, own, 1)
    return (
        output,
        grad_tokens,
        gain_own[0],
        final_in[:, :q_cols],
        final_in[:, q_cols : q_cols + k_cols],
        final_in[:, q_cols + k_cols :],
        final_out.T,
        gain_own[1],
        final_gate,
        final_up,
        final_down.T,
    )


def solution(mesh):
    return jax.shard_map(
        local,
        mesh=mesh,
        in_specs=(
            P("dp", "tensor", None),
            P("dp", "tensor", None),
            P("dp", None),
            P("dp", None),
            P("dp"),
            P("dp", "tensor"),
            P("dp", "tensor"),
            P("dp", "tensor"),
            P("tensor", "dp"),
            P("dp"),
            P("dp", "tensor"),
            P("dp", "tensor"),
            P("tensor", "dp"),
        ),
        out_specs=(
            P("dp", "tensor", None),
            P("dp", "tensor", None),
            P("dp"),
            P("dp", "tensor"),
            P("dp", "tensor"),
            P("dp", "tensor"),
            P("tensor", "dp"),
            P("dp"),
            P("dp", "tensor"),
            P("dp", "tensor"),
            P("tensor", "dp"),
        ),
        check_vma=False,
    )
```

time: 1040 us -> 771 us (0.74)
  blocking collectives: 289 us -> 52.9 us
  matrix products: 102 us -> 86.5 us
  waiting for transfers between devices: 568 us -> 557 us
    all_gather x10 -> x1, blocking collectives: 239 us -> 10.4 us  [gather_weights(): lax.all_gather(jnp.stack([gain_attn, gain_ffn], axis=0), 'dp', axis=1, ti...]
    reduce_scatter x15 -> x9, waiting for transfers between devices: 498 us -> 304 us  [the longest x5 181 us: reduce_weights(): lax.psum_scatter(low, 'dp', scatter_dimension=0, tiled=True)]
    all_gather x5 -> x7, waiting for transfers between devices: 67.1 us -> 252 us  [the longest x4 142 us: gather_rows(): return lax.all_gather(rows, 'tensor', axis=1, tiled=True)]
    unnamed x2 -> x0, blocking collectives: 39.7 us -> none
    psum x1, blocking collectives: 10.6 us -> 42.5 us  [local(): lax.psum(jnp.stack([term_gain1, term_gain2], axis=0), ('dp', 'tensor'))]
    unnamed x223 -> x73, local copies, waits for them, and re-layouts: 20.1 us -> 6.18 us
    dot_general x14 -> x5, matrix products: 31.9 us -> 24.8 us  [contract_rows(): lax.dot_general(left, right, (((0,), (0,)), ((), ())), preferred_element_...]
    dot_general x26 -> x9, matrix products: 44.4 us -> 37.4 us  [the longest x1 9.97 us: local(): both = jnp.dot(full2, gate_up, preferred_element_type=jnp.float32)]
  transfers between devices with their start and end apart: 20 -> 16, of which waited for: 16 -> 15; matrix products, arithmetic and copies ran while one was open for 10% -> 12% of each run, Pallas kernels for 0% -> 0%
where the time goes in v1:
time: 771 us; the launch traced here: 764 us
  waiting for transfers between devices  557 us (72%)
  matrix products  86.5 us (11%)
  blocking collectives  52.9 us (7%)
  other arithmetic  28.6 us (4%)
  local copies, waits for them, and re-layouts  22.7 us (3%)
  between operations  15 us (2%)
    reduce_scatter x5, waiting for transfers between devices, reduce_weights(): lax.psum_scatter(low, 'dp', scatter_dimension=0, tiled=True)  181 us
    all_gather x4, waiting for transfers between devices, gather_rows(): return lax.all_gather(rows, 'tensor', axis=1, tiled=True)  142 us
    reduce_scatter x4, waiting for transfers between devices, scatter_rows(): lax.psum_scatter(low, 'tensor', scatter_dimension=1, tiled=True)  123 us
    psum x1, blocking collectives, local(): lax.psum(jnp.stack([term_gain1, term_gain2], axis=0), ('dp', 'tensor'))  42.5 us
    all_gather x1, waiting for transfers between devices, gather_weights(): lax.all_gather(jnp.concatenate([w_gate, w_up], axis=1), 'dp', axis=0, til...  41.5 us
    all_gather x1, waiting for transfers between devices, gather_weights(): lax.all_gather(jnp.concatenate([w_query, w_key, w_value, w_out.T], axis=1...  35.2 us
    all_gather x1, waiting for transfers between devices, gather_weights(): down = lax.all_gather(w_down.T, 'dp', axis=0, tiled=True)  32.9 us
    dot_general x5, matrix products, contract_rows(): lax.dot_general(left, right, (((0,), (0,)), ((), ())), preferred_element_...  24.8 us
  transfers between devices with their start and end apart: 16, of which 15 were waited for; matrix products, arithmetic and copies ran while one was open for 12% of the time, Pallas kernels for 0%

profile of v1, /device:TPU:0, one launch (start us, length us, event | category | flops | bytes accessed | tf_op | source)
XLA Modules:
  0.0 763.8 jit_solution(17415708524543095408)
XLA Ops:
  10.0 10.4 %all-gather = bf16[8,192,2]{1,2,0:T(2,128)(2,1)S(1)} all-gather(bf16[1,192,2]{1,2,0:T(2,128)(2,1)S(1)} %maximum_bitcast_fusion.8), channel_id=1, replica_groups=mesh['dp'=8,'tensor'=4] {'dp'}, dimensions={0}, use_global_device_ids=true | all-gather | bytes 6912 | tf_op jit(solution)/shard_map/all_gather | solution.py:66
  25.8 40.8 %all-gather.9.cloned.1.call-done = bf16[2,320,1536]{2,1,0:T(8,128)(2,1)} async-done(((bf16[2,80,1536]{2,1,0:T(8,128)(2,1)}), bf16[2,320,1536]{2,1,0:T(8,128)(2,1)}) %all-gather.9.cloned.1.call-update) | async-done | bytes 1966096 | tf_op jit(solution)/shard_map/all_gather | solution.py:76
  66.5 35.2 %all-gather.11.cloned.1.call-done = bf16[1536,1152]{1,0:T(8,128)(2,1)} async-done(((bf16[192,1152]{1,0:T(8,128)(2,1)}), bf16[1536,1152]{1,0:T(8,128)(2,1)}) %all-gather.11.cloned.1.call-update) | async-done | bytes 3538960 | tf_op jit(solution)/shard_map/all_gather | solution.py:67
  101.7 3.9 fusion.8
  107.7 4.7 fusion.63
  115.2 3.9 convolution_convert_fusion.7
  120.3 40.7 %reduce-scatter.10.cloned.1.call-done = bf16[2,80,1536]{2,1,0:T(8,128)(2,1)} async-done(((bf16[2,320,1536]{2,1,0:T(8,128)(2,1)}), bf16[2,80,1536]{2,1,0:T(8,128)(2,1)}) %reduce-scatter.10.cloned.1.call-update) | async-done | bytes 491536 | tf_op jit(solution)/shard_map/reduce_scatter | solution.py:81
  166.3 41.5 %all-gather.15.cloned.1.call-done = bf16[1536,2048]{1,0:T(8,128)(2,1)} async-done(((bf16[192,2048]{1,0:T(8,128)(2,1)}), bf16[1536,2048]{1,0:T(8,128)(2,1)}) %all-gather.15.cloned.1.call-update) | async-done | bytes 6291472 | tf_op jit(solution)/shard_map/all_gather | solution.py:70
  207.8 45.5 %all-gather.13.cloned.1.call-done = bf16[2,320,1536]{2,1,0:T(8,128)(2,1)} async-done(((bf16[2,80,1536]{2,1,0:T(8,128)(2,1)}), bf16[2,320,1536]{2,1,0:T(8,128)(2,1)}) %all-gather.13.cloned.1.call-update) | async-done | bytes 1966096 | tf_op jit(solution)/shard_map/all_gather | solution.py:76
  253.3 10.0 %fusion.68 = f32[640,2048]{1,0:T(8,128)} fusion(bf16[640,1536]{1,0:T(8,128)(2,1)} %bitcast.147, bf16[1536,2048]{1,0:T(8,128)(2,1)} %all-gather.15.cloned.1.call-done), kind=kOutput, calls=%fused_computation.125 | convolution fusion | flops 4026531840 | bytes 13500416 | tf_op jit(solution)/shard_map/dot_general | solution.py:155
  263.3 34.4 %all-gather.19.cloned.1.call-done = bf16[2,320,1536]{2,1,0:T(8,128)(2,1)} async-done(((bf16[2,80,1536]{2,1,0:T(8,128)(2,1)}), bf16[2,320,1536]{2,1,0:T(8,128)(2,1)}) %all-gather.19.cloned.1.call-update) | async-done | bytes 1966096 | tf_op jit(solution)/shard_map/all_gather | solution.py:76
  297.7 32.9 %all-gather.17.cloned.1.call-done = bf16[1536,1024]{1,0:T(8,128)(2,1)} async-done(((bf16[192,1024]{1,0:T(8,128)(2,1)}), bf16[1536,1024]{1,0:T(8,128)(2,1)}) %all-gather.17.cloned.1.call-update) | async-done | bytes 3145744 | tf_op jit(solution)/shard_map/all_gather | solution.py:71
  330.6 8.4 %multiply_convert_fusion.1 = (bf16[640,1024]{1,0:T(8,128)(2,1)S(1)}, bf16[640,1024]{1,0:T(8,128)(2,1)S(1)}, bf16[640,1024]{1,0:T(8,128)(2,1)}) fusion(f32[640,2048]{1,0:T(8,128)} %fusion.68, bf16[640,1536]{1,0:T(8,128)(2,1)} %bitcast.150, bf16[1536,1024]{1,0:T(8,128)(2,1)} %all-gather.17.cloned.1.call-done), kind=kOutput, calls=%fused_computation.22 | convolution fusion | flops 2023751680 | bytes 14286848 | tf_op jit(solution)/shard_map/dot_general | solution.py:162
  339.0 5.5 convolution_convert_fusion.5
  344.6 41.7 %reduce-scatter.14.cloned.1.call-done = bf16[2,80,1536]{2,1,0:T(8,128)(2,1)} async-done(((bf16[2,320,1536]{2,1,0:T(8,128)(2,1)}), bf16[2,80,1536]{2,1,0:T(8,128)(2,1)}) %reduce-scatter.14.cloned.1.call-update) | async-done | bytes 491536 | tf_op jit(solution)/shard_map/reduce_scatter | solution.py:81
  390.1 6.2 convolution_convert_fusion.2
  396.5 6.4 convolution_convert_fusion.1
  403.0 6.3 convolution_convert_fusion
  411.2 21.6 %all-gather.21.cloned.1.call-done = bf16[2,320,1536]{2,1,0:T(8,128)(2,1)} async-done(((bf16[2,80,1536]{2,1,0:T(8,128)(2,1)}), bf16[2,320,1536]{2,1,0:T(8,128)(2,1)}) %all-gather.21.cloned.1.call-update) | async-done | bytes 1966096 | tf_op jit(solution)/shard_map/all_gather | solution.py:76
  432.8 3.0 convolution_convert_fusion.10
  441.2 3.3 fusion.1
  460.3 3.4 convolution_convert_fusion.3
  465.0 4.8 convolution_convert_fusion.4
  471.1 5.4 convolution_convert_fusion.6
  476.5 4.4 reduce-scatter.22.cloned.1.call-done
  482.9 47.5 %reduce-scatter.24.cloned.1.call-done = bf16[192,1024]{1,0:T(8,128)(2,1)} async-done(((bf16[1536,1024]{1,0:T(8,128)(2,1)}), bf16[192,1024]{1,0:T(8,128)(2,1)}) %reduce-scatter.24.cloned.1.call-update) | async-done | bytes 393232 | tf_op jit(solution)/shard_map/reduce_scatter | solution.py:86
  532.4 47.4 %reduce-scatter.26.cloned.1.call-done = bf16[192,1024]{1,0:T(8,128)(2,1)} async-done(((bf16[1536,1024]{1,0:T(8,128)(2,1)}), bf16[192,1024]{1,0:T(8,128)(2,1)}) %reduce-scatter.26.cloned.1.call-update) | async-done | bytes 393232 | tf_op jit(solution)/shard_map/reduce_scatter | solution.py:86
  581.8 38.0 %reduce-scatter.20.cloned.1.call-done = bf16[192,384]{1,0:T(8,128)(2,1)} async-done(((bf16[1536,384]{1,0:T(8,128)(2,1)}), bf16[192,384]{1,0:T(8,128)(2,1)}) %reduce-scatter.20.cloned.1.call-update) | async-done | bytes 147472 | tf_op jit(solution)/shard_map/reduce_scatter | solution.py:86
  621.4 43.9 %reduce-scatter.18.cloned.1.call-done = bf16[192,768]{1,0:T(8,128)(2,1)} async-done(((bf16[1536,768]{1,0:T(8,128)(2,1)}), bf16[192,768]{1,0:T(8,128)(2,1)}) %reduce-scatter.18.cloned.1.call-update) | async-done | bytes 294928 | tf_op jit(solution)/shard_map/reduce_scatter | solution.py:86
  668.7 40.4 %reduce-scatter.16.cloned.1.call-done = bf16[2,80,1536]{2,1,0:T(8,128)(2,1)} async-done(((bf16[2,320,1536]{2,1,0:T(8,128)(2,1)}), bf16[2,80,1536]{2,1,0:T(8,128)(2,1)}) %reduce-scatter.16.cloned.1.call-update) | async-done | bytes 491536 | tf_op jit(solution)/shard_map/reduce_scatter | solution.py:81
  710.6 42.5 %psum.7 = f32[2,1536]{1,0:T(2,128)S(1)} all-reduce(f32[2,1536]{1,0:T(2,128)S(1)} %pad_maximum_fusion.3), channel_id=1, replica_groups=mesh['dp'=8,'tensor'=4] {'dp','tensor'}, use_global_device_ids=true, to_apply=%region_16.17 | all-reduce | flops 3072 | bytes 24576 | tf_op jit(solution)/shard_map/psum | solution.py:204
  753.7 3.1 fusion.30
  (175 shorter events, 61.7 us)
Async XLA Ops:
  7.2 15.5 %copy-start.24 = (bf16[384,192]{0,1:T(8,128)(2,1)S(1)}, bf16[384,192]{0,1:T(8,128)(2,1)}, u32[]{:S(2)}) copy-start(bf16[384,192]{0,1:T(8,128)(2,1)} %param.21) | copy-start | bytes 442372
  7.2 15.5 %copy-start.26 = (bf16[192,192]{1,0:T(8,128)(2,1)S(1)}, bf16[192,192]{1,0:T(8,128)(2,1)}, u32[]{:S(2)}) copy-start(bf16[192,192]{1,0:T(8,128)(2,1)} %param.20) | copy-start | bytes 221188
  7.2 15.5 %copy-start.25 = (bf16[192,192]{1,0:T(8,128)(2,1)S(1)}, bf16[192,192]{1,0:T(8,128)(2,1)}, u32[]{:S(2)}) copy-start(bf16[192,192]{1,0:T(8,128)(2,1)} %param.19) | copy-start | bytes 221188
  7.2 15.5 %copy-start.23 = (bf16[192,384]{1,0:T(8,128)(2,1)S(1)}, bf16[192,384]{1,0:T(8,128)(2,1)}, u32[]{:S(2)}) copy-start(bf16[192,384]{1,0:T(8,128)(2,1)} %param.18) | copy-start | bytes 442372
  7.2 16.4 %copy-start.28 = (s32[2,3]{1,0:T(2,128)S(1)}, s32[2,3]{1,0:T(2,128)}, u32[]{:S(2)}) copy-start(s32[2,3]{1,0:T(2,128)} %param.16) | copy-start | bytes 76
  7.2 16.8 %copy-start.27 = (s32[2,320]{1,0:T(2,128)S(1)}, s32[2,320]{1,0:T(2,128)}, u32[]{:S(2)}) copy-start(s32[2,320]{1,0:T(2,128)} %param.15) | copy-start | bytes 7684
  7.2 59.3 %all-gather.9.cloned.1.call-start = ((), (), s32[]{:S(2)}) async-start(), calls=%async_computation.9 | async-start | bytes 2457600 | tf_op jit(solution)/shard_map/all_gather | solution.py:76
  22.6 79.1 %all-gather.11.cloned.1.call-start = ((), (), s32[]{:S(2)}) async-start(), calls=%async_computation.10 | async-start | bytes 3981312 | tf_op jit(solution)/shard_map/all_gather | solution.py:67
  23.6 137.3 %reduce-scatter.10.cloned.1.call-start = ((), (), s32[]{:S(2)}) async-start(), calls=%async_computation.11 | async-start | bytes 2457600 | tf_op jit(solution)/shard_map/reduce_scatter | solution.py:81
  25.8 81.8 %copy-start.5 = (f32[2,320,48]{1,2,0:T(8,128)}, f32[2,320,48]{1,2,0:T(8,128)S(1)}, u32[]{:S(2)}) copy-start(f32[2,320,48]{1,2,0:T(8,128)S(1)} %get-tuple-element.34) | copy-start | bytes 368644
  25.8 81.8 %copy-start.7 = (f32[2,320,48]{1,2,0:T(8,128)}, f32[2,320,48]{1,2,0:T(8,128)S(1)}, u32[]{:S(2)}) copy-start(f32[2,320,48]{1,2,0:T(8,128)S(1)} %get-tuple-element.35) | copy-start | bytes 368644
  107.5 5.0 copy-start.15
  119.1 41.8 %copy-start = (bf16[2,80,1536]{2,1,0:T(8,128)(2,1)S(1)}, bf16[2,80,1536]{2,1,0:T(8,128)(2,1)}, u32[]{:S(2)}) copy-start(bf16[2,80,1536]{2,1,0:T(8,128)(2,1)} %param.13) | copy-start | bytes 1474564
  119.2 88.6 %all-gather.15.cloned.1.call-start = ((), (), s32[]{:S(2)}) async-start(), calls=%async_computation.13 | async-start | bytes 7077888 | tf_op jit(solution)/shard_map/all_gather | solution.py:70
  120.2 44.2 %copy-start.2 = (bf16[2,80,1536]{2,1,0:T(8,128)(2,1)S(1)}, bf16[2,80,1536]{2,1,0:T(8,128)(2,1)}, u32[]{:S(2)}) copy-start(bf16[2,80,1536]{2,1,0:T(8,128)(2,1)} %param.14) | copy-start | bytes 1474564
  120.2 133.1 %all-gather.13.cloned.1.call-start = ((), (), s32[]{:S(2)}) async-start(), calls=%async_computation.12 | async-start | bytes 2457600 | tf_op jit(solution)/shard_map/all_gather | solution.py:76
  164.2 133.4 %all-gather.19.cloned.1.call-start = ((), (), s32[]{:S(2)}) async-start(), calls=%async_computation.16 | async-start | bytes 2457600 | tf_op jit(solution)/shard_map/all_gather | solution.py:76
  165.3 165.3 %all-gather.17.cloned.1.call-start = ((), (), s32[]{:S(2)}) async-start(), calls=%async_computation.14 | async-start | bytes 3538944 | tf_op jit(solution)/shard_map/all_gather | solution.py:71
  166.1 220.2 %reduce-scatter.14.cloned.1.call-start = ((), (), s32[]{:S(2)}) async-start(), calls=%async_computation.17 | async-start | bytes 2457600 | tf_op jit(solution)/shard_map/reduce_scatter | solution.py:81
  330.6 8.4 %copy-start.29 = (bf16[1536,2048]{1,0:T(8,128)(2,1)S(1)}, bf16[1536,2048]{1,0:T(8,128)(2,1)}, u32[]{:S(2)}) copy-start(bf16[1536,2048]{1,0:T(8,128)(2,1)} %all-gather.15.cloned.1.call-done) | copy-start | bytes 18874372
  339.0 5.5 copy-start.33
  339.0 5.5 copy-start.34
  344.5 41.8 %copy-start.1 = (bf16[2,80,1536]{2,1,0:T(8,128)(2,1)S(1)}, bf16[2,80,1536]{2,1,0:T(8,128)(2,1)}, u32[]{:S(2)}) copy-start(bf16[2,80,1536]{2,1,0:T(8,128)(2,1)} %reduce-scatter.10.cloned.1.call-done) | copy-start | bytes 1474564
  344.5 88.3 %all-gather.21.cloned.1.call-start = ((), (), s32[]{:S(2)}) async-start(), calls=%async_computation.18 | async-start | bytes 2457600 | tf_op jit(solution)/shard_map/all_gather | solution.py:76
  390.0 90.9 %reduce-scatter.22.cloned.1.call-start = ((), (), s32[]{:S(2)}) async-start(), calls=%async_computation.22 | async-start | bytes 3538944 | tf_op jit(solution)/shard_map/reduce_scatter | solution.py:86
  396.3 134.2 %reduce-scatter.24.cloned.1.call-start = ((), (), s32[]{:S(2)}) async-start(), calls=%async_computation.23 | async-start | bytes 3538944 | tf_op jit(solution)/shard_map/reduce_scatter | solution.py:86
  403.0 176.8 %reduce-scatter.26.cloned.1.call-start = ((), (), s32[]{:S(2)}) async-start(), calls=%async_computation.24 | async-start | bytes 3538944 | tf_op jit(solution)/shard_map/reduce_scatter | solution.py:86
  409.3 210.4 %reduce-scatter.20.cloned.1.call-start = ((), (), s32[]{:S(2)}) async-start(), calls=%async_computation.21 | async-start | bytes 1327104 | tf_op jit(solution)/shard_map/reduce_scatter | solution.py:86
  451.0 214.3 %reduce-scatter.18.cloned.1.call-start = ((), (), s32[]{:S(2)}) async-start(), calls=%async_computation.20 | async-start | bytes 2654208 | tf_op jit(solution)/shard_map/reduce_scatter | solution.py:86
  463.8 245.3 %reduce-scatter.16.cloned.1.call-start = ((), (), s32[]{:S(2)}) async-start(), calls=%async_computation.19 | async-start | bytes 2457600 | tf_op jit(solution)/shard_map/reduce_scatter | solution.py:81
  469.8 283.9 %reduce-scatter.12.cloned.1.call-start = ((), (), s32[]{:S(2)}) async-start(), calls=%async_computation.15 | async-start | bytes 2457600 | tf_op jit(solution)/shard_map/reduce_scatter | solution.py:81
  532.4 221.3 %copy-start.3 = (bf16[2,80,1536]{2,1,0:T(8,128)(2,1)S(1)}, bf16[2,80,1536]{2,1,0:T(8,128)(2,1)}, u32[]{:S(2)}) copy-start(bf16[2,80,1536]{2,1,0:T(8,128)(2,1)} %reduce-scatter.14.cloned.1.call-done) | copy-start | bytes 1474564
  (19 other events, 48.3 us)
Sparse Core Ops, SparseCore 0:
  22.7 43.7 all-gather.8
  69.0 32.6 all-gather.10
  119.3 41.5 reduce-scatter.9
  163.2 44.4 all-gather.14
  209.8 43.4 all-gather.12
  255.3 42.3 all-gather.18
  299.5 31.0 all-gather.16
  344.6 41.5 reduce-scatter.13
  390.1 42.6 all-gather.20
  436.0 44.8 reduce-scatter.21
  484.3 46.0 reduce-scatter.23
  533.7 46.0 reduce-scatter.25
  583.0 36.6 reduce-scatter.19
  622.9 42.3 reduce-scatter.17
  667.5 41.5 reduce-scatter.15
  711.3 41.7 reduce-scatter.11

commit v2 on v1

--- a/solution.py
+++ b/solution.py
@@ -1,6 +1,10 @@
+import functools
+
 import jax
 import jax.numpy as jnp
 from jax import lax
+from jax.experimental import pallas as pl
+from jax.experimental.pallas import tpu as pltpu
 from jax.sharding import PartitionSpec as P
 
 HEAD = 96
@@ -86,7 +90,7 @@
     return lax.psum_scatter(low, "dp", scatter_dimension=0, tiled=True).astype(jnp.float32)
 
 
-def local(
+def spread_out(
     tokens,
     cotangent,
     order,
@@ -217,6 +221,907 @@
         final_up,
         final_down.T,
     )
+
+
+BF = jnp.bfloat16
+F32 = jnp.float32
+MESH = pl.DeviceIdType.MESH
+LANES = 128
+
+
+def nn(left, right):
+    return lax.dot_general(left, right, (((1,), (0,)), ((), ())), preferred_element_type=F32)
+
+
+def nt(left, right):
+    return lax.dot_general(left, right, (((1,), (1,)), ((), ())), preferred_element_type=F32)
+
+
+def tn(left, right):
+    return lax.dot_general(left, right, (((0,), (0,)), ((), ())), preferred_element_type=F32)
+
+
+def al(value, unit):
+    return pl.multiple_of(value, unit)
+
+
+def block_kernel(dims, *refs):
+    (rows, seq, width, shard, qp, kp, ff, groups) = dims
+    (tok, cot, wg_h, wi_h, wo_h, wu_h, wd_h, ordr, cols, cosr, sinr) = refs[:11]
+    (out_h, gtok_h, gdown_h, ggate_h, gup_h, gout_h, gin_h, ggain_h) = refs[11:19]
+    (wgn, wi, wo, wu, wd, xf, n1, n2, gf, qkv, ob, dob, act, dgu, pr, hb, dh, pa, pb, ra, rb,
+     gb, xb, hop, fin, stage, acc, gains, gsum, gex, ybuf, tbuf,
+     wsend, wrecv, zsend, zrecv, rsend, rrecv, gsend, grecv, esend, erecv, lsem, osem, credit, zfree) = refs[19:]
+    ghf = xf
+    heads = qp // LANES
+    per_group = heads // groups
+    inw = qp + 2 * kp
+    d = lax.axis_index("dp")
+    z = lax.axis_index("tensor")
+    c = d % 2
+    flip = 1 - 2 * c
+    near_x = d + 2 - 4 * ((d // 2) % 2)
+    near_y = d + 4 - 8 * (d // 4)
+    aa = near_x * (1 - c) + near_y * c
+    bb = near_y * (1 - c) + near_x * c
+    dd = aa + bb - d
+    pp = d + flip
+    chip_own, chip_a, chip_b, chip_d = d // 2, aa // 2, bb // 2, dd // 2
+    chip_x, chip_y = near_x // 2, near_y // 2
+    own = 1 * z * rows
+    zdev = {"tensor": z + 1}, {"tensor": z - 1}
+
+    def rcopy(src, dst, ssem, rsem, dev):
+        return pltpu.make_async_remote_copy(
+            src_ref=src, dst_ref=dst, send_sem=ssem, recv_sem=rsem, device_id=dev, device_id_type=MESH
+        )
+
+    barrier = pltpu.get_barrier_semaphore()
+    for dev in (pp, aa, bb):
+        pl.semaphore_signal(barrier, inc=1, device_id={"dp": dev}, device_id_type=MESH)
+    for step in (1, 2, 3):
+        pl.semaphore_signal(
+            barrier, inc=1, device_id={"tensor": (z + step) % 4}, device_id_type=MESH
+        )
+    pl.semaphore_wait(barrier, 6)
+
+    wunits = ((wg_h, wgn, 16), (wi_h, wi, shard), (wo_h, wo, shard), (wu_h, wu, shard), (wd_h, wd, shard))
+
+    def wblk(u, i):
+        n = wunits[u][2]
+        return wunits[u][1].at[pl.ds(al(n * i, 16), n)]
+
+    def w_start(u):
+        src = wunits[u][0]
+        pltpu.make_async_copy(src, wblk(u, d), lsem.at[u]).start()
+        rcopy(src, wblk(u, d), wsend.at[u, 0], wrecv.at[u, 0], {"dp": aa}).start()
+        rcopy(src, wblk(u, d), wsend.at[u, 1], wrecv.at[u, 1], {"dp": bb}).start()
+        rcopy(src, wblk(u, d), wsend.at[u, 2], wrecv.at[u, 3], {"dp": pp}).start()
+
+    def w_wait(u, slot, i):
+        rcopy(wblk(u, i), wblk(u, i), wsend.at[u, 0], wrecv.at[u, slot], {"dp": aa}).wait_recv()
+
+    def w_relay(u):
+        w_wait(u, 1, bb)
+        rcopy(wblk(u, bb), wblk(u, bb), wsend.at[u, 3], wrecv.at[u, 2], {"dp": aa}).start()
+        rcopy(wblk(u, bb), wblk(u, bb), wsend.at[u, 4], wrecv.at[u, 5], {"dp": pp}).start()
+        w_wait(u, 0, aa)
+        rcopy(wblk(u, aa), wblk(u, aa), wsend.at[u, 5], wrecv.at[u, 4], {"dp": pp}).start()
+
+    def w_diag(u):
+        w_wait(u, 2, dd)
+        rcopy(wblk(u, dd), wblk(u, dd), wsend.at[u, 6], wrecv.at[u, 6], {"dp": pp}).start()
+
+    def w_done(u):
+        w_wait(u, 3, pp)
+        w_wait(u, 4, bb + flip)
+        w_wait(u, 5, aa + flip)
+        w_wait(u, 6, dd + flip)
+        pltpu.make_async_copy(wunits[u][0], wblk(u, d), lsem.at[u]).wait()
+
+    def w_sent(u):
+        for slot in range(7):
+            rcopy(wblk(u, d), wblk(u, d), wsend.at[u, slot], wrecv.at[u, 0], {"dp": aa}).wait_send()
+
+    zfull = (xf, gf, n2, ghf)
+    zhbm = (tok, cot, None, None)
+
+    def zblk(u, s, i):
+        return zfull[u].at[pl.ds(al(s * seq + i * rows, 16), rows)]
+
+    def zag_send(u, s, k, way):
+        i = z - k if way == 0 else z + k
+        go = (z < 3) & (i >= 0) if way == 0 else (z > 0) & (i <= 3)
+
+        @pl.when(go)
+        def _():
+            src = zhbm[u].at[s] if k == 0 and zhbm[u] is not None else zblk(u, s, i)
+            rcopy(src, zblk(u, s, i), zsend.at[u, s, way, k], zrecv.at[u, s, way, k], zdev[way]).start()
+
+    def zag_recv(u, s, k, way):
+        i = z - 1 - k if way == 0 else z + 1 + k
+        go = (i >= 0) if way == 0 else (i <= 3)
+
+        @pl.when(go)
+        def _():
+            rcopy(
+                zblk(u, s, i), zblk(u, s, i), zsend.at[u, s, way, k], zrecv.at[u, s, way, k], zdev[way]
+            ).wait_recv()
+
+    def zag_start(u, s):
+        if zhbm[u] is not None:
+            pltpu.make_async_copy(zhbm[u].at[s], zblk(u, s, z), lsem.at[8 + 2 * u + s]).start()
+        for way in (0, 1):
+            zag_send(u, s, 0, way)
+
+    def zag_fwd(u, s, k):
+        for way in (0, 1):
+            zag_recv(u, s, k - 1, way)
+            zag_send(u, s, k, way)
+
+    def zag_done(u, s):
+        for way in (0, 1):
+            zag_recv(u, s, 2, way)
+        if zhbm[u] is not None:
+            pltpu.make_async_copy(zhbm[u].at[s], zblk(u, s, z), lsem.at[8 + 2 * u + s]).wait()
+
+    def zag_sent(u, s):
+        for k in range(3):
+            for way in (0, 1):
+                i = z - k if way == 0 else z + k
+                go = (z < 3) & (i >= 0) if way == 0 else (z > 0) & (i <= 3)
+
+                @pl.when(go)
+                def _():
+                    rcopy(
+                        zblk(u, s, i), zblk(u, s, i), zsend.at[u, s, way, k], zrecv.at[u, s, way, k], zdev[way]
+                    ).wait_send()
+
+    zpart = (pa, pb, pa, pb)
+    zgot = (ra, rb, ra, rb)
+
+    def pblk(u, s, i):
+        return zpart[u].at[pl.ds(al(s * seq + i * rows, 16), rows)]
+
+    def rblk(u, s, way, i):
+        return zgot[u].at[s, way, i]
+
+    def rs_copy(u, s, way, k):
+        dest = 3 - k if way == 0 else k
+        slot = dest - 1 if way == 0 else dest
+        return rcopy(
+            pblk(u, s, dest), rblk(u, s, way, slot), rsend.at[u, s, way, k], rrecv.at[u, s, way, k], zdev[way]
+        )
+
+    def add_rows(u, s, dest, way, slot):
+        base = s * seq + dest * rows
+
+        def body(i, carry):
+            at = pl.ds(al(base + i * 16, 16), 16)
+            got = zgot[u][s, way, slot, pl.ds(al(i * 16, 16), 16), :]
+            zpart[u][at, :] = (zpart[u][at, :].astype(F32) + got.astype(F32)).astype(BF)
+            return carry
+
+        lax.fori_loop(0, rows // 16, body, 0)
+
+    def rs_step(u, s, k):
+        if u == 3 and k == 0:
+            @pl.when(z > 0)
+            def _():
+                pl.semaphore_wait(zfree.at[s, 0], 1)
+
+            @pl.when(z < 3)
+            def _():
+                pl.semaphore_wait(zfree.at[s, 1], 1)
+
+        for way in (0, 1):
+            dest = 3 - k if way == 0 else k
+            slot = dest - 1 if way == 0 else dest
+            sends = (z < dest) if way == 0 else (z > dest)
+            inner = (z > 0) if way == 0 else (z < 3)
+
+            @pl.when(sends)
+            def _():
+                @pl.when(inner)
+                def _():
+                    rs_copy(u, s, way, k).wait_recv()
+                    add_rows(u, s, dest, way, slot)
+
+                rs_copy(u, s, way, k).start()
+
+    def rs_final(u, s):
+        def first(i, carry):
+            at = pl.ds(al(i * 16, 16), 16)
+            acc[at, :] = zpart[u][pl.ds(al(s * seq + own + i * 16, 16), 16), :].astype(F32)
+            return carry
+
+        lax.fori_loop(0, rows // 16, first, 0)
+        for way in (0, 1):
+            there = (z > 0) if way == 0 else (z < 3)
+            slot = z - 1 if way == 0 else z
+            k = 3 - z if way == 0 else z
+
+            @pl.when(there)
+            def _():
+                rcopy(
+                    pblk(u, s, z), rblk(u, s, way, slot), rsend.at[u, s, way, k], rrecv.at[u, s, way, k], zdev[way]
+                ).wait_recv()
+
+                def more(i, carry):
+                    at = pl.ds(al(i * 16, 16), 16)
+                    acc[at, :] += zgot[u][s, way, slot, at, :].astype(F32)
+                    return carry
+
+                lax.fori_loop(0, rows // 16, more, 0)
+
+        if u == 1:
+            @pl.when(z < 3)
+            def _():
+                pl.semaphore_signal(zfree.at[s, 0], inc=1, device_id=zdev[0], device_id_type=MESH)
+
+            @pl.when(z > 0)
+            def _():
+                pl.semaphore_signal(zfree.at[s, 1], inc=1, device_id=zdev[1], device_id_type=MESH)
+
+    def rs_sent(u, s):
+        for way in (0, 1):
+            for k in range(3):
+                dest = 3 - k if way == 0 else k
+                sends = (z < dest) if way == 0 else (z > dest)
+
+                @pl.when(sends)
+                def _():
+                    rs_copy(u, s, way, k).wait_send()
+
+    gunits = (
+        (gf, act, 0, ff, gdown_h),
+        (n2, dgu, 0, ff, ggate_h),
+        (n2, dgu, ff, ff, gup_h),
+        (ghf, ob, 0, qp, gout_h),
+        (n1, act, 0, inw, gin_h),
+    )
+    pair = 2 * shard
+
+    def xslot(u, chip):
+        b, n = u % 2, gunits[u][3]
+        return xb.at[b, pl.ds(al(chip * shard, 16), shard), pl.ds(0, n)]
+
+    def gslot(u, chip, core):
+        b, n = u % 2, gunits[u][3]
+        return gb.at[b, pl.ds(al(chip * pair + core * shard, 16), shard), pl.ds(0, n)]
+
+    def g_exchange(u, chip, i):
+        return rcopy(gslot(u, chip, 1 - c), xslot(u, chip), gsend.at[u, i], grecv.at[u, i], {"dp": pp})
+
+    chips = (chip_d, chip_x, chip_y, chip_own)
+
+    def g_compute(u):
+        left, right, at, n, _ = gunits[u]
+        if u >= 2:
+            pl.semaphore_wait(credit.at[0], 1)
+        for i, chip in enumerate(chips):
+            tile = 256
+
+            def body(j, carry):
+                lhs = left[:, pl.ds(al(chip * pair, LANES), pair)]
+                got = tn(lhs, right[:, pl.ds(al(at + j * tile, tile), tile)])
+                gb[u % 2, pl.ds(al(chip * pair, 16), pair), pl.ds(al(j * tile, tile), tile)] = got.astype(BF)
+                return carry
+
+            lax.fori_loop(0, n // tile, body, 0)
+            g_exchange(u, chip, i).start()
+
+    def g_add(u, chip, extra=None):
+        b, n = u % 2, gunits[u][3]
+
+        def body(i, carry):
+            at = pl.ds(al(chip * shard + i * 16, 16), 16)
+            mine = gb[b, pl.ds(al(chip * pair + c * shard + i * 16, 16), 16), pl.ds(0, n)].astype(F32)
+            total = mine + xb[b, at, pl.ds(0, n)].astype(F32)
+            if extra is not None:
+                total = total + extra[b, pl.ds(al(i * 16, 16), 16), pl.ds(0, n)].astype(F32)
+            xb[b, at, pl.ds(0, n)] = total.astype(BF)
+            return carry
+
+        lax.fori_loop(0, shard // 16, body, 0)
+
+    def g_hop(u):
+        b, n = u % 2, gunits[u][3]
+        return rcopy(xslot(u, chip_d), hop.at[b, :, pl.ds(0, n)], gsend.at[u, 4], grecv.at[u, 4], {"dp": aa})
+
+    def g_last(u, way):
+        b, n = u % 2, gunits[u][3]
+        chip, dev = (chip_a, aa) if way == 0 else (chip_b, bb)
+        return rcopy(
+            xslot(u, chip), fin.at[b, way, :, pl.ds(0, n)], gsend.at[u, 5 + way], grecv.at[u, 5 + way], {"dp": dev}
+        )
+
+    def g_first(u):
+        g_exchange(u, chip_d, 0).wait_recv()
+        g_add(u, chip_d)
+        if u >= 2:
+            pl.semaphore_wait(credit.at[1], 1)
+        g_hop(u).start()
+        g_exchange(u, chip_x, 1).wait_recv()
+        g_exchange(u, chip_y, 2).wait_recv()
+        g_add(u, chip_a)
+        g_last(u, 0).start()
+
+    def g_second(u):
+        g_hop(u).wait_recv()
+        g_add(u, chip_b, hop)
+        if u >= 2:
+            pl.semaphore_wait(credit.at[2], 1)
+        g_last(u, 1).start()
+
+    def g_finish(u):
+        b, n, out = u % 2, gunits[u][3], gunits[u][4]
+        g_exchange(u, chip_own, 3).wait_recv()
+        g_last(u, 0).wait_recv()
+        g_last(u, 1).wait_recv()
+
+        def body(i, carry):
+            at = pl.ds(al(i * 16, 16), 16)
+            total = gb[b, pl.ds(al(chip_own * pair + c * shard + i * 16, 16), 16), pl.ds(0, n)].astype(F32)
+            total = total + xb[b, pl.ds(al(chip_own * shard + i * 16, 16), 16), pl.ds(0, n)].astype(F32)
+            total = total + fin[b, 0, at, pl.ds(0, n)].astype(F32)
+            stage[b, at, pl.ds(0, n)] = total + fin[b, 1, at, pl.ds(0, n)].astype(F32)
+            return carry
+
+        if u >= 2:
+            g_out(u - 2).wait()
+        lax.fori_loop(0, shard // 16, body, 0)
+        g_out(u).start()
+        for i in range(4):
+            g_exchange(u, chips[i], i).wait_send()
+        g_hop(u).wait_send()
+        g_last(u, 0).wait_send()
+        g_last(u, 1).wait_send()
+        if u < 3:
+            pl.semaphore_signal(credit.at[0], inc=1, device_id={"dp": pp}, device_id_type=MESH)
+            pl.semaphore_signal(credit.at[1], inc=1, device_id={"dp": aa}, device_id_type=MESH)
+            pl.semaphore_signal(credit.at[2], inc=1, device_id={"dp": bb}, device_id_type=MESH)
+
+    def g_out(u):
+        b, n, out = u % 2, gunits[u][3], gunits[u][4]
+        return pltpu.make_async_copy(stage.at[b, :, pl.ds(0, n)], out, osem.at[u])
+
+    def norm1(s):
+        gain = gains[0:1, :]
+
+        def body(i, carry):
+            at = pl.ds(al(s * seq + i * 16, 16), 16)
+            x = xf[at, :].astype(F32)
+            scale = lax.rsqrt(jnp.mean(x * x, axis=-1, keepdims=True) + eps)
+            n1[at, :] = (x * scale * gain).astype(BF)
+            return carry
+
+        lax.fori_loop(0, seq // 16, body, 0)
+
+    head_scale = HEAD ** (-0.5)
+
+    def project(s):
+        at = pl.ds(s * seq, seq)
+        cosine, sine = cosr[s], sinr[s]
+        for j in range(inw // 256):
+            both = nn(n1[at, :], wi[:, pl.ds(j * 256, 256)])
+            for half in range(2):
+                col = j * 256 + half * LANES
+                part = both[:, half * LANES : (half + 1) * LANES]
+                if col < qp + kp:
+                    part = part * cosine + pltpu.roll(part, LANES // 2, 1) * sine
+                if col < qp:
+                    part = part * head_scale
+                qkv[at, pl.ds(col, LANES)] = part.astype(BF)
+
+    def attend(s):
+        at = pl.ds(s * seq, seq)
+        oc = ordr[s]
+        mask = (oc <= cols[s, :, 0:1]) & (oc >= cols[s, :, 1:2])
+
+        def body(h, carry):
+            g = h // per_group
+            q = qkv[at, pl.ds(al(h * LANES, LANES), LANES)]
+            k = qkv[at, pl.ds(al(qp + g * LANES, LANES), LANES)]
+            v = qkv[at, pl.ds(al(qp + kp + g * LANES, LANES), LANES)]
+            sc = jnp.where(mask, nt(q, k), -1e30)
+            e = jnp.exp(sc - jnp.max(sc, axis=-1, keepdims=True))
+            p = e * (1.0 / jnp.sum(e, axis=-1, keepdims=True))
+            pr[s * heads + h] = p
+            ob[at, pl.ds(al(h * LANES, LANES), LANES)] = nn(p.astype(BF), v).astype(BF)
+            return carry
+
+        lax.fori_loop(0, heads, body, 0)
+
+    def spread(s, dst, left, weight, tile):
+        at = pl.ds(s * seq, seq)
+
+        def body(j, carry):
+            col = al(j * tile, tile)
+            dst[at, pl.ds(col, tile)] = nt(left[at, :], weight[pl.ds(col, tile), :]).astype(BF)
+            return carry
+
+        lax.fori_loop(0, width // tile, body, 0)
+
+    def norm2(s):
+        gain = gains[1:2, :]
+        base = s * rows
+
+        def body(i, carry):
+            r = pl.ds(al(i * 16, 16), 16)
+            h = tbuf[s, r, :].astype(F32) + acc[r, :]
+            hb[pl.ds(al(base + i * 16, 16), 16), :] = h
+            scale = lax.rsqrt(jnp.mean(h * h, axis=-1, keepdims=True) + eps)
+            n2[pl.ds(al(s * seq + own + i * 16, 16), 16), :] = (h * scale * gain).astype(BF)
+            return carry
+
+        lax.fori_loop(0, rows // 16, body, 0)
+
+    def mask_grad(s):
+        def body(i, carry):
+            at = pl.ds(al(s * seq + i * 16, 16), 16)
+            gf[at, :] = (gf[at, :].astype(F32) * cols[s, pl.ds(al(i * 16, 16), 16), 2:3]).astype(BF)
+            return carry
+
+        lax.fori_loop(0, seq // 16, body, 0)
+
+    def feed(s):
+        at = pl.ds(s * seq, seq)
+
+        def body(t, carry):
+            col = al(t * 256, 256)
+            gate = nn(n2[at, :], wu[:, pl.ds(col, 256)])
+            upper = nn(n2[at, :], wu[:, pl.ds(al(ff + t * 256, 256), 256)])
+            back = nn(gf[at, :], wd[:, pl.ds(col, 256)])
+            sigma = 1.0 / (1.0 + jnp.exp(-gate))
+            swish = gate * sigma
+            act[at, pl.ds(col, 256)] = (swish * upper).astype(BF)
+            dgu[at, pl.ds(col, 256)] = (back * upper * sigma * (1.0 + gate * (1.0 - sigma))).astype(BF)
+            dgu[at, pl.ds(al(ff + t * 256, 256), 256)] = (back * swish).astype(BF)
+            return carry
+
+        lax.fori_loop(0, ff // 256, body, 0)
+
+    def finish_out(s):
+        def body(i, carry):
+            r = pl.ds(al(i * 16, 16), 16)
+            real = cols[s, pl.ds(al(own + i * 16, 16), 16), 2:3]
+            y = (hb[pl.ds(al(s * rows + i * 16, 16), 16), :] + acc[r, :]) * real
+            ybuf[s, r, :] = y.astype(BF)
+            return carry
+
+        lax.fori_loop(0, rows // 16, body, 0)
+        pltpu.make_async_copy(ybuf.at[s], out_h.at[s], osem.at[5 + s]).start()
+
+    def norm2_back(s):
+        gain = gains[1:2, :]
+
+        def body(i, carry):
+            r = pl.ds(al(i * 16, 16), 16)
+            ro = pl.ds(al(s * rows + i * 16, 16), 16)
+            h = hb[ro, :]
+            scale = lax.rsqrt(jnp.mean(h * h, axis=-1, keepdims=True) + eps)
+            unit = h * scale
+            grad = acc[r, :]
+            inner = grad * gain
+            dy = gf[pl.ds(al(s * seq + own + i * 16, 16), 16), :].astype(F32)
+            dhr = dy + scale * (inner - unit * jnp.mean(inner * unit, axis=-1, keepdims=True))
+            dh[ro, :] = dhr
+            ghf[pl.ds(al(s * seq + own + i * 16, 16), 16), :] = dhr.astype(BF)
+            return carry + jnp.sum(grad * unit, axis=0, keepdims=True)
+
+        return lax.fori_loop(0, rows // 16, body, jnp.zeros((1, width), F32))
+
+    def grad_heads(s):
+        at = pl.ds(s * seq, seq)
+        for j in range(qp // 256):
+            dob[at, pl.ds(j * 256, 256)] = nn(ghf[at, :], wo[:, pl.ds(j * 256, 256)]).astype(BF)
+
+    def attend_back(s):
+        at = pl.ds(s * seq, seq)
+        cosine, sine = cosr[s], sinr[s]
+
+        def body(g, carry):
+            k = qkv[at, pl.ds(al(qp + g * LANES, LANES), LANES)]
+            v = qkv[at, pl.ds(al(qp + kp + g * LANES, LANES), LANES)]
+            dk = jnp.zeros((seq, LANES), F32)
+            dv = jnp.zeros((seq, LANES), F32)
+            for m in range(per_group):
+                h = g * per_group + m
+                hat = pl.ds(al(h * LANES, LANES), LANES)
+                q = qkv[at, hat]
+                do = dob[at, hat]
+                p = pr[s * heads + h]
+                dp = nt(do, v)
+                ds = (p * (dp - jnp.sum(p * dp, axis=-1, keepdims=True))).astype(BF)
+                dv = dv + tn(p.astype(BF), do)
+                dk = dk + tn(ds, q)
+                dq = nn(ds, k) * head_scale
+                act[at, hat] = (dq * cosine - pltpu.roll(dq, LANES // 2, 1) * sine).astype(BF)
+            act[at, pl.ds(al(qp + g * LANES, LANES), LANES)] = (
+                dk * cosine - pltpu.roll(dk, LANES // 2, 1) * sine
+            ).astype(BF)
+            act[at, pl.ds(al(qp + kp + g * LANES, LANES), LANES)] = dv.astype(BF)
+            return carry
+
+        lax.fori_loop(0, groups, body, 0)
+
+    def norm1_back(s):
+        gain = gains[0:1, :]
+
+        def body(i, carry):
+            r = pl.ds(al(i * 16, 16), 16)
+            ro = pl.ds(al(s * rows + i * 16, 16), 16)
+            x = tbuf[s, r, :].astype(F32)
+            scale = lax.rsqrt(jnp.mean(x * x, axis=-1, keepdims=True) + eps)
+            unit = x * scale
+            grad = acc[r, :]
+            inner = grad * gain
+            dh[ro, :] = dh[ro, :] + scale * (inner - unit * jnp.mean(inner * unit, axis=-1, keepdims=True))
+            return carry + jnp.sum(grad * unit, axis=0, keepdims=True)
+
+        total = lax.fori_loop(0, rows // 16, body, jnp.zeros((1, width), F32))
+        pltpu.make_async_copy(
+            dh.at[pl.ds(s * rows, rows)], gtok_h.at[s], osem.at[7 + s]
+        ).start()
+        return total
+
+    for s in (0, 1):
+        pltpu.make_async_copy(tok.at[s], tbuf.at[s], lsem.at[5 + s]).start()
+    zag_start(0, 0)
+    w_start(0)
+    w_start(1)
+    w_start(2)
+    zag_fwd(0, 0, 1)
+    zag_start(0, 1)
+    w_relay(0)
+    w_relay(1)
+    w_start(3)
+    zag_fwd(0, 0, 2)
+    zag_fwd(0, 1, 1)
+    w_relay(2)
+    w_start(4)
+    w_diag(0)
+    w_diag(1)
+    w_diag(2)
+    w_done(0)
+    for j in range(4):
+        at = pl.ds(j * pair, pair)
+        gains[:, at] = (
+            wgn[pl.ds(32 * j, 16), :].astype(F32) + wgn[pl.ds(32 * j + 16, 16), :].astype(F32)
+        )
+    zag_done(0, 0)
+    zag_fwd(0, 1, 2)
+    zag_start(1, 0)
+    norm1(0)
+    w_done(1)
+    project(0)
+    w_relay(3)
+    zag_done(0, 1)
+    zag_fwd(1, 0, 1)
+    zag_start(1, 1)
+    attend(0)
+    w_done(2)
+    spread(0, pa, ob, wo, 512)
+    rs_step(0, 0, 0)
+    zag_fwd(1, 0, 2)
+    zag_fwd(1, 1, 1)
+    w_relay(4)
+    w_diag(3)
+    norm1(1)
+    rs_step(0, 0, 1)
+    project(1)
+    rs_step(0, 0, 2)
+    zag_fwd(1, 1, 2)
+    attend(1)
+    for s in (0, 1):
+        pltpu.make_async_copy(tok.at[s], tbuf.at[s], lsem.at[5 + s]).wait()
+        zag_sent(0, s)
+    spread(1, pa, ob, wo, 512)
+    rs_step(0, 1, 0)
+    rs_final(0, 0)
+    norm2(0)
+    zag_start(2, 0)
+    w_diag(4)
+    zag_done(1, 0)
+    mask_prep = mask_grad
+    rs_step(0, 1, 1)
+    zag_fwd(2, 0, 1)
+    rs_step(0, 1, 2)
+    zag_sent(1, 0)
+    mask_prep(0)
+    rs_final(0, 1)
+    norm2(1)
+    zag_start(2, 1)
+    zag_fwd(2, 0, 2)
+    zag_done(1, 1)
+    zag_fwd(2, 1, 1)
+    zag_sent(1, 1)
+    mask_prep(1)
+    w_done(3)
+    w_done(4)
+    rs_sent(0, 0)
+    rs_sent(0, 1)
+    zag_done(2, 0)
+    feed(0)
+    zag_fwd(2, 1, 2)
+    spread(0, pa, dgu, wu, 256)
+    rs_step(2, 0, 0)
+    zag_done(2, 1)
+    spread(0, pb, act, wd, 512)
+    rs_step(2, 0, 1)
+    feed(1)
+    rs_step(2, 0, 2)
+    spread(1, pa, dgu, wu, 256)
+    rs_step(2, 1, 0)
+    rs_final(2, 0)
+    gain2 = norm2_back(0)
+    zag_start(3, 0)
+    rs_step(1, 0, 0)
+    spread(1, pb, act, wd, 512)
+    rs_step(2, 1, 1)
+    zag_fwd(3, 0, 1)
+    g_compute(0)
+    rs_step(2, 1, 2)
+    zag_fwd(3, 0, 2)
+    rs_step(1, 1, 0)
+    rs_final(2, 1)
+    gain2 = gain2 + norm2_back(1)
+    for j in range(4):
+        gsum[4 + j : 5 + j, :] = gain2[:, j * pair : (j + 1) * pair]
+    zag_start(3, 1)
+    g_first(0)
+    g_compute(1)
+    rs_step(1, 0, 1)
+    zag_fwd(3, 1, 1)
+    zag_done(3, 0)
+    grad_heads(0)
+    rs_step(1, 0, 2)
+    rs_step(1, 1, 1)
+    zag_fwd(3, 1, 2)
+    rs_step(1, 1, 2)
+    g_second(0)
+    g_first(1)
+    rs_final(1, 0)
+    finish_out(0)
+    rs_final(1, 1)
+    finish_out(1)
+    rs_sent(1, 0)
+    rs_sent(1, 1)
+    g_finish(0)
+    g_compute(2)
+    attend_back(0)
+    spread(0, pb, act, wi, 512)
+    rs_step(3, 0, 0)
+    g_second(1)
+    g_first(2)
+    zag_done(3, 1)
+    grad_heads(1)
+    rs_step(3, 0, 1)
+    attend_back(1)
+    rs_step(3, 0, 2)
+    spread(1, pb, act, wi, 512)
+    rs_step(3, 1, 0)
+    g_finish(1)
+    g_second(2)
+    g_compute(3)
+    rs_step(3, 1, 1)
+    g_first(3)
+    g_finish(2)
+    g_compute(4)
+    rs_step(3, 1, 2)
+    g_first(4)
+    g_second(3)
+    rs_final(3, 0)
+    gain1 = norm1_back(0)
+    g_second(4)
+    g_finish(3)
+    rs_final(3, 1)
+    gain1 = gain1 + norm1_back(1)
+    for j in range(4):
+        gsum[j : j + 1, :] = gain1[:, j * pair : (j + 1) * pair]
+
+    def e_copy(i, dev, src):
+        return rcopy(src, gex.at[i], esend.at[i], erecv.at[i], dev)
+
+    for step in (1, 2, 3):
+        e_copy(step - 1, {"tensor": (z + step) % 4}, gsum).start()
+    for step in (1, 2, 3):
+        e_copy(step - 1, {"tensor": (z + step) % 4}, gsum).wait()
+    gsum2 = gsum[...] + gex[0] + gex[1] + gex[2]
+    gex[6] = gsum2
+    e_copy(3, {"dp": pp}, gex.at[6]).start()
+    g_finish(4)
+    e_copy(3, {"dp": pp}, gex.at[6]).wait()
+    gex[7] = gex[6] + gex[3]
+    e_copy(4, {"dp": aa}, gex.at[7]).start()
+    e_copy(4, {"dp": aa}, gex.at[7]).wait()
+    gex[8] = gex[7] + gex[4]
+    e_copy(5, {"dp": bb}, gex.at[8]).start()
+    e_copy(5, {"dp": bb}, gex.at[8]).wait()
+    gsum[...] = gex[8] + gex[5]
+    last = pltpu.make_async_copy(gsum, ggain_h, osem.at[9])
+    last.start()
+    for u in range(5):
+        w_sent(u)
+    for u in (2, 3):
+        for s in (0, 1):
+            zag_sent(u, s)
+    for u in (2, 3):
+        for s in (0, 1):
+            rs_sent(u, s)
+    g_out(3).wait()
+    g_out(4).wait()
+    for s in (0, 1):
+        pltpu.make_async_copy(ybuf.at[s], out_h.at[s], osem.at[5 + s]).wait()
+        pltpu.make_async_copy(dh.at[pl.ds(s * rows, rows)], gtok_h.at[s], osem.at[7 + s]).wait()
+    last.wait()
+
+
+def pad_heads(weight):
+    depth = weight.shape[0]
+    halves = weight.reshape(depth, -1, 2, HEAD // 2)
+    return jnp.pad(halves, ((0, 0), (0, 0), (0, 0), (0, 64 - HEAD // 2))).reshape(depth, -1)
+
+
+def cut_heads(grad):
+    depth = grad.shape[0]
+    return grad.reshape(depth, -1, 2, 64)[..., : HEAD // 2].reshape(depth, -1)
+
+
+def fused(
+    tokens,
+    cotangent,
+    order,
+    lengths,
+    gain_attn,
+    w_query,
+    w_key,
+    w_value,
+    w_out,
+    gain_ffn,
+    w_gate,
+    w_up,
+    w_down,
+):
+    micro, rows, width = tokens.shape
+    seq = rows * lax.axis_size("tensor")
+    shard = w_query.shape[0]
+    ff = w_gate.shape[1]
+    groups = w_key.shape[1] // HEAD
+    w_in = pad_heads(jnp.concatenate([w_query, w_key, w_value], axis=1))
+    qp = w_query.shape[1] // HEAD * LANES
+    kp = groups * LANES
+    inw = qp + 2 * kp
+    w_back = pad_heads(w_out.T)
+    gate_up = jnp.concatenate([w_gate, w_up], axis=1)
+    gain = jnp.stack([gain_attn, gain_ffn], axis=0)
+    low = jnp.pad(gain, ((0, 14), (0, shard)))
+    high = jnp.pad(gain, ((0, 14), (shard, 0)))
+    gain = jnp.where(lax.axis_index("dp") % 2 == 0, low, high)
+
+    starts = jnp.cumsum(lengths, axis=1, dtype=jnp.int32) - lengths
+    docs = jnp.sum((order[:, :, None] >= starts[:, None, 1:]).astype(jnp.int32), axis=2)
+    onehot = docs[:, :, None] == jnp.arange(lengths.shape[1], dtype=jnp.int32)
+    first = jnp.sum(jnp.where(onehot, starts[:, None, :], 0), axis=2)
+    real = (docs < lengths.shape[1] - 1).astype(F32)
+    cols = jnp.stack([order.astype(F32), first.astype(F32), real], axis=2)
+    freqs = rope_base ** (-2.0 * jnp.arange(HEAD // 2, dtype=F32) / HEAD)
+    angles = (order - first).astype(F32)[:, :, None] * freqs
+    gap = ((0, 0), (0, 0), (0, 64 - HEAD // 2))
+    cosine, sine = jnp.pad(jnp.cos(angles), gap), jnp.pad(jnp.sin(angles), gap)
+    cosine = jnp.concatenate([cosine, cosine], axis=2)
+    sine = jnp.concatenate([-sine, sine], axis=2)
+
+    total = micro * seq
+    vm = pltpu.VMEM
+    dma = pltpu.SemaphoreType.DMA
+    scratch = [
+        vm((8 * 16, 2 * shard), BF),
+        vm((width, inw), BF),
+        vm((width, qp), BF),
+        vm((width, 2 * ff), BF),
+        vm((width, ff), BF),
+        vm((total, width), BF),
+        vm((total, width), BF),
+        vm((total, width), BF),
+        vm((total, width), BF),
+        vm((total, inw), BF),
+        vm((total, qp), BF),
+        vm((total, qp), BF),
+        vm((total, ff), BF),
+        vm((total, 2 * ff), BF),
+        vm((micro * qp // LANES, seq, seq), F32),
+        vm((micro * rows, width), F32),
+        vm((micro * rows, width), F32),
+        vm((total, width), BF),
+        vm((total, width), BF),
+        vm((micro, 2, 3, rows, width), BF),
+        vm((micro, 2, 3, rows, width), BF),
+        vm((2, width, ff), BF),
+        vm((2, width // 2, ff), BF),
+        vm((2, shard, ff), BF),
+        vm((2, 2, shard, ff), BF),
+        vm((2, shard, ff), F32),
+        vm((rows, width), F32),
+        vm((16, width), F32),
+        vm((8, width // 4), F32),
+        vm((9, 8, width // 4), F32),
+        vm((micro, rows, width), BF),
+        vm((micro, rows, width), BF),
+        dma((5, 7)),
+        dma((5, 7)),
+        dma((4, 2, 2, 3)),
+        dma((4, 2, 2, 3)),
+        dma((4, 2, 2, 3)),
+        dma((4, 2, 2, 3)),
+        dma((5, 7)),
+        dma((5, 7)),
+        dma((6,)),
+        dma((6,)),
+        dma((12,)),
+        dma((10,)),
+        pltpu.SemaphoreType.REGULAR((3,)),
+        pltpu.SemaphoreType.REGULAR((2, 2)),
+    ]
+    hbm = pl.BlockSpec(memory_space=pl.ANY)
+    vmem = pl.BlockSpec(memory_space=pltpu.VMEM)
+    shapes = [
+        jax.ShapeDtypeStruct((micro, rows, width), BF),
+        jax.ShapeDtypeStruct((micro, rows, width), F32),
+        jax.ShapeDtypeStruct((shard, ff), F32),
+        jax.ShapeDtypeStruct((shard, ff), F32),
+        jax.ShapeDtypeStruct((shard, ff), F32),
+        jax.ShapeDtypeStruct((shard, qp), F32),
+        jax.ShapeDtypeStruct((shard, inw), F32),
+        jax.ShapeDtypeStruct((8, width // 4), F32),
+    ]
+    dims = (rows, seq, width, shard, qp, kp, ff, groups)
+    out, gtok, gdown, ggate, gup, gout, gin, ggain = pl.pallas_call(
+        functools.partial(block_kernel, dims),
+        out_shape=shapes,
+        in_specs=[hbm] * 7 + [vmem] * 4,
+        out_specs=[hbm] * 8,
+        scratch_shapes=scratch,
+        compiler_params=pltpu.CompilerParams(
+            collective_id=0, has_side_effects=True, vmem_limit_bytes=67_043_328
+        ),
+        name="block",
+    )(
+        tokens,
+        cotangent,
+        gain,
+        w_in,
+        w_back,
+        gate_up,
+        w_down.T,
+        order.astype(F32)[:, None, :],
+        cols,
+        cosine,
+        sine,
+    )
+    gains = ggain.reshape(2, width)
+    gain_own = lax.dynamic_slice_in_dim(gains, lax.axis_index("dp") * shard, shard, 1)
+    grads_in = cut_heads(gin)
+    q_cols, k_cols = w_query.shape[1], w_key.shape[1]
+    return (
+        out,
+        gtok,
+        gain_own[0],
+        grads_in[:, :q_cols],
+        grads_in[:, q_cols : q_cols + k_cols],
+        grads_in[:, q_cols + k_cols :],
+        cut_heads(gout).T,
+        gain_own[1],
+        ggate,
+        gup,
+        gdown.T,
+    )
+
+
+def local(tokens, *rest):
+    fits = lax.axis_size("dp") == 8 and lax.axis_size("tensor") == 4 and tokens.shape[0] == 2
+    return (fused if fits else spread_out)(tokens, *rest)
 
 
 def solution(mesh):

time: 771 us -> 387 us (0.50)
  waiting for transfers between devices: 557 us -> 0 us
  Pallas kernels: 0 us -> 358 us
  matrix products: 86.5 us -> 0 us
  blocking collectives: 52.9 us -> 0 us
  other arithmetic: 28.6 us -> 7.19 us
  between operations: 15 us -> 0.89 us
    pallas_call x0 -> x1, Pallas kernels: none -> 358 us  [fused(): pl.pallas_call(functools.partial(block_kernel, dims), out_shape=shapes, i...]
    reduce_scatter x9 -> x0, waiting for transfers between devices: 304 us -> none  [the longest x5 181 us: reduce_weights(): lax.psum_scatter(low, 'dp', scatter_dimension=0, tiled=True)]
    all_gather x7 -> x0, waiting for transfers between devices: 252 us -> none  [the longest x4 142 us: gather_rows(): return lax.all_gather(rows, 'tensor', axis=1, tiled=True)]
    dot_general x18 -> x0, matrix products: 81.8 us -> none  [the longest x5 24.8 us: contract_rows(): lax.dot_general(left, right, (((0,), (0,)), ((), ())), preferred_element_...]
    psum x1 -> x0, blocking collectives: 42.5 us -> none  [local(): lax.psum(jnp.stack([term_gain1, term_gain2], axis=0), ('dp', 'tensor'))]
    convert_element_type x10 -> x2, other arithmetic: 11.8 us -> 0.77 us  [the longest x1 0.77 us: fused(): angles = (order - first).astype(F32)[:, :, None] * freqs]
    all_gather x1 -> x0, blocking collectives: 10.4 us -> none  [gather_weights(): lax.all_gather(jnp.stack([gain_attn, gain_ffn], axis=0), 'dp', axis=1, ti...]
  transfers between devices with their start and end apart: 16 -> 0, of which waited for: 15 -> 0; matrix products, arithmetic and copies ran while one was open for 12% -> 0% of each run, Pallas kernels for 0% -> 0%
where the time goes in v2:
time: 387 us; the launch traced here: 384 us
  Pallas kernels  358 us (93%)
  local copies, waits for them, and re-layouts  17.2 us (4%)
  other arithmetic  7.19 us (2%)
    pallas_call x1, Pallas kernels, fused(): pl.pallas_call(functools.partial(block_kernel, dims), out_shape=shapes, i...  358 us
    unnamed x39, local copies, waits for them, and re-layouts  9.88 us

profile of v2, /device:TPU:0, one launch (start us, length us, event | category | flops | bytes accessed | tf_op | source)
XLA Modules:
  0.0 383.8 jit_solution(6358291705069096397)
XLA Ops:
  0.7 0.7 stack.17
  1.3 0.7 stack.18
  2.0 0.7 pad_select_fusion.refs_2_
  2.7 0.8 reduce_window_sum.11
  3.5 0.7 sub.6
  4.3 0.8 fusion.1
  5.2 0.8 subtract_convert_fusion
  6.0 1.2 multiply_sine_fusion
  7.3 1.1 pad_maximum_fusion.2
  8.4 0.9 copy.60.refs_8_
  9.3 0.6 broadcast_in_dim.14.refs_7_
  9.9 0.1 copy.53
  10.5 0.9 copy.58.refs_3_
  11.5 0.9 pad_maximum_fusion.refs_5_
  12.4 0.1 copy.56
  12.6 0.8 copy.59.refs_4_
  13.4 358.5 %block.1 = (bf16[2,80,1536]{2,1,0:T(8,128)(2,1)}, f32[2,80,1536]{2,1,0:T(8,128)}, f32[192,1024]{1,0:T(8,128)}, f32[192,1024]{1,0:T(8,128)}, f32[192,1024]{1,0:T(...) custom-call(bf16[2,80,1536]{2,1,0:T(8,128)(2,1)} %refs_0_.1, bf16[2,80,1536]{2,1,0:T(8,128)(2,1)} %refs_1_.1, ...), custom_call_target="tpu_custom_call" | custom-call | tf_op jit(solution)/shard_map/block/pallas_call | solution.py:1080
  371.9 1.5 copy.61
  373.5 0.9 copy.63
  374.4 0.8 copy.64
  375.2 0.8 copy.65
  376.0 0.2 copy.62
  376.2 0.9 copy.66
  377.1 0.6 fusion.4
  377.8 0.8 copy.72
  378.6 0.9 copy.73
  379.5 0.5 copy-done.3
  380.0 0.9 copy.74
  380.9 0.5 copy-done.2
  381.5 0.9 copy.75
  382.3 0.5 copy-done.1
  382.9 0.9 copy.76
  (42 shorter events, 1.0 us)
Async XLA Ops:
  7.3 2.6 copy-start.8
  7.3 2.7 copy-start.10
  7.3 2.8 copy-start.11
  10.4 1.1 copy-start.6
  10.4 1.1 copy-start.7
  10.5 2.0 copy-start.9
  373.5 2.5 copy-start.5
  376.0 1.1 copy-start.12
  376.0 1.8 copy-start.4
  376.2 2.3 copy-start
  378.6 1.5 copy-start.3
  380.0 1.4 copy-start.2
  381.5 1.4 copy-start.1

commit v3 on v2

--- a/solution.py
+++ b/solution.py
@@ -249,9 +249,9 @@
     (rows, seq, width, shard, qp, kp, ff, groups) = dims
     (tok, cot, wg_h, wi_h, wo_h, wu_h, wd_h, ordr, cols, cosr, sinr) = refs[:11]
     (out_h, gtok_h, gdown_h, ggate_h, gup_h, gout_h, gin_h, ggain_h) = refs[11:19]
-    (wgn, wi, wo, wu, wd, xf, n1, n2, gf, qkv, ob, dob, act, dgu, pr, hb, dh, pa, pb, ra, rb,
+    (wgn, wi, wo, wu, wd, xf, n1, n2, gf, qkv, ob, dob, act, dq3, dgu, pr, hb, dh, pa, pb, ra, rb,
      gb, xb, hop, fin, stage, acc, gains, gsum, gex, ybuf, tbuf,
-     wsend, wrecv, zsend, zrecv, rsend, rrecv, gsend, grecv, esend, erecv, lsem, osem, credit, zfree) = refs[19:]
+     wsend, wrecv, zsend, zrecv, rsend, rrecv, gsend, grecv, esend, erecv, lsem, osem, credit) = refs[19:]
     ghf = xf
     heads = qp // LANES
     per_group = heads // groups
@@ -277,13 +277,13 @@
         )
 
     barrier = pltpu.get_barrier_semaphore()
-    for dev in (pp, aa, bb):
-        pl.semaphore_signal(barrier, inc=1, device_id={"dp": dev}, device_id_type=MESH)
+    for step in range(1, 8):
+        pl.semaphore_signal(barrier, inc=1, device_id={"dp": (d + step) % 8}, device_id_type=MESH)
     for step in (1, 2, 3):
         pl.semaphore_signal(
             barrier, inc=1, device_id={"tensor": (z + step) % 4}, device_id_type=MESH
         )
-    pl.semaphore_wait(barrier, 6)
+    pl.semaphore_wait(barrier, 10)
 
     wunits = ((wg_h, wgn, 16), (wi_h, wi, shard), (wo_h, wo, shard), (wu_h, wu, shard), (wd_h, wd, shard))
 
@@ -365,6 +365,14 @@
         if zhbm[u] is not None:
             pltpu.make_async_copy(zhbm[u].at[s], zblk(u, s, z), lsem.at[8 + 2 * u + s]).wait()
 
+    def ag(u, s, t):
+        if t == 0:
+            zag_start(u, s)
+        elif t < 3:
+            zag_fwd(u, s, t)
+        else:
+            zag_done(u, s)
+
     def zag_sent(u, s):
         for k in range(3):
             for way in (0, 1):
@@ -377,108 +385,71 @@
                         zblk(u, s, i), zblk(u, s, i), zsend.at[u, s, way, k], zrecv.at[u, s, way, k], zdev[way]
                     ).wait_send()
 
-    zpart = (pa, pb, pa, pb)
-    zgot = (ra, rb, ra, rb)
-
-    def pblk(u, s, i):
-        return zpart[u].at[pl.ds(al(s * seq + i * rows, 16), rows)]
-
-    def rblk(u, s, way, i):
-        return zgot[u].at[s, way, i]
-
-    def rs_copy(u, s, way, k):
-        dest = 3 - k if way == 0 else k
-        slot = dest - 1 if way == 0 else dest
+    zpart = (pa, pb, pa, pa)
+    zgot = (ra, rb, ra, ra)
+
+    def rs_copy(u, s, way, t, dest):
         return rcopy(
-            pblk(u, s, dest), rblk(u, s, way, slot), rsend.at[u, s, way, k], rrecv.at[u, s, way, k], zdev[way]
+            zpart[u].at[pl.ds(al(s * seq + dest * rows, 16), rows)],
+            zgot[u].at[s, way, t],
+            rsend.at[u, s, way, t],
+            rrecv.at[u, s, way, t],
+            zdev[way],
         )
 
-    def add_rows(u, s, dest, way, slot):
-        base = s * seq + dest * rows
-
-        def body(i, carry):
-            at = pl.ds(al(base + i * 16, 16), 16)
-            got = zgot[u][s, way, slot, pl.ds(al(i * 16, 16), 16), :]
-            zpart[u][at, :] = (zpart[u][at, :].astype(F32) + got.astype(F32)).astype(BF)
-            return carry
-
-        lax.fori_loop(0, rows // 16, body, 0)
-
-    def rs_step(u, s, k):
-        if u == 3 and k == 0:
-            @pl.when(z > 0)
-            def _():
-                pl.semaphore_wait(zfree.at[s, 0], 1)
-
-            @pl.when(z < 3)
-            def _():
-                pl.semaphore_wait(zfree.at[s, 1], 1)
-
+    def rs(u, s, t):
         for way in (0, 1):
-            dest = 3 - k if way == 0 else k
-            slot = dest - 1 if way == 0 else dest
-            sends = (z < dest) if way == 0 else (z > dest)
-            inner = (z > 0) if way == 0 else (z < 3)
-
-            @pl.when(sends)
-            def _():
-                @pl.when(inner)
+            from_end = z if way == 0 else 3 - z
+
+            def wait_and(target, base):
+                rs_copy(u, s, way, t - 1, z).wait_recv()
+
+                def body(i, carry):
+                    at = pl.ds(al(base + i * 16, 16), 16)
+                    got = zgot[u][s, way, t - 1, pl.ds(al(i * 16, 16), 16), :].astype(F32)
+                    target[at, :] = (target[at, :].astype(F32) + got).astype(target.dtype)
+                    return carry
+
+                lax.fori_loop(0, rows // 16, body, 0)
+
+            if t == 3:
+                if way == 0:
+                    def first(i, carry):
+                        at = pl.ds(al(i * 16, 16), 16)
+                        acc[at, :] = zpart[u][pl.ds(al(s * seq + own + i * 16, 16), 16), :].astype(F32)
+                        return carry
+
+                    lax.fori_loop(0, rows // 16, first, 0)
+
+                @pl.when(from_end > 0)
                 def _():
-                    rs_copy(u, s, way, k).wait_recv()
-                    add_rows(u, s, dest, way, slot)
-
-                rs_copy(u, s, way, k).start()
-
-    def rs_final(u, s):
-        def first(i, carry):
-            at = pl.ds(al(i * 16, 16), 16)
-            acc[at, :] = zpart[u][pl.ds(al(s * seq + own + i * 16, 16), 16), :].astype(F32)
-            return carry
-
-        lax.fori_loop(0, rows // 16, first, 0)
-        for way in (0, 1):
-            there = (z > 0) if way == 0 else (z < 3)
-            slot = z - 1 if way == 0 else z
-            k = 3 - z if way == 0 else z
-
-            @pl.when(there)
-            def _():
-                rcopy(
-                    pblk(u, s, z), rblk(u, s, way, slot), rsend.at[u, s, way, k], rrecv.at[u, s, way, k], zdev[way]
-                ).wait_recv()
-
-                def more(i, carry):
-                    at = pl.ds(al(i * 16, 16), 16)
-                    acc[at, :] += zgot[u][s, way, slot, at, :].astype(F32)
-                    return carry
-
-                lax.fori_loop(0, rows // 16, more, 0)
-
-        if u == 1:
-            @pl.when(z < 3)
-            def _():
-                pl.semaphore_signal(zfree.at[s, 0], inc=1, device_id=zdev[0], device_id_type=MESH)
-
-            @pl.when(z > 0)
-            def _():
-                pl.semaphore_signal(zfree.at[s, 1], inc=1, device_id=zdev[1], device_id_type=MESH)
+                    wait_and(acc, 0)
+            else:
+                dest = 3 + z - t if way == 0 else t - from_end
+
+                @pl.when(from_end <= t)
+                def _():
+                    if t > 0:
+                        @pl.when(from_end > 0)
+                        def _():
+                            wait_and(zpart[u], s * seq + dest * rows)
+
+                    rs_copy(u, s, way, t, dest).start()
 
     def rs_sent(u, s):
         for way in (0, 1):
-            for k in range(3):
-                dest = 3 - k if way == 0 else k
-                sends = (z < dest) if way == 0 else (z > dest)
-
-                @pl.when(sends)
+            from_end = z if way == 0 else 3 - z
+            for t in range(3):
+                @pl.when(from_end <= t)
                 def _():
-                    rs_copy(u, s, way, k).wait_send()
+                    rs_copy(u, s, way, t, z).wait_send()
 
     gunits = (
         (gf, act, 0, ff, gdown_h),
         (n2, dgu, 0, ff, ggate_h),
         (n2, dgu, ff, ff, gup_h),
         (ghf, ob, 0, qp, gout_h),
-        (n1, act, 0, inw, gin_h),
+        (n1, dq3, 0, inw, gin_h),
     )
     pair = 2 * shard
 
@@ -737,11 +708,11 @@
                 dv = dv + tn(p.astype(BF), do)
                 dk = dk + tn(ds, q)
                 dq = nn(ds, k) * head_scale
-                act[at, hat] = (dq * cosine - pltpu.roll(dq, LANES // 2, 1) * sine).astype(BF)
-            act[at, pl.ds(al(qp + g * LANES, LANES), LANES)] = (
+                dq3[at, hat] = (dq * cosine - pltpu.roll(dq, LANES // 2, 1) * sine).astype(BF)
+            dq3[at, pl.ds(al(qp + g * LANES, LANES), LANES)] = (
                 dk * cosine - pltpu.roll(dk, LANES // 2, 1) * sine
             ).astype(BF)
-            act[at, pl.ds(al(qp + kp + g * LANES, LANES), LANES)] = dv.astype(BF)
+            dq3[at, pl.ds(al(qp + kp + g * LANES, LANES), LANES)] = dv.astype(BF)
             return carry
 
         lax.fori_loop(0, groups, body, 0)
@@ -766,190 +737,191 @@
         ).start()
         return total
 
+    X, COT, N2, GH = 0, 1, 2, 3
+    BR, FFN, DN2, DN1 = 0, 1, 2, 3
+
+    def attn_grad(s):
+        grad_heads(s)
+        attend_back(s)
+        rs_sent(DN2, s)
+        spread(s, pa, dq3, wi, 512)
+
     for s in (0, 1):
         pltpu.make_async_copy(tok.at[s], tbuf.at[s], lsem.at[5 + s]).start()
-    zag_start(0, 0)
     w_start(0)
+    ag(X, 0, 0)
     w_start(1)
+    ag(X, 0, 1)
+    w_relay(0)
+    w_diag(0)
+    ag(X, 0, 2)
+    ag(X, 1, 0)
+    w_relay(1)
     w_start(2)
-    zag_fwd(0, 0, 1)
-    zag_start(0, 1)
-    w_relay(0)
-    w_relay(1)
-    w_start(3)
-    zag_fwd(0, 0, 2)
-    zag_fwd(0, 1, 1)
-    w_relay(2)
-    w_start(4)
-    w_diag(0)
-    w_diag(1)
-    w_diag(2)
     w_done(0)
     for j in range(4):
         at = pl.ds(j * pair, pair)
         gains[:, at] = (
             wgn[pl.ds(32 * j, 16), :].astype(F32) + wgn[pl.ds(32 * j + 16, 16), :].astype(F32)
         )
-    zag_done(0, 0)
-    zag_fwd(0, 1, 2)
-    zag_start(1, 0)
+    ag(X, 0, 3)
     norm1(0)
+    ag(X, 1, 1)
+    w_diag(1)
+    w_relay(2)
+    w_start(3)
     w_done(1)
     project(0)
-    w_relay(3)
-    zag_done(0, 1)
-    zag_fwd(1, 0, 1)
-    zag_start(1, 1)
+    w_diag(2)
     attend(0)
+    ag(X, 1, 2)
     w_done(2)
     spread(0, pa, ob, wo, 512)
-    rs_step(0, 0, 0)
-    zag_fwd(1, 0, 2)
-    zag_fwd(1, 1, 1)
-    w_relay(4)
-    w_diag(3)
+    rs(BR, 0, 0)
+    w_start(4)
+    ag(X, 1, 3)
+    rs(BR, 0, 1)
+    ag(COT, 0, 0)
     norm1(1)
-    rs_step(0, 0, 1)
     project(1)
-    rs_step(0, 0, 2)
-    zag_fwd(1, 1, 2)
+    rs(BR, 0, 2)
+    ag(COT, 0, 1)
     attend(1)
     for s in (0, 1):
         pltpu.make_async_copy(tok.at[s], tbuf.at[s], lsem.at[5 + s]).wait()
-        zag_sent(0, s)
+    rs(BR, 0, 3)
+    norm2(0)
+    ag(N2, 0, 0)
+    ag(COT, 0, 2)
     spread(1, pa, ob, wo, 512)
-    rs_step(0, 1, 0)
-    rs_final(0, 0)
-    norm2(0)
-    zag_start(2, 0)
+    rs(BR, 1, 0)
+    ag(N2, 0, 1)
+    w_relay(3)
+    ag(COT, 0, 3)
+    zag_sent(COT, 0)
+    mask_grad(0)
+    rs(BR, 1, 1)
+    ag(N2, 0, 2)
+    w_relay(4)
+    w_diag(3)
+    rs(BR, 1, 2)
+    ag(COT, 1, 0)
     w_diag(4)
-    zag_done(1, 0)
-    mask_prep = mask_grad
-    rs_step(0, 1, 1)
-    zag_fwd(2, 0, 1)
-    rs_step(0, 1, 2)
-    zag_sent(1, 0)
-    mask_prep(0)
-    rs_final(0, 1)
-    norm2(1)
-    zag_start(2, 1)
-    zag_fwd(2, 0, 2)
-    zag_done(1, 1)
-    zag_fwd(2, 1, 1)
-    zag_sent(1, 1)
-    mask_prep(1)
+    ag(N2, 0, 3)
     w_done(3)
     w_done(4)
-    rs_sent(0, 0)
-    rs_sent(0, 1)
-    zag_done(2, 0)
     feed(0)
-    zag_fwd(2, 1, 2)
+    rs(BR, 1, 3)
+    norm2(1)
+    ag(N2, 1, 0)
+    ag(COT, 1, 1)
+    zag_sent(X, 0)
+    rs_sent(BR, 0)
     spread(0, pa, dgu, wu, 256)
-    rs_step(2, 0, 0)
-    zag_done(2, 1)
+    rs(DN2, 0, 0)
+    ag(N2, 1, 1)
+    rs(DN2, 0, 1)
+    ag(COT, 1, 2)
     spread(0, pb, act, wd, 512)
-    rs_step(2, 0, 1)
+    ag(N2, 1, 2)
+    rs(DN2, 0, 2)
+    ag(COT, 1, 3)
+    zag_sent(COT, 1)
+    mask_grad(1)
+    ag(N2, 1, 3)
+    rs(DN2, 0, 3)
+    gain2 = norm2_back(0)
+    ag(GH, 0, 0)
+    rs(FFN, 0, 0)
     feed(1)
-    rs_step(2, 0, 2)
+    zag_sent(X, 1)
+    rs_sent(BR, 1)
     spread(1, pa, dgu, wu, 256)
-    rs_step(2, 1, 0)
-    rs_final(2, 0)
-    gain2 = norm2_back(0)
-    zag_start(3, 0)
-    rs_step(1, 0, 0)
+    rs(DN2, 1, 0)
+    ag(GH, 0, 1)
+    rs(FFN, 0, 1)
     spread(1, pb, act, wd, 512)
-    rs_step(2, 1, 1)
-    zag_fwd(3, 0, 1)
+    rs(DN2, 1, 1)
+    ag(GH, 0, 2)
+    rs(FFN, 0, 2)
     g_compute(0)
-    rs_step(2, 1, 2)
-    zag_fwd(3, 0, 2)
-    rs_step(1, 1, 0)
-    rs_final(2, 1)
+    rs(DN2, 1, 2)
+    ag(GH, 0, 3)
+    attn_grad(0)
+    rs(DN1, 0, 0)
+    rs(FFN, 0, 3)
+    finish_out(0)
+    rs(DN2, 1, 3)
     gain2 = gain2 + norm2_back(1)
-    for j in range(4):
-        gsum[4 + j : 5 + j, :] = gain2[:, j * pair : (j + 1) * pair]
-    zag_start(3, 1)
+    ag(GH, 1, 0)
+    rs(DN1, 0, 1)
     g_first(0)
     g_compute(1)
-    rs_step(1, 0, 1)
-    zag_fwd(3, 1, 1)
-    zag_done(3, 0)
-    grad_heads(0)
-    rs_step(1, 0, 2)
-    rs_step(1, 1, 1)
-    zag_fwd(3, 1, 2)
-    rs_step(1, 1, 2)
+    ag(GH, 1, 1)
+    rs(DN1, 0, 2)
     g_second(0)
     g_first(1)
-    rs_final(1, 0)
-    finish_out(0)
-    rs_final(1, 1)
-    finish_out(1)
-    rs_sent(1, 0)
-    rs_sent(1, 1)
+    ag(GH, 1, 2)
     g_finish(0)
     g_compute(2)
-    attend_back(0)
-    spread(0, pb, act, wi, 512)
-    rs_step(3, 0, 0)
+    rs(DN1, 0, 3)
+    gain1 = norm1_back(0)
+    rs(FFN, 1, 0)
     g_second(1)
+    ag(GH, 1, 3)
+    attn_grad(1)
+    rs(DN1, 1, 0)
+    rs(FFN, 1, 1)
     g_first(2)
-    zag_done(3, 1)
-    grad_heads(1)
-    rs_step(3, 0, 1)
-    attend_back(1)
-    rs_step(3, 0, 2)
-    spread(1, pb, act, wi, 512)
-    rs_step(3, 1, 0)
     g_finish(1)
+    g_compute(3)
+    rs(DN1, 1, 1)
+    rs(FFN, 1, 2)
     g_second(2)
-    g_compute(3)
-    rs_step(3, 1, 1)
     g_first(3)
     g_finish(2)
     g_compute(4)
-    rs_step(3, 1, 2)
+    rs(DN1, 1, 2)
+    g_second(3)
     g_first(4)
-    g_second(3)
-    rs_final(3, 0)
-    gain1 = norm1_back(0)
-    g_second(4)
+    rs(FFN, 1, 3)
+    finish_out(1)
     g_finish(3)
-    rs_final(3, 1)
+    rs(DN1, 1, 3)
     gain1 = gain1 + norm1_back(1)
     for j in range(4):
         gsum[j : j + 1, :] = gain1[:, j * pair : (j + 1) * pair]
-
-    def e_copy(i, dev, src):
+        gsum[4 + j : 5 + j, :] = gain2[:, j * pair : (j + 1) * pair]
+
+    def e_copy(i, src):
+        dev = {"tensor": (z + i + 1) % 4} if i < 3 else {"dp": (d + i - 2) % 8}
         return rcopy(src, gex.at[i], esend.at[i], erecv.at[i], dev)
 
-    for step in (1, 2, 3):
-        e_copy(step - 1, {"tensor": (z + step) % 4}, gsum).start()
-    for step in (1, 2, 3):
-        e_copy(step - 1, {"tensor": (z + step) % 4}, gsum).wait()
-    gsum2 = gsum[...] + gex[0] + gex[1] + gex[2]
-    gex[6] = gsum2
-    e_copy(3, {"dp": pp}, gex.at[6]).start()
+    for i in range(3):
+        e_copy(i, gsum).start()
+    g_second(4)
+    for i in range(3):
+        e_copy(i, gsum).wait()
+    gex[10] = gsum[...] + gex[0] + gex[1] + gex[2]
+    for i in range(3, 10):
+        e_copy(i, gex.at[10]).start()
     g_finish(4)
-    e_copy(3, {"dp": pp}, gex.at[6]).wait()
-    gex[7] = gex[6] + gex[3]
-    e_copy(4, {"dp": aa}, gex.at[7]).start()
-    e_copy(4, {"dp": aa}, gex.at[7]).wait()
-    gex[8] = gex[7] + gex[4]
-    e_copy(5, {"dp": bb}, gex.at[8]).start()
-    e_copy(5, {"dp": bb}, gex.at[8]).wait()
-    gsum[...] = gex[8] + gex[5]
+    for i in range(3, 10):
+        e_copy(i, gex.at[10]).wait()
+    total = gex[10]
+    for i in range(3, 10):
+        total = total + gex[i]
+    gsum[...] = total
     last = pltpu.make_async_copy(gsum, ggain_h, osem.at[9])
     last.start()
     for u in range(5):
         w_sent(u)
-    for u in (2, 3):
+    for u in (N2, GH):
         for s in (0, 1):
             zag_sent(u, s)
-    for u in (2, 3):
-        for s in (0, 1):
-            rs_sent(u, s)
+    for s in (0, 1):
+        rs_sent(FFN, s)
+        rs_sent(DN1, s)
     g_out(3).wait()
     g_out(4).wait()
     for s in (0, 1):
@@ -1030,6 +1002,7 @@
         vm((total, qp), BF),
         vm((total, qp), BF),
         vm((total, ff), BF),
+        vm((total, inw), BF),
         vm((total, 2 * ff), BF),
         vm((micro * qp // LANES, seq, seq), F32),
         vm((micro * rows, width), F32),
@@ -1046,7 +1019,7 @@
         vm((rows, width), F32),
         vm((16, width), F32),
         vm((8, width // 4), F32),
-        vm((9, 8, width // 4), F32),
+        vm((11, 8, width // 4), F32),
         vm((micro, rows, width), BF),
         vm((micro, rows, width), BF),
         dma((5, 7)),
@@ -1057,12 +1030,11 @@
         dma((4, 2, 2, 3)),
         dma((5, 7)),
         dma((5, 7)),
-        dma((6,)),
-        dma((6,)),
+        dma((10,)),
+        dma((10,)),
         dma((12,)),
         dma((10,)),
         pltpu.SemaphoreType.REGULAR((3,)),
-        pltpu.SemaphoreType.REGULAR((2, 2)),
     ]
     hbm = pl.BlockSpec(memory_space=pl.ANY)
     vmem = pl.BlockSpec(memory_space=pltpu.VMEM)

time: 387 us -> 287 us (0.74)
  Pallas kernels: 358 us -> 260 us
    pallas_call x1, Pallas kernels: 358 us -> 260 us  [fused(): pl.pallas_call(functools.partial(block_kernel, dims), out_shape=shapes, i...]
where the time goes in v3:
time: 287 us; the launch traced here: 286 us
  Pallas kernels  260 us (91%)
  local copies, waits for them, and re-layouts  17.2 us (6%)
  other arithmetic  7.19 us (3%)
    pallas_call x1, Pallas kernels, fused(): pl.pallas_call(functools.partial(block_kernel, dims), out_shape=shapes, i...  260 us
    unnamed x39, local copies, waits for them, and re-layouts  9.88 us

profile of v3, /device:TPU:0, one launch (start us, length us, event | category | flops | bytes accessed | tf_op | source)
XLA Modules:
  0.0 285.6 jit_solution(15259116183162759072)
XLA Ops:
  0.7 0.7 stack.17
  1.3 0.7 stack.18
  2.0 0.7 pad_select_fusion.refs_2_
  2.7 0.8 reduce_window_sum.11
  3.5 0.7 sub.6
  4.3 0.8 fusion.1
  5.2 0.8 subtract_convert_fusion
  6.0 1.2 multiply_sine_fusion
  7.3 1.1 pad_maximum_fusion.2
  8.4 0.9 copy.60.refs_8_
  9.3 0.6 broadcast_in_dim.14.refs_7_
  9.9 0.1 copy.53
  10.5 0.9 copy.58.refs_3_
  11.5 0.9 pad_maximum_fusion.refs_5_
  12.4 0.1 copy.56
  12.6 0.8 copy.59.refs_4_
  13.4 260.3 %block.1 = (bf16[2,80,1536]{2,1,0:T(8,128)(2,1)}, f32[2,80,1536]{2,1,0:T(8,128)}, f32[192,1024]{1,0:T(8,128)}, f32[192,1024]{1,0:T(8,128)}, f32[192,1024]{1,0:T(...) custom-call(bf16[2,80,1536]{2,1,0:T(8,128)(2,1)} %refs_0_.1, bf16[2,80,1536]{2,1,0:T(8,128)(2,1)} %refs_1_.1, ...), custom_call_target="tpu_custom_call" | custom-call | tf_op jit(solution)/shard_map/block/pallas_call | solution.py:1052
  273.8 1.5 copy.61
  275.4 0.9 copy.63
  276.3 0.8 copy.64
  277.1 0.8 copy.65
  277.9 0.2 copy.62
  278.1 0.9 copy.66
  279.0 0.6 fusion.4
  279.6 0.8 copy.72
  280.4 0.9 copy.73
  281.4 0.5 copy-done.3
  281.9 0.9 copy.74
  282.8 0.5 copy-done.2
  283.3 0.9 copy.75
  284.2 0.5 copy-done.1
  284.7 0.9 copy.76
  (42 shorter events, 1.0 us)
Async XLA Ops:
  7.3 2.6 copy-start.8
  7.3 2.7 copy-start.10
  7.3 2.8 copy-start.11
  10.4 1.1 copy-start.6
  10.4 1.1 copy-start.7
  10.5 2.0 copy-start.9
  275.4 2.5 copy-start.5
  277.9 1.1 copy-start.12
  277.9 1.8 copy-start.4
  278.1 2.3 copy-start
  280.4 1.5 copy-start.3
  281.9 1.4 copy-start.2
  283.3 1.4 copy-start.1

commit v4 on v3

--- a/solution.py
+++ b/solution.py
@@ -250,7 +250,7 @@
     (tok, cot, wg_h, wi_h, wo_h, wu_h, wd_h, ordr, cols, cosr, sinr) = refs[:11]
     (out_h, gtok_h, gdown_h, ggate_h, gup_h, gout_h, gin_h, ggain_h) = refs[11:19]
     (wgn, wi, wo, wu, wd, xf, n1, n2, gf, qkv, ob, dob, act, dq3, dgu, pr, hb, dh, pa, pb, ra, rb,
-     gb, xb, hop, fin, stage, acc, gains, gsum, gex, ybuf, tbuf,
+     gb, xb, hop, fin, stage, acc, gains, gpart, gsum, gex, ybuf, tbuf,
      wsend, wrecv, zsend, zrecv, rsend, rrecv, gsend, grecv, esend, erecv, lsem, osem, credit) = refs[19:]
     ghf = xf
     heads = qp // LANES
@@ -301,10 +301,12 @@
     def w_wait(u, slot, i):
         rcopy(wblk(u, i), wblk(u, i), wsend.at[u, 0], wrecv.at[u, slot], {"dp": aa}).wait_recv()
 
-    def w_relay(u):
+    def w_relayb(u):
         w_wait(u, 1, bb)
         rcopy(wblk(u, bb), wblk(u, bb), wsend.at[u, 3], wrecv.at[u, 2], {"dp": aa}).start()
         rcopy(wblk(u, bb), wblk(u, bb), wsend.at[u, 4], wrecv.at[u, 5], {"dp": pp}).start()
+
+    def w_relaya(u):
         w_wait(u, 0, aa)
         rcopy(wblk(u, aa), wblk(u, aa), wsend.at[u, 5], wrecv.at[u, 4], {"dp": pp}).start()
 
@@ -354,24 +356,16 @@
         for way in (0, 1):
             zag_send(u, s, 0, way)
 
-    def zag_fwd(u, s, k):
-        for way in (0, 1):
-            zag_recv(u, s, k - 1, way)
-            zag_send(u, s, k, way)
-
-    def zag_done(u, s):
-        for way in (0, 1):
-            zag_recv(u, s, 2, way)
-        if zhbm[u] is not None:
-            pltpu.make_async_copy(zhbm[u].at[s], zblk(u, s, z), lsem.at[8 + 2 * u + s]).wait()
-
-    def ag(u, s, t):
+    def ag(u, s, t, way=None):
         if t == 0:
             zag_start(u, s)
-        elif t < 3:
-            zag_fwd(u, s, t)
-        else:
-            zag_done(u, s)
+            return
+        zag_recv(u, s, t - 1, way)
+        if t < 3:
+            zag_send(u, s, t, way)
+
+    def own_here(u, s):
+        pltpu.make_async_copy(zhbm[u].at[s], zblk(u, s, z), lsem.at[8 + 2 * u + s]).wait()
 
     def zag_sent(u, s):
         for k in range(3):
@@ -397,8 +391,8 @@
             zdev[way],
         )
 
-    def rs(u, s, t):
-        for way in (0, 1):
+    def rs(u, s, t, ways=(0, 1)):
+        for way in ways:
             from_end = z if way == 0 else 3 - z
 
             def wait_and(target, base):
@@ -466,21 +460,21 @@
 
     chips = (chip_d, chip_x, chip_y, chip_own)
 
-    def g_compute(u):
+    def g_compute(u, i):
         left, right, at, n, _ = gunits[u]
-        if u >= 2:
+        chip = chips[i]
+        if u >= 2 and i == 0:
             pl.semaphore_wait(credit.at[0], 1)
-        for i, chip in enumerate(chips):
-            tile = 256
-
-            def body(j, carry):
-                lhs = left[:, pl.ds(al(chip * pair, LANES), pair)]
-                got = tn(lhs, right[:, pl.ds(al(at + j * tile, tile), tile)])
-                gb[u % 2, pl.ds(al(chip * pair, 16), pair), pl.ds(al(j * tile, tile), tile)] = got.astype(BF)
-                return carry
-
-            lax.fori_loop(0, n // tile, body, 0)
-            g_exchange(u, chip, i).start()
+        tile = 256
+
+        def body(j, carry):
+            lhs = left[:, pl.ds(al(chip * pair, LANES), pair)]
+            got = tn(lhs, right[:, pl.ds(al(at + j * tile, tile), tile)])
+            gb[u % 2, pl.ds(al(chip * pair, 16), pair), pl.ds(al(j * tile, tile), tile)] = got.astype(BF)
+            return carry
+
+        lax.fori_loop(0, n // tile, body, 0)
+        g_exchange(u, chip, i).start()
 
     def g_add(u, chip, extra=None):
         b, n = u % 2, gunits[u][3]
@@ -513,6 +507,8 @@
         if u >= 2:
             pl.semaphore_wait(credit.at[1], 1)
         g_hop(u).start()
+
+    def g_firstb(u):
         g_exchange(u, chip_x, 1).wait_recv()
         g_exchange(u, chip_y, 2).wait_recv()
         g_add(u, chip_a)
@@ -557,17 +553,38 @@
         b, n, out = u % 2, gunits[u][3], gunits[u][4]
         return pltpu.make_async_copy(stage.at[b, :, pl.ds(0, n)], out, osem.at[u])
 
-    def norm1(s):
+    def gain_rows():
+        for j in range(4):
+            at = pl.ds(j * pair, pair)
+            gains[:, at] = (
+                wgn[pl.ds(32 * j, 16), :].astype(F32) + wgn[pl.ds(32 * j + 16, 16), :].astype(F32)
+            )
+
+    def norm1(s, t):
         gain = gains[0:1, :]
 
-        def body(i, carry):
-            at = pl.ds(al(s * seq + i * 16, 16), 16)
-            x = xf[at, :].astype(F32)
-            scale = lax.rsqrt(jnp.mean(x * x, axis=-1, keepdims=True) + eps)
-            n1[at, :] = (x * scale * gain).astype(BF)
-            return carry
-
-        lax.fori_loop(0, seq // 16, body, 0)
+        def shard_rows(i):
+            def body(r, carry):
+                at = pl.ds(al(s * seq + i * rows + r * 16, 16), 16)
+                x = xf[at, :].astype(F32)
+                scale = lax.rsqrt(jnp.mean(x * x, axis=-1, keepdims=True) + eps)
+                n1[at, :] = (x * scale * gain).astype(BF)
+                return carry
+
+            lax.fori_loop(0, rows // 16, body, 0)
+
+        if t == 0:
+            own_here(0, s)
+            shard_rows(z)
+            return
+
+        @pl.when(z - t >= 0)
+        def _():
+            shard_rows(z - t)
+
+        @pl.when(z + t <= 3)
+        def _():
+            shard_rows(z + t)
 
     head_scale = HEAD ** (-0.5)
 
@@ -628,25 +645,19 @@
 
         lax.fori_loop(0, rows // 16, body, 0)
 
-    def mask_grad(s):
-        def body(i, carry):
-            at = pl.ds(al(s * seq + i * 16, 16), 16)
-            gf[at, :] = (gf[at, :].astype(F32) * cols[s, pl.ds(al(i * 16, 16), 16), 2:3]).astype(BF)
-            return carry
-
-        lax.fori_loop(0, seq // 16, body, 0)
-
     def feed(s):
         at = pl.ds(s * seq, seq)
+        real = cols[s, :, 2:3]
+        own_here(1, s)
 
         def body(t, carry):
             col = al(t * 256, 256)
             gate = nn(n2[at, :], wu[:, pl.ds(col, 256)])
             upper = nn(n2[at, :], wu[:, pl.ds(al(ff + t * 256, 256), 256)])
-            back = nn(gf[at, :], wd[:, pl.ds(col, 256)])
+            back = nn(gf[at, :], wd[:, pl.ds(col, 256)]) * real
             sigma = 1.0 / (1.0 + jnp.exp(-gate))
             swish = gate * sigma
-            act[at, pl.ds(col, 256)] = (swish * upper).astype(BF)
+            act[at, pl.ds(col, 256)] = (swish * upper * real).astype(BF)
             dgu[at, pl.ds(col, 256)] = (back * upper * sigma * (1.0 + gate * (1.0 - sigma))).astype(BF)
             dgu[at, pl.ds(al(ff + t * 256, 256), 256)] = (back * swish).astype(BF)
             return carry
@@ -676,12 +687,13 @@
             grad = acc[r, :]
             inner = grad * gain
             dy = gf[pl.ds(al(s * seq + own + i * 16, 16), 16), :].astype(F32)
+            dy = dy * cols[s, pl.ds(al(own + i * 16, 16), 16), 2:3]
             dhr = dy + scale * (inner - unit * jnp.mean(inner * unit, axis=-1, keepdims=True))
             dh[ro, :] = dhr
             ghf[pl.ds(al(s * seq + own + i * 16, 16), 16), :] = dhr.astype(BF)
             return carry + jnp.sum(grad * unit, axis=0, keepdims=True)
 
-        return lax.fori_loop(0, rows // 16, body, jnp.zeros((1, width), F32))
+        gpart[1:2, :] += lax.fori_loop(0, rows // 16, body, jnp.zeros((1, width), F32))
 
     def grad_heads(s):
         at = pl.ds(s * seq, seq)
@@ -731,192 +743,279 @@
             dh[ro, :] = dh[ro, :] + scale * (inner - unit * jnp.mean(inner * unit, axis=-1, keepdims=True))
             return carry + jnp.sum(grad * unit, axis=0, keepdims=True)
 
-        total = lax.fori_loop(0, rows // 16, body, jnp.zeros((1, width), F32))
+        gpart[0:1, :] += lax.fori_loop(0, rows // 16, body, jnp.zeros((1, width), F32))
         pltpu.make_async_copy(
             dh.at[pl.ds(s * rows, rows)], gtok_h.at[s], osem.at[7 + s]
         ).start()
-        return total
 
     X, COT, N2, GH = 0, 1, 2, 3
     BR, FFN, DN2, DN1 = 0, 1, 2, 3
 
-    def attn_grad(s):
-        grad_heads(s)
-        attend_back(s)
-        rs_sent(DN2, s)
-        spread(s, pa, dq3, wi, 512)
-
+    def tok_copy(s):
+        return pltpu.make_async_copy(tok.at[s], tbuf.at[s], lsem.at[5 + s])
+
+    def fin_br(s):
+        rs(BR, s, 3)
+        tok_copy(s).wait()
+        norm2(s)
+        ag(N2, s, 0)
+
+    def fin_dn2(s):
+        rs(DN2, s, 3)
+        norm2_back(s)
+        ag(GH, s, 0)
+
+    def fin_ffn(s):
+        rs(FFN, s, 3)
+        finish_out(s)
+
+    def fin_dn1(s):
+        rs(DN1, s, 3)
+        norm1_back(s)
+
+    def e_copy(i):
+        dev = {"tensor": (z + i + 1) % 4} if i < 3 else {"dp": (d + i - 2) % 8}
+        return rcopy(gsum if i < 3 else gex.at[10], gex.at[i], esend.at[i], erecv.at[i], dev)
+
+    def e1s():
+        for j in range(4):
+            gsum[j : j + 1, :] = gpart[0:1, j * pair : (j + 1) * pair]
+            gsum[4 + j : 5 + j, :] = gpart[1:2, j * pair : (j + 1) * pair]
+        for i in range(3):
+            e_copy(i).start()
+
+    def e1w():
+        for i in range(3):
+            e_copy(i).wait()
+        gex[10] = gsum[...] + gex[0] + gex[1] + gex[2]
+        for i in range(3, 10):
+            e_copy(i).start()
+
+    def e2w():
+        for i in range(3, 10):
+            e_copy(i).wait()
+        total = gex[10]
+        for i in range(3, 10):
+            total = total + gex[i]
+        gsum[...] = total
+
+    gpart[...] = jnp.zeros_like(gpart)
     for s in (0, 1):
-        pltpu.make_async_copy(tok.at[s], tbuf.at[s], lsem.at[5 + s]).start()
+        tok_copy(s).start()
+    ag(X, 0, 0)
     w_start(0)
-    ag(X, 0, 0)
     w_start(1)
-    ag(X, 0, 1)
-    w_relay(0)
+    ag(X, 1, 0)
+    w_start(2)
+    w_relayb(1)
+    ag(X, 0, 1, 1)
+    ag(X, 0, 1, 0)
+    ag(X, 1, 1, 0)
+    ag(X, 1, 1, 1)
+    w_relaya(0)
+    w_diag(1)
+    w_relayb(0)
+    ag(X, 0, 2, 0)
     w_diag(0)
-    ag(X, 0, 2)
-    ag(X, 1, 0)
-    w_relay(1)
-    w_start(2)
+    w_relaya(1)
+    w_relayb(2)
+    w_start(3)
+    ag(X, 0, 2, 1)
     w_done(0)
-    for j in range(4):
-        at = pl.ds(j * pair, pair)
-        gains[:, at] = (
-            wgn[pl.ds(32 * j, 16), :].astype(F32) + wgn[pl.ds(32 * j + 16, 16), :].astype(F32)
-        )
-    ag(X, 0, 3)
-    norm1(0)
-    ag(X, 1, 1)
-    w_diag(1)
-    w_relay(2)
-    w_start(3)
+    gain_rows()
+    ag(COT, 0, 0)
+    norm1(0, 1)
+    ag(X, 1, 2, 0)
+    norm1(0, 0)
+    ag(COT, 1, 0)
+    w_relaya(2)
+    norm1(1, 0)
+    ag(X, 1, 2, 1)
     w_done(1)
+    ag(X, 0, 3, 0)
+    w_diag(2)
+    ag(X, 0, 3, 1)
+    norm1(0, 2)
+    norm1(0, 3)
     project(0)
-    w_diag(2)
+    w_done(2)
     attend(0)
-    ag(X, 1, 2)
-    w_done(2)
     spread(0, pa, ob, wo, 512)
-    rs(BR, 0, 0)
+    rs(BR, 0, 0, (1,))
+    ag(COT, 0, 1, 1)
+    rs(BR, 0, 0, (0,))
+    ag(COT, 0, 1, 0)
+    rs(BR, 0, 1, (0,))
+    norm1(1, 1)
+    w_relaya(3)
+    rs(BR, 0, 1, (1,))
+    w_relayb(3)
+    rs(BR, 0, 2, (0,))
+    ag(X, 1, 3, 0)
+    ag(X, 1, 3, 1)
+    norm1(1, 3)
+    rs(BR, 0, 2, (1,))
+    norm1(1, 2)
+    project(1)
+    ag(COT, 0, 2, 0)
+    ag(COT, 0, 2, 1)
     w_start(4)
-    ag(X, 1, 3)
-    rs(BR, 0, 1)
-    ag(COT, 0, 0)
-    norm1(1)
-    project(1)
-    rs(BR, 0, 2)
-    ag(COT, 0, 1)
     attend(1)
-    for s in (0, 1):
-        pltpu.make_async_copy(tok.at[s], tbuf.at[s], lsem.at[5 + s]).wait()
-    rs(BR, 0, 3)
-    norm2(0)
-    ag(N2, 0, 0)
-    ag(COT, 0, 2)
+    fin_br(0)
+    rs_sent(BR, 0)
     spread(1, pa, ob, wo, 512)
-    rs(BR, 1, 0)
-    ag(N2, 0, 1)
-    w_relay(3)
-    ag(COT, 0, 3)
-    zag_sent(COT, 0)
-    mask_grad(0)
-    rs(BR, 1, 1)
-    ag(N2, 0, 2)
-    w_relay(4)
+    rs(BR, 1, 0, (0,))
+    w_relayb(4)
+    rs(BR, 1, 0, (1,))
+    ag(N2, 0, 1, 1)
+    ag(N2, 0, 1, 0)
     w_diag(3)
-    rs(BR, 1, 2)
-    ag(COT, 1, 0)
+    rs(BR, 1, 1, (1,))
+    w_relaya(4)
+    rs(BR, 1, 1, (0,))
+    zag_sent(X, 0)
+    ag(COT, 0, 3, 1)
+    ag(N2, 0, 2, 1)
     w_diag(4)
-    ag(N2, 0, 3)
+    ag(N2, 0, 2, 0)
+    w_done(4)
+    rs(BR, 1, 2, (1,))
+    ag(N2, 0, 3, 0)
+    rs(BR, 1, 2, (0,))
+    ag(COT, 1, 1, 0)
+    ag(N2, 0, 3, 1)
+    ag(COT, 1, 1, 1)
+    ag(COT, 0, 3, 0)
     w_done(3)
-    w_done(4)
     feed(0)
-    rs(BR, 1, 3)
-    norm2(1)
-    ag(N2, 1, 0)
-    ag(COT, 1, 1)
-    zag_sent(X, 0)
-    rs_sent(BR, 0)
+    fin_br(1)
     spread(0, pa, dgu, wu, 256)
-    rs(DN2, 0, 0)
-    ag(N2, 1, 1)
-    rs(DN2, 0, 1)
-    ag(COT, 1, 2)
+    rs(DN2, 0, 0, (0,))
+    ag(COT, 1, 2, 0)
+    ag(N2, 1, 1, 1)
+    rs(DN2, 0, 0, (1,))
+    ag(N2, 1, 1, 0)
+    rs_sent(BR, 1)
+    rs(DN2, 0, 1, (1,))
+    ag(COT, 1, 2, 1)
+    rs(DN2, 0, 1, (0,))
     spread(0, pb, act, wd, 512)
-    ag(N2, 1, 2)
-    rs(DN2, 0, 2)
-    ag(COT, 1, 3)
-    zag_sent(COT, 1)
-    mask_grad(1)
-    ag(N2, 1, 3)
-    rs(DN2, 0, 3)
-    gain2 = norm2_back(0)
-    ag(GH, 0, 0)
-    rs(FFN, 0, 0)
+    rs(FFN, 0, 0, (1,))
+    rs(FFN, 0, 0, (0,))
+    ag(N2, 1, 2, 1)
+    ag(N2, 1, 2, 0)
+    zag_sent(X, 1)
+    rs(DN2, 0, 2, (0,))
+    ag(COT, 1, 3, 0)
+    rs(DN2, 0, 2, (1,))
+    ag(COT, 1, 3, 1)
+    rs(FFN, 0, 1, (1,))
+    rs(FFN, 0, 1, (0,))
+    ag(N2, 1, 3, 0)
+    ag(N2, 1, 3, 1)
     feed(1)
-    zag_sent(X, 1)
-    rs_sent(BR, 1)
+    fin_dn2(0)
     spread(1, pa, dgu, wu, 256)
-    rs(DN2, 1, 0)
-    ag(GH, 0, 1)
-    rs(FFN, 0, 1)
+    g_compute(0, 0)
+    ag(GH, 0, 1, 1)
+    rs(DN2, 1, 0, (1,))
+    ag(GH, 0, 1, 0)
+    rs(DN2, 1, 0, (0,))
+    g_compute(0, 1)
+    g_compute(0, 2)
+    g_compute(0, 3)
+    rs(DN2, 1, 1, (1,))
+    g_first(0)
+    rs(DN2, 1, 1, (0,))
+    ag(GH, 0, 2, 0)
+    g_compute(1, 0)
+    ag(GH, 0, 2, 1)
+    rs(DN2, 1, 2, (1,))
+    rs(DN2, 1, 2, (0,))
     spread(1, pb, act, wd, 512)
-    rs(DN2, 1, 1)
-    ag(GH, 0, 2)
-    rs(FFN, 0, 2)
-    g_compute(0)
-    rs(DN2, 1, 2)
-    ag(GH, 0, 3)
-    attn_grad(0)
-    rs(DN1, 0, 0)
-    rs(FFN, 0, 3)
-    finish_out(0)
-    rs(DN2, 1, 3)
-    gain2 = gain2 + norm2_back(1)
-    ag(GH, 1, 0)
-    rs(DN1, 0, 1)
-    g_first(0)
-    g_compute(1)
-    ag(GH, 1, 1)
-    rs(DN1, 0, 2)
+    g_firstb(0)
+    rs(FFN, 1, 0, (1,))
+    rs_sent(DN2, 0)
     g_second(0)
+    ag(GH, 0, 3, 0)
+    g_compute(1, 1)
+    g_compute(1, 2)
+    g_compute(1, 3)
+    rs(FFN, 1, 0, (0,))
     g_first(1)
-    ag(GH, 1, 2)
+    ag(GH, 0, 3, 1)
+    fin_dn2(1)
+    grad_heads(0)
+    attend_back(0)
+    spread(0, pa, dq3, wi, 512)
+    rs(DN1, 0, 0, (0,))
     g_finish(0)
-    g_compute(2)
-    rs(DN1, 0, 3)
-    gain1 = norm1_back(0)
-    rs(FFN, 1, 0)
+    rs(DN1, 0, 0, (1,))
+    g_firstb(1)
+    g_compute(2, 0)
+    ag(GH, 1, 1, 0)
+    ag(GH, 1, 1, 1)
+    g_compute(2, 1)
+    rs(DN1, 0, 1, (0,))
+    rs(DN1, 0, 1, (1,))
+    g_first(2)
+    g_compute(2, 2)
+    ag(GH, 1, 2, 0)
+    rs(FFN, 1, 1, (0,))
+    g_compute(2, 3)
+    ag(GH, 1, 2, 1)
+    rs_sent(DN2, 1)
+    rs(FFN, 0, 2, (1,))
+    rs(FFN, 1, 1, (1,))
+    g_firstb(2)
+    g_second(2)
+    rs(FFN, 0, 2, (0,))
+    ag(GH, 1, 3, 0)
     g_second(1)
-    ag(GH, 1, 3)
-    attn_grad(1)
-    rs(DN1, 1, 0)
-    rs(FFN, 1, 1)
-    g_first(2)
+    ag(GH, 1, 3, 1)
+    grad_heads(1)
+    attend_back(1)
+    spread(1, pa, dq3, wi, 512)
+    rs(DN1, 1, 0, (1,))
+    rs(DN1, 1, 0, (0,))
     g_finish(1)
-    g_compute(3)
-    rs(DN1, 1, 1)
-    rs(FFN, 1, 2)
-    g_second(2)
+    g_compute(3, 0)
+    g_compute(3, 1)
+    rs(DN1, 1, 1, (0,))
     g_first(3)
+    rs(DN1, 1, 1, (1,))
     g_finish(2)
-    g_compute(4)
-    rs(DN1, 1, 2)
+    rs(DN1, 0, 2, (0,))
+    g_compute(3, 2)
+    fin_ffn(0)
+    rs(DN1, 0, 2, (1,))
+    g_compute(3, 3)
+    g_firstb(3)
+    g_compute(4, 0)
     g_second(3)
+    rs(DN1, 1, 2, (0,))
     g_first(4)
-    rs(FFN, 1, 3)
-    finish_out(1)
+    rs(DN1, 1, 2, (1,))
+    g_compute(4, 1)
+    g_compute(4, 2)
+    g_firstb(4)
+    g_compute(4, 3)
+    rs(FFN, 1, 2, (1,))
+    g_second(4)
+    rs(FFN, 1, 2, (0,))
+    fin_dn1(0)
+    fin_dn1(1)
+    e1s()
     g_finish(3)
-    rs(DN1, 1, 3)
-    gain1 = gain1 + norm1_back(1)
-    for j in range(4):
-        gsum[j : j + 1, :] = gain1[:, j * pair : (j + 1) * pair]
-        gsum[4 + j : 5 + j, :] = gain2[:, j * pair : (j + 1) * pair]
-
-    def e_copy(i, src):
-        dev = {"tensor": (z + i + 1) % 4} if i < 3 else {"dp": (d + i - 2) % 8}
-        return rcopy(src, gex.at[i], esend.at[i], erecv.at[i], dev)
-
-    for i in range(3):
-        e_copy(i, gsum).start()
-    g_second(4)
-    for i in range(3):
-        e_copy(i, gsum).wait()
-    gex[10] = gsum[...] + gex[0] + gex[1] + gex[2]
-    for i in range(3, 10):
-        e_copy(i, gex.at[10]).start()
+    e1w()
     g_finish(4)
-    for i in range(3, 10):
-        e_copy(i, gex.at[10]).wait()
-    total = gex[10]
-    for i in range(3, 10):
-        total = total + gex[i]
-    gsum[...] = total
+    fin_ffn(1)
+    e2w()
     last = pltpu.make_async_copy(gsum, ggain_h, osem.at[9])
     last.start()
     for u in range(5):
         w_sent(u)
-    for u in (N2, GH):
+    for u in (COT, N2, GH):
         for s in (0, 1):
             zag_sent(u, s)
     for s in (0, 1):
@@ -1018,6 +1117,7 @@
         vm((2, shard, ff), F32),
         vm((rows, width), F32),
         vm((16, width), F32),
+        vm((8, width), F32),
         vm((8, width // 4), F32),
         vm((11, 8, width // 4), F32),
         vm((micro, rows, width), BF),

time: 287 us -> 242 us (0.84)
  Pallas kernels: 260 us -> 216 us
    pallas_call x1, Pallas kernels: 260 us -> 216 us  [fused(): pl.pallas_call(functools.partial(block_kernel, dims), out_shape=shapes, i...]
where the time goes in v4:
time: 242 us
  Pallas kernels  216 us (89%)
  local copies, waits for them, and re-layouts  17.2 us (7%)
  other arithmetic  7.19 us (3%)
    pallas_call x1, Pallas kernels, fused(): pl.pallas_call(functools.partial(block_kernel, dims), out_shape=shapes, i...  216 us
    unnamed x39, local copies, waits for them, and re-layouts  9.88 us

profile of v4, /device:TPU:0, one launch (start us, length us, event | category | flops | bytes accessed | tf_op | source)
XLA Modules:
  0.0 241.6 jit_solution(11289710321410123452)
XLA Ops:
  0.7 0.7 stack.17
  1.3 0.7 stack.18
  2.0 0.7 pad_select_fusion.refs_2_
  2.7 0.8 reduce_window_sum.11
  3.5 0.7 sub.6
  4.3 0.8 fusion.1
  5.2 0.8 subtract_convert_fusion
  6.0 1.2 multiply_sine_fusion
  7.3 1.1 pad_maximum_fusion.2
  8.4 0.9 copy.60.refs_8_
  9.3 0.6 broadcast_in_dim.14.refs_7_
  9.9 0.1 copy.53
  10.5 0.9 copy.58.refs_3_
  11.5 0.9 pad_maximum_fusion.refs_5_
  12.4 0.1 copy.56
  12.6 0.8 copy.59.refs_4_
  13.4 216.3 %block.1 = (bf16[2,80,1536]{2,1,0:T(8,128)(2,1)}, f32[2,80,1536]{2,1,0:T(8,128)}, f32[192,1024]{1,0:T(8,128)}, f32[192,1024]{1,0:T(8,128)}, f32[192,1024]{1,0:T(...) custom-call(bf16[2,80,1536]{2,1,0:T(8,128)(2,1)} %refs_0_.1, bf16[2,80,1536]{2,1,0:T(8,128)(2,1)} %refs_1_.1, ...), custom_call_target="tpu_custom_call" | custom-call | tf_op jit(solution)/shard_map/block/pallas_call | solution.py:1152
  229.8 1.5 copy.61
  231.4 0.9 copy.63
  232.3 0.8 copy.64
  233.1 0.8 copy.65
  233.9 0.2 copy.62
  234.1 0.9 copy.66
  235.0 0.6 fusion.4
  235.6 0.8 copy.72
  236.4 0.9 copy.73
  237.4 0.5 copy-done.3
  237.9 0.9 copy.74
  238.8 0.5 copy-done.2
  239.3 0.9 copy.75
  240.2 0.5 copy-done.1
  240.7 0.9 copy.76
  (42 shorter events, 1.0 us)
Async XLA Ops:
  7.3 2.6 %copy-start.8 = (bf16[192,384]{1,0:T(8,128)(2,1)S(1)}, bf16[192,384]{1,0:T(8,128)(2,1)}, u32[]{:S(2)}) copy-start(bf16[192,384]{1,0:T(8,128)(2,1)} %param.18) | copy-start | bytes 442372
  7.3 2.7 %copy-start.10 = (bf16[192,192]{1,0:T(8,128)(2,1)S(1)}, bf16[192,192]{1,0:T(8,128)(2,1)}, u32[]{:S(2)}) copy-start(bf16[192,192]{1,0:T(8,128)(2,1)} %param.19) | copy-start | bytes 221188
  7.3 2.8 %copy-start.11 = (bf16[192,192]{1,0:T(8,128)(2,1)S(1)}, bf16[192,192]{1,0:T(8,128)(2,1)}, u32[]{:S(2)}) copy-start(bf16[192,192]{1,0:T(8,128)(2,1)} %param.20) | copy-start | bytes 221188
  10.4 1.1 copy-start.6
  10.4 1.1 copy-start.7
  10.5 2.0 copy-start.9
  231.4 2.5 %copy-start.5 = (f32[192,512]{1,0:T(8,128)S(1)}, f32[192,512]{1,0:T(8,128)}, u32[]{:S(2)}) copy-start(f32[192,512]{1,0:T(8,128)} %get-tuple-element.23) | copy-start | bytes 1179652
  233.9 1.1 copy-start.12
  233.9 1.8 copy-start.4
  234.1 2.3 copy-start
  236.4 1.5 copy-start.3
  237.9 1.4 copy-start.2
  239.3 1.4 copy-start.1

commit v5 on v4

--- a/solution.py
+++ b/solution.py
@@ -1,4 +1,5 @@
 import functools
+import math
 
 import jax
 import jax.numpy as jnp
@@ -247,15 +248,16 @@
 
 def block_kernel(dims, *refs):
     (rows, seq, width, shard, qp, kp, ff, groups) = dims
-    (tok, cot, wg_h, wi_h, wo_h, wu_h, wd_h, ordr, cols, cosr, sinr) = refs[:11]
-    (out_h, gtok_h, gdown_h, ggate_h, gup_h, gout_h, gin_h, ggain_h) = refs[11:19]
+    (tok, cot, wg_h, wq_h, wk_h, wv_h, wo_h, wa_h, wb_h, wd_h, ordr, lens) = refs[:12]
+    (out_h, gtok_h, gdown_h, ggate_h, gup_h, gout_h, gin_h, ggain_h) = refs[12:20]
     (wgn, wi, wo, wu, wd, xf, n1, n2, gf, qkv, ob, dob, act, dq3, dgu, pr, hb, dh, pa, pb, ra, rb,
      gb, xb, hop, fin, stage, acc, gains, gpart, gsum, gex, ybuf, tbuf,
-     wsend, wrecv, zsend, zrecv, rsend, rrecv, gsend, grecv, esend, erecv, lsem, osem, credit) = refs[19:]
+     wsend, wrecv, zsend, zrecv, rsend, rrecv, gsend, grecv, esend, erecv, lsem, osem, credit, psem, rq, rk, rv, ro, cols, cosr, sinr) = refs[20:]
     ghf = xf
     heads = qp // LANES
     per_group = heads // groups
     inw = qp + 2 * kp
+    pair = 2 * shard
     d = lax.axis_index("dp")
     z = lax.axis_index("tensor")
     c = d % 2
@@ -283,17 +285,85 @@
         pl.semaphore_signal(
             barrier, inc=1, device_id={"tensor": (z + step) % 4}, device_id_type=MESH
         )
-    pl.semaphore_wait(barrier, 10)
-
-    wunits = ((wg_h, wgn, 16), (wi_h, wi, shard), (wo_h, wo, shard), (wu_h, wu, shard), (wd_h, wd, shard))
+
+    def raw_copy(i):
+        src, dst = (
+            (wq_h, rq),
+            (wk_h, rk),
+            (wv_h, rv),
+            (wo_h, ro),
+            (wd_h, wd.at[pl.ds(al(shard * d, 16), shard), :]),
+            (wa_h, wu.at[pl.ds(al(shard * d, 16), shard), pl.ds(0, ff)]),
+            (wb_h, wu.at[pl.ds(al(shard * d, 16), shard), pl.ds(ff, ff)]),
+        )[i]
+        return pltpu.make_async_copy(src, dst, psem.at[i])
+
+    def head_map(n):
+        row = lax.broadcasted_iota(jnp.int32, (n // HEAD * HEAD, n // HEAD * LANES), 0)
+        col = lax.broadcasted_iota(jnp.int32, (n // HEAD * HEAD, n // HEAD * LANES), 1)
+        lane = col % 64
+        want = (col // 64) * (HEAD // 2) + lane
+        return jnp.where((lane < HEAD // 2) & (row == want), 1.0, 0.0).astype(BF)
+
+    def prep_in():
+        at = pl.ds(al(shard * d, 16), shard)
+        for i in range(3):
+            raw_copy(i).wait()
+        wide = head_map(rq.shape[1])
+        narrow = head_map(rk.shape[1])
+        wi[at, pl.ds(0, qp)] = nn(rq[...], wide).astype(BF)
+        wi[at, pl.ds(qp, kp)] = nn(rk[...], narrow).astype(BF)
+        wi[at, pl.ds(qp + kp, kp)] = nn(rv[...], narrow).astype(BF)
+
+    def prep_out():
+        raw_copy(3).wait()
+        wo[pl.ds(al(shard * d, 16), shard), :] = nn(ro[...], head_map(ro.shape[1])).astype(BF)
+
+    def prep_rows(s):
+        row = lax.broadcasted_iota(jnp.int32, (seq, seq), 0)
+        col = lax.broadcasted_iota(jnp.int32, (seq, seq), 1)
+        same = jnp.where(row == col, 1.0, 0.0).astype(BF)
+        mid = seq // 2
+        packed = (ordr[s : s + 1, :] - mid).astype(F32)
+        place = nt(same, jnp.broadcast_to(packed, (LANES, seq)).astype(BF)) + mid
+        start = lens[s, 0]
+        first = jnp.zeros((seq, LANES), F32)
+        for n in range(1, lens.shape[1]):
+            begin = start.astype(F32)
+            first = jnp.where(place >= begin, begin, first)
+            real = jnp.where(place >= begin, 0.0, 1.0)
+            start = start + lens[s, n]
+        lane = lax.broadcasted_iota(jnp.int32, (seq, LANES), 1)
+        cols[s] = jnp.where(lane == 0, place, jnp.where(lane == 1, first, real))
+        one = lax.broadcasted_iota(jnp.int32, (8, LANES), 1)
+        field = one % 64
+        freqs = jnp.exp((-2.0 * math.log(rope_base) / HEAD) * field.astype(F32))
+        freqs = jnp.where(field < HEAD // 2, freqs, 0.0)[0:1, :]
+        angles = (place - first) * freqs
+        cosr[s] = jnp.cos(angles)
+        sine = jnp.sin(angles)
+        sinr[s] = jnp.where(lane < 64, -sine, sine)
+
+    wunits = (
+        (wgn, 16, 0, pair),
+        (wi, shard, 0, inw),
+        (wo, shard, 0, qp),
+        (wu, shard, 0, ff),
+        (wu, shard, ff, ff),
+        (wd, shard, 0, ff),
+    )
 
     def wblk(u, i):
-        n = wunits[u][2]
-        return wunits[u][1].at[pl.ds(al(n * i, 16), n)]
+        ref, n, at, cut = wunits[u]
+        return ref.at[pl.ds(al(n * i, 16), n), pl.ds(at, cut)]
 
     def w_start(u):
-        src = wunits[u][0]
-        pltpu.make_async_copy(src, wblk(u, d), lsem.at[u]).start()
+        src = wblk(u, d)
+        if u == 0:
+            src = wg_h
+            pltpu.make_async_copy(src, wblk(u, d), lsem.at[u]).start()
+        if u >= 3:
+            raw_copy((5, 6, 4)[u - 3]).wait()
         rcopy(src, wblk(u, d), wsend.at[u, 0], wrecv.at[u, 0], {"dp": aa}).start()
         rcopy(src, wblk(u, d), wsend.at[u, 1], wrecv.at[u, 1], {"dp": bb}).start()
         rcopy(src, wblk(u, d), wsend.at[u, 2], wrecv.at[u, 3], {"dp": pp}).start()
@@ -319,7 +389,8 @@
         w_wait(u, 4, bb + flip)
         w_wait(u, 5, aa + flip)
         w_wait(u, 6, dd + flip)
-        pltpu.make_async_copy(wunits[u][0], wblk(u, d), lsem.at[u]).wait()
+        if u == 0:
+            pltpu.make_async_copy(wg_h, wblk(u, d), lsem.at[u]).wait()
 
     def w_sent(u):
         for slot in range(7):
@@ -445,8 +516,6 @@
         (ghf, ob, 0, qp, gout_h),
         (n1, dq3, 0, inw, gin_h),
     )
-    pair = 2 * shard
-
     def xslot(u, chip):
         b, n = u % 2, gunits[u][3]
         return xb.at[b, pl.ds(al(chip * shard, 16), shard), pl.ds(0, n)]
@@ -602,9 +671,9 @@
                     part = part * head_scale
                 qkv[at, pl.ds(col, LANES)] = part.astype(BF)
 
-    def attend(s):
+    def attend(s, part):
         at = pl.ds(s * seq, seq)
-        oc = ordr[s]
+        oc = ordr[s : s + 1, :].astype(F32)
         mask = (oc <= cols[s, :, 0:1]) & (oc >= cols[s, :, 1:2])
 
         def body(h, carry):
@@ -619,14 +688,29 @@
             ob[at, pl.ds(al(h * LANES, LANES), LANES)] = nn(p.astype(BF), v).astype(BF)
             return carry
 
-        lax.fori_loop(0, heads, body, 0)
-
-    def spread(s, dst, left, weight, tile):
+        half = heads // 2
+        lax.fori_loop(part * half, (part + 1) * half, body, 0)
+
+    def spread(s, dst, left, weight, tile, part=0, parts=1):
         at = pl.ds(s * seq, seq)
 
         def body(j, carry):
             col = al(j * tile, tile)
             dst[at, pl.ds(col, tile)] = nt(left[at, :], weight[pl.ds(col, tile), :]).astype(BF)
+            return carry
+
+        count = width // tile // parts
+        lax.fori_loop(part * count, (part + 1) * count, body, 0)
+
+    def spread_gain(s):
+        at = pl.ds(s * seq, seq)
+        tile = 512
+
+        def body(j, carry):
+            col = pl.ds(al(j * tile, tile), tile)
+            got = nt(dq3[at, :], wi[col, :])
+            pa[at, col] = got.astype(BF)
+            gpart[0:1, col] += jnp.sum(got * n1[at, col].astype(F32), axis=0, keepdims=True)
             return carry
 
         lax.fori_loop(0, width // tile, body, 0)
@@ -645,10 +729,11 @@
 
         lax.fori_loop(0, rows // 16, body, 0)
 
-    def feed(s):
+    def feed(s, part):
         at = pl.ds(s * seq, seq)
         real = cols[s, :, 2:3]
-        own_here(1, s)
+        if part == 0:
+            own_here(1, s)
 
         def body(t, carry):
             col = al(t * 256, 256)
@@ -662,7 +747,8 @@
             dgu[at, pl.ds(al(ff + t * 256, 256), 256)] = (back * swish).astype(BF)
             return carry
 
-        lax.fori_loop(0, ff // 256, body, 0)
+        count = ff // 256 // 4
+        lax.fori_loop(part * count, (part + 1) * count, body, 0)
 
     def finish_out(s):
         def body(i, carry):
@@ -741,9 +827,9 @@
             grad = acc[r, :]
             inner = grad * gain
             dh[ro, :] = dh[ro, :] + scale * (inner - unit * jnp.mean(inner * unit, axis=-1, keepdims=True))
-            return carry + jnp.sum(grad * unit, axis=0, keepdims=True)
-
-        gpart[0:1, :] += lax.fori_loop(0, rows // 16, body, jnp.zeros((1, width), F32))
+            return carry
+
+        lax.fori_loop(0, rows // 16, body, 0)
         pltpu.make_async_copy(
             dh.at[pl.ds(s * rows, rows)], gtok_h.at[s], osem.at[7 + s]
         ).start()
@@ -779,7 +865,8 @@
 
     def e1s():
         for j in range(4):
-            gsum[j : j + 1, :] = gpart[0:1, j * pair : (j + 1) * pair]
+            at = pl.ds(j * pair, pair)
+            gsum[j : j + 1, :] = gpart[0:1, at] / gains[0:1, at]
             gsum[4 + j : 5 + j, :] = gpart[1:2, j * pair : (j + 1) * pair]
         for i in range(3):
             e_copy(i).start()
@@ -799,221 +886,243 @@
             total = total + gex[i]
         gsum[...] = total
 
+    for i in range(7):
+        raw_copy(i).start()
     gpart[...] = jnp.zeros_like(gpart)
     for s in (0, 1):
         tok_copy(s).start()
+    pl.semaphore_wait(barrier, 10)
     ag(X, 0, 0)
+    ag(X, 1, 0)
+    prep_out()
+    prep_in()
     w_start(0)
     w_start(1)
-    ag(X, 1, 0)
     w_start(2)
-    w_relayb(1)
     ag(X, 0, 1, 1)
+    w_relayb(0)
+    prep_rows(0)
     ag(X, 0, 1, 0)
-    ag(X, 1, 1, 0)
-    ag(X, 1, 1, 1)
-    w_relaya(0)
-    w_diag(1)
-    w_relayb(0)
-    ag(X, 0, 2, 0)
-    w_diag(0)
+    ag(COT, 0, 0)
     w_relaya(1)
     w_relayb(2)
-    w_start(3)
+    ag(X, 0, 2, 0)
+    prep_rows(1)
+    ag(X, 1, 1, 0)
+    w_relaya(2)
+    w_relayb(1)
+    w_diag(0)
+    w_diag(2)
+    w_relaya(0)
     ag(X, 0, 2, 1)
     w_done(0)
     gain_rows()
-    ag(COT, 0, 0)
+    ag(X, 1, 1, 1)
+    norm1(0, 0)
+    w_start(3)
+    ag(COT, 0, 1, 0)
+    norm1(1, 0)
+    norm1(0, 2)
     norm1(0, 1)
-    ag(X, 1, 2, 0)
-    norm1(0, 0)
     ag(COT, 1, 0)
-    w_relaya(2)
-    norm1(1, 0)
-    ag(X, 1, 2, 1)
+    w_diag(1)
+    ag(X, 0, 3, 0)
+    ag(X, 0, 3, 1)
     w_done(1)
-    ag(X, 0, 3, 0)
-    w_diag(2)
-    ag(X, 0, 3, 1)
-    norm1(0, 2)
     norm1(0, 3)
     project(0)
+    attend(0, 0)
+    attend(0, 1)
+    w_start(4)
+    ag(COT, 0, 1, 1)
+    w_start(5)
+    ag(X, 1, 2, 1)
     w_done(2)
-    attend(0)
     spread(0, pa, ob, wo, 512)
+    rs(BR, 0, 0, (0,))
+    rs(BR, 0, 1, (0,))
+    ag(X, 1, 2, 0)
     rs(BR, 0, 0, (1,))
-    ag(COT, 0, 1, 1)
-    rs(BR, 0, 0, (0,))
-    ag(COT, 0, 1, 0)
-    rs(BR, 0, 1, (0,))
-    norm1(1, 1)
-    w_relaya(3)
     rs(BR, 0, 1, (1,))
-    w_relayb(3)
+    rs(BR, 0, 2, (1,))
+    norm1(1, 2)
     rs(BR, 0, 2, (0,))
+    ag(COT, 0, 2, 0)
+    ag(COT, 0, 2, 1)
     ag(X, 1, 3, 0)
     ag(X, 1, 3, 1)
     norm1(1, 3)
-    rs(BR, 0, 2, (1,))
-    norm1(1, 2)
+    w_relayb(3)
+    norm1(1, 1)
+    w_relayb(4)
+    fin_br(0)
     project(1)
-    ag(COT, 0, 2, 0)
-    ag(COT, 0, 2, 1)
-    w_start(4)
-    attend(1)
-    fin_br(0)
+    w_relayb(5)
+    w_relaya(4)
     rs_sent(BR, 0)
+    attend(1, 0)
+    attend(1, 1)
+    w_relaya(3)
     spread(1, pa, ob, wo, 512)
+    rs(BR, 1, 0, (1,))
     rs(BR, 1, 0, (0,))
-    w_relayb(4)
-    rs(BR, 1, 0, (1,))
+    w_diag(3)
+    zag_sent(X, 0)
+    ag(COT, 0, 3, 0)
+    w_relaya(5)
     ag(N2, 0, 1, 1)
+    w_done(3)
     ag(N2, 0, 1, 0)
-    w_diag(3)
+    w_diag(5)
     rs(BR, 1, 1, (1,))
-    w_relaya(4)
     rs(BR, 1, 1, (0,))
-    zag_sent(X, 0)
+    ag(N2, 0, 2, 1)
+    ag(N2, 0, 2, 0)
+    w_diag(4)
+    w_done(4)
     ag(COT, 0, 3, 1)
-    ag(N2, 0, 2, 1)
-    w_diag(4)
-    ag(N2, 0, 2, 0)
-    w_done(4)
     rs(BR, 1, 2, (1,))
+    ag(N2, 0, 3, 1)
+    w_done(5)
+    rs(BR, 1, 2, (0,))
     ag(N2, 0, 3, 0)
-    rs(BR, 1, 2, (0,))
     ag(COT, 1, 1, 0)
-    ag(N2, 0, 3, 1)
+    feed(0, 0)
+    feed(0, 1)
+    feed(0, 2)
     ag(COT, 1, 1, 1)
-    ag(COT, 0, 3, 0)
-    w_done(3)
-    feed(0)
     fin_br(1)
-    spread(0, pa, dgu, wu, 256)
+    feed(0, 3)
+    spread(0, pa, dgu, wu, 256, 0, 2)
+    spread(0, pa, dgu, wu, 256, 1, 2)
+    rs(DN2, 0, 0, (1,))
+    ag(COT, 1, 2, 0)
     rs(DN2, 0, 0, (0,))
-    ag(COT, 1, 2, 0)
+    spread(0, pb, act, wd, 512)
+    rs_sent(BR, 1)
     ag(N2, 1, 1, 1)
-    rs(DN2, 0, 0, (1,))
     ag(N2, 1, 1, 0)
-    rs_sent(BR, 1)
+    rs(DN2, 0, 1, (0,))
+    ag(N2, 1, 2, 1)
     rs(DN2, 0, 1, (1,))
-    ag(COT, 1, 2, 1)
-    rs(DN2, 0, 1, (0,))
-    spread(0, pb, act, wd, 512)
     rs(FFN, 0, 0, (1,))
     rs(FFN, 0, 0, (0,))
-    ag(N2, 1, 2, 1)
+    ag(COT, 1, 2, 1)
+    rs(DN2, 0, 2, (1,))
+    zag_sent(X, 1)
     ag(N2, 1, 2, 0)
-    zag_sent(X, 1)
     rs(DN2, 0, 2, (0,))
     ag(COT, 1, 3, 0)
-    rs(DN2, 0, 2, (1,))
+    rs(FFN, 0, 1, (1,))
     ag(COT, 1, 3, 1)
-    rs(FFN, 0, 1, (1,))
+    ag(N2, 1, 3, 1)
+    ag(N2, 1, 3, 0)
+    feed(1, 0)
     rs(FFN, 0, 1, (0,))
-    ag(N2, 1, 3, 0)
-    ag(N2, 1, 3, 1)
-    feed(1)
+    feed(1, 1)
+    feed(1, 2)
+    feed(1, 3)
     fin_dn2(0)
-    spread(1, pa, dgu, wu, 256)
+    spread(1, pa, dgu, wu, 256, 0, 2)
+    spread(1, pa, dgu, wu, 256, 1, 2)
+    rs(DN2, 1, 0, (1,))
     g_compute(0, 0)
-    ag(GH, 0, 1, 1)
-    rs(DN2, 1, 0, (1,))
-    ag(GH, 0, 1, 0)
     rs(DN2, 1, 0, (0,))
     g_compute(0, 1)
     g_compute(0, 2)
+    ag(GH, 0, 1, 0)
+    g_first(0)
+    ag(GH, 0, 1, 1)
     g_compute(0, 3)
+    rs(DN2, 1, 1, (0,))
     rs(DN2, 1, 1, (1,))
-    g_first(0)
-    rs(DN2, 1, 1, (0,))
+    g_firstb(0)
+    ag(GH, 0, 2, 1)
     ag(GH, 0, 2, 0)
     g_compute(1, 0)
-    ag(GH, 0, 2, 1)
+    rs(DN2, 1, 2, (0,))
     rs(DN2, 1, 2, (1,))
-    rs(DN2, 1, 2, (0,))
+    g_compute(1, 1)
     spread(1, pb, act, wd, 512)
-    g_firstb(0)
+    rs(FFN, 1, 0, (0,))
+    ag(GH, 0, 3, 0)
+    g_second(0)
     rs(FFN, 1, 0, (1,))
+    ag(GH, 0, 3, 1)
+    g_compute(1, 2)
+    g_first(1)
+    fin_dn2(1)
     rs_sent(DN2, 0)
-    g_second(0)
-    ag(GH, 0, 3, 0)
-    g_compute(1, 1)
-    g_compute(1, 2)
-    g_compute(1, 3)
-    rs(FFN, 1, 0, (0,))
-    g_first(1)
-    ag(GH, 0, 3, 1)
-    fin_dn2(1)
+    g_firstb(1)
     grad_heads(0)
     attend_back(0)
-    spread(0, pa, dq3, wi, 512)
-    rs(DN1, 0, 0, (0,))
+    spread_gain(0)
     g_finish(0)
     rs(DN1, 0, 0, (1,))
-    g_firstb(1)
-    g_compute(2, 0)
+    rs(DN1, 0, 0, (0,))
     ag(GH, 1, 1, 0)
     ag(GH, 1, 1, 1)
+    rs(FFN, 1, 1, (0,))
+    g_compute(1, 3)
+    g_second(1)
+    g_compute(2, 0)
     g_compute(2, 1)
+    rs(FFN, 1, 1, (1,))
+    ag(GH, 1, 2, 0)
+    rs(DN1, 0, 1, (1,))
+    ag(GH, 1, 2, 1)
+    g_first(2)
     rs(DN1, 0, 1, (0,))
-    rs(DN1, 0, 1, (1,))
-    g_first(2)
+    rs_sent(DN2, 1)
     g_compute(2, 2)
-    ag(GH, 1, 2, 0)
-    rs(FFN, 1, 1, (0,))
     g_compute(2, 3)
-    ag(GH, 1, 2, 1)
-    rs_sent(DN2, 1)
+    rs(FFN, 1, 2, (0,))
+    g_finish(1)
+    g_firstb(2)
     rs(FFN, 0, 2, (1,))
-    rs(FFN, 1, 1, (1,))
-    g_firstb(2)
+    ag(GH, 1, 3, 0)
     g_second(2)
-    rs(FFN, 0, 2, (0,))
-    ag(GH, 1, 3, 0)
-    g_second(1)
     ag(GH, 1, 3, 1)
+    g_compute(3, 0)
     grad_heads(1)
     attend_back(1)
-    spread(1, pa, dq3, wi, 512)
+    spread_gain(1)
+    rs(DN1, 1, 0, (0,))
+    g_compute(3, 1)
+    g_first(3)
     rs(DN1, 1, 0, (1,))
-    rs(DN1, 1, 0, (0,))
-    g_finish(1)
-    g_compute(3, 0)
-    g_compute(3, 1)
-    rs(DN1, 1, 1, (0,))
-    g_first(3)
-    rs(DN1, 1, 1, (1,))
+    g_compute(3, 2)
+    g_compute(3, 3)
+    rs(FFN, 1, 2, (1,))
+    e1s()
+    g_firstb(3)
+    rs(FFN, 0, 2, (0,))
     g_finish(2)
-    rs(DN1, 0, 2, (0,))
-    g_compute(3, 2)
-    fin_ffn(0)
-    rs(DN1, 0, 2, (1,))
-    g_compute(3, 3)
-    g_firstb(3)
     g_compute(4, 0)
     g_second(3)
+    rs(DN1, 1, 1, (1,))
+    g_compute(4, 1)
+    rs(DN1, 1, 1, (0,))
+    rs(DN1, 0, 2, (0,))
+    rs(DN1, 0, 2, (1,))
+    g_first(4)
+    g_compute(4, 2)
+    g_compute(4, 3)
+    fin_ffn(1)
+    g_firstb(4)
+    g_second(4)
+    fin_ffn(0)
+    rs(DN1, 1, 2, (1,))
     rs(DN1, 1, 2, (0,))
-    g_first(4)
-    rs(DN1, 1, 2, (1,))
-    g_compute(4, 1)
-    g_compute(4, 2)
-    g_firstb(4)
-    g_compute(4, 3)
-    rs(FFN, 1, 2, (1,))
-    g_second(4)
-    rs(FFN, 1, 2, (0,))
+    g_finish(3)
     fin_dn1(0)
-    fin_dn1(1)
-    e1s()
-    g_finish(3)
     e1w()
     g_finish(4)
-    fin_ffn(1)
     e2w()
+    fin_dn1(1)
     last = pltpu.make_async_copy(gsum, ggain_h, osem.at[9])
     last.start()
-    for u in range(5):
+    for u in range(6):
         w_sent(u)
     for u in (COT, N2, GH):
         for s in (0, 1):
@@ -1029,15 +1138,60 @@
     last.wait()
 
 
-def pad_heads(weight):
-    depth = weight.shape[0]
-    halves = weight.reshape(depth, -1, 2, HEAD // 2)
-    return jnp.pad(halves, ((0, 0), (0, 0), (0, 0), (0, 64 - HEAD // 2))).reshape(depth, -1)
-
-
-def cut_heads(grad):
-    depth = grad.shape[0]
-    return grad.reshape(depth, -1, 2, 64)[..., : HEAD // 2].reshape(depth, -1)
+def finish_kernel(dims, *refs):
+    (qp, kp, shard) = dims
+    ins, outs, bufs, (sem_in, sem_out) = refs[:8], refs[8:19], refs[19:33], refs[33:]
+    given, made = bufs[:8], bufs[8:]
+    d = lax.axis_index("dp")
+
+    def load(i):
+        return pltpu.make_async_copy(ins[i], given[i], sem_in.at[i])
+
+    def save(i, src):
+        return pltpu.make_async_copy(src, outs[i], sem_out.at[i])
+
+    def head_map(n):
+        row = lax.broadcasted_iota(jnp.int32, (n, n // HEAD * LANES), 0)
+        col = lax.broadcasted_iota(jnp.int32, (n, n // HEAD * LANES), 1)
+        lane = col % 64
+        want = (col // 64) * (HEAD // 2) + lane
+        return jnp.where((lane < HEAD // 2) & (row == want), 1.0, 0.0).astype(BF)
+
+    def picked(value, which):
+        high = value.astype(BF)
+        rest = value - high.astype(F32)
+        mid = rest.astype(BF)
+        low = (rest - mid.astype(F32)).astype(BF)
+        return nt(high, which) + (nt(mid, which) + nt(low, which))
+
+    order = (1, 2, 0, 3, 4, 5, 6, 7)
+    for i in order:
+        load(i).start()
+    ggain, gin, gout = given[:3]
+    tone, ttwo, tq, tk, tv, tout = made
+    wide, narrow = head_map(tq.shape[1]), head_map(tk.shape[1])
+    load(1).wait()
+    tq[...] = picked(gin[:, :qp], wide)
+    save(2, tq).start()
+    tk[...] = picked(gin[:, qp : qp + kp], narrow)
+    save(3, tk).start()
+    tv[...] = picked(gin[:, qp + kp :], narrow)
+    save(4, tv).start()
+    load(2).wait()
+    tout[...] = picked(gout[...], wide)
+    save(5, tout).start()
+    load(0).wait()
+    for i, ref in enumerate((tone, ttwo)):
+        line = ggain[pl.ds(4 * i + d // 2, 1), :]
+        ref[...] = jnp.where(d % 2 == 0, line[:, :shard], line[:, shard:])
+        save(i, ref).start()
+    for i in range(3, 8):
+        load(i).wait()
+        save(i + 3, given[i]).start()
+    for i, ref in enumerate(made):
+        save(i, ref).wait()
+    for i in range(3, 8):
+        save(i + 3, given[i]).wait()
 
 
 def fused(
@@ -1060,29 +1214,17 @@
     shard = w_query.shape[0]
     ff = w_gate.shape[1]
     groups = w_key.shape[1] // HEAD
-    w_in = pad_heads(jnp.concatenate([w_query, w_key, w_value], axis=1))
-    qp = w_query.shape[1] // HEAD * LANES
+    q_cols, k_cols = w_query.shape[1], w_key.shape[1]
+    qp = q_cols // HEAD * LANES
     kp = groups * LANES
     inw = qp + 2 * kp
-    w_back = pad_heads(w_out.T)
-    gate_up = jnp.concatenate([w_gate, w_up], axis=1)
-    gain = jnp.stack([gain_attn, gain_ffn], axis=0)
-    low = jnp.pad(gain, ((0, 14), (0, shard)))
-    high = jnp.pad(gain, ((0, 14), (shard, 0)))
-    gain = jnp.where(lax.axis_index("dp") % 2 == 0, low, high)
-
-    starts = jnp.cumsum(lengths, axis=1, dtype=jnp.int32) - lengths
-    docs = jnp.sum((order[:, :, None] >= starts[:, None, 1:]).astype(jnp.int32), axis=2)
-    onehot = docs[:, :, None] == jnp.arange(lengths.shape[1], dtype=jnp.int32)
-    first = jnp.sum(jnp.where(onehot, starts[:, None, :], 0), axis=2)
-    real = (docs < lengths.shape[1] - 1).astype(F32)
-    cols = jnp.stack([order.astype(F32), first.astype(F32), real], axis=2)
-    freqs = rope_base ** (-2.0 * jnp.arange(HEAD // 2, dtype=F32) / HEAD)
-    angles = (order - first).astype(F32)[:, :, None] * freqs
-    gap = ((0, 0), (0, 0), (0, 64 - HEAD // 2))
-    cosine, sine = jnp.pad(jnp.cos(angles), gap), jnp.pad(jnp.sin(angles), gap)
-    cosine = jnp.concatenate([cosine, cosine], axis=2)
-    sine = jnp.concatenate([-sine, sine], axis=2)
+    even = lax.axis_index("dp") % 2 == 0
+
+    def placed(gain):
+        return jnp.where(even, jnp.pad(gain, (0, shard)), jnp.pad(gain, (shard, 0)))[None, :]
+
+    line = lax.broadcasted_iota(jnp.int32, (16, 2 * shard), 0)
+    gain = jnp.where(line == 0, placed(gain_attn), placed(gain_ffn))
 
     total = micro * seq
     vm = pltpu.VMEM
@@ -1122,8 +1264,8 @@
         vm((11, 8, width // 4), F32),
         vm((micro, rows, width), BF),
         vm((micro, rows, width), BF),
-        dma((5, 7)),
-        dma((5, 7)),
+        dma((6, 7)),
+        dma((6, 7)),
         dma((4, 2, 2, 3)),
         dma((4, 2, 2, 3)),
         dma((4, 2, 2, 3)),
@@ -1135,24 +1277,34 @@
         dma((12,)),
         dma((10,)),
         pltpu.SemaphoreType.REGULAR((3,)),
+        dma((7,)),
+        vm(w_query.shape, BF),
+        vm(w_key.shape, BF),
+        vm(w_value.shape, BF),
+        vm(w_out.shape[::-1], BF),
+        vm((micro, seq, LANES), F32),
+        vm((micro, seq, LANES), F32),
+        vm((micro, seq, LANES), F32),
     ]
     hbm = pl.BlockSpec(memory_space=pl.ANY)
     vmem = pl.BlockSpec(memory_space=pltpu.VMEM)
+    smem = pl.BlockSpec(memory_space=pltpu.SMEM)
+    shape = jax.ShapeDtypeStruct
     shapes = [
-        jax.ShapeDtypeStruct((micro, rows, width), BF),
-        jax.ShapeDtypeStruct((micro, rows, width), F32),
-        jax.ShapeDtypeStruct((shard, ff), F32),
-        jax.ShapeDtypeStruct((shard, ff), F32),
-        jax.ShapeDtypeStruct((shard, ff), F32),
-        jax.ShapeDtypeStruct((shard, qp), F32),
-        jax.ShapeDtypeStruct((shard, inw), F32),
-        jax.ShapeDtypeStruct((8, width // 4), F32),
+        shape((micro, rows, width), BF),
+        shape((micro, rows, width), F32),
+        shape((shard, ff), F32),
+        shape((shard, ff), F32),
+        shape((shard, ff), F32),
+        shape((shard, qp), F32),
+        shape((shard, inw), F32),
+        shape((8, width // 4), F32),
     ]
     dims = (rows, seq, width, shard, qp, kp, ff, groups)
     out, gtok, gdown, ggate, gup, gout, gin, ggain = pl.pallas_call(
         functools.partial(block_kernel, dims),
         out_shape=shapes,
-        in_specs=[hbm] * 7 + [vmem] * 4,
+        in_specs=[hbm] * 10 + [vmem, smem],
         out_specs=[hbm] * 8,
         scratch_shapes=scratch,
         compiler_params=pltpu.CompilerParams(
@@ -1163,32 +1315,34 @@
         tokens,
         cotangent,
         gain,
-        w_in,
-        w_back,
-        gate_up,
+        w_query,
+        w_key,
+        w_value,
+        w_out.T,
+        w_gate,
+        w_up,
         w_down.T,
-        order.astype(F32)[:, None, :],
-        cols,
-        cosine,
-        sine,
-    )
-    gains = ggain.reshape(2, width)
-    gain_own = lax.dynamic_slice_in_dim(gains, lax.axis_index("dp") * shard, shard, 1)
-    grads_in = cut_heads(gin)
-    q_cols, k_cols = w_query.shape[1], w_key.shape[1]
-    return (
-        out,
-        gtok,
-        gain_own[0],
-        grads_in[:, :q_cols],
-        grads_in[:, q_cols : q_cols + k_cols],
-        grads_in[:, q_cols + k_cols :],
-        cut_heads(gout).T,
-        gain_own[1],
-        ggate,
-        gup,
-        gdown.T,
-    )
+        order,
+        lengths,
+    )
+    made = [
+        shape((1, shard), F32),
+        shape((1, shard), F32),
+        shape((shard, q_cols), F32),
+        shape((shard, k_cols), F32),
+        shape((shard, k_cols), F32),
+        shape((shard, q_cols), F32),
+    ]
+    given = [ggain, gin, gout, out, gtok, ggate, gup, gdown]
+    one, two, gq, gk, gv, gout, out, gtok, ggate, gup, gdown = pl.pallas_call(
+        functools.partial(finish_kernel, (qp, kp, shard)),
+        out_shape=made + [shape(x.shape, x.dtype) for x in given[3:]],
+        in_specs=[hbm] * 8,
+        out_specs=[hbm] * 11,
+        scratch_shapes=[vm(x.shape, x.dtype) for x in given + made] + [dma((8,)), dma((11,))],
+        name="finish",
+    )(*given)
+    return out, gtok, one[0], gq, gk, gv, gout.T, two[0], ggate, gup, gdown.T
 
 
 def local(tokens, *rest):

time: 242 us -> 216 us (0.89)
  local copies, waits for them, and re-layouts: 17.2 us -> 0.64 us
  other arithmetic: 7.19 us -> 0.76 us
  Pallas kernels: 216 us -> 212 us
    pallas_call x1, Pallas kernels: 216 us -> 207 us  [fused(): pl.pallas_call(functools.partial(block_kernel, dims), out_shape=shapes, i...]
    unnamed x39 -> x4, local copies, waits for them, and re-layouts: 9.88 us -> 0.64 us
    pallas_call x0 -> x1, Pallas kernels: none -> 4.66 us  [fused(): pl.pallas_call(functools.partial(finish_kernel, (qp, kp, shard)), out_sha...]
where the time goes in v5:
time: 216 us; the launch traced here: 214 us
  Pallas kernels  212 us (98%)
    pallas_call x1, Pallas kernels, fused(): pl.pallas_call(functools.partial(block_kernel, dims), out_shape=shapes, i...  207 us
    pallas_call x1, Pallas kernels, fused(): pl.pallas_call(functools.partial(finish_kernel, (qp, kp, shard)), out_sha...  4.66 us

profile of v5, /device:TPU:0, one launch (start us, length us, event | category | flops | bytes accessed | tf_op | source)
XLA Modules:
  0.0 213.9 jit_solution(14205308511869448032)
XLA Ops:
  0.7 0.0 copy-start
  0.7 0.0 copy-start.1
  0.7 0.6 copy-done
  1.3 0.0 copy-done.1
  1.3 0.1 pad_select_fusion
  1.4 0.7 broadcast_select_fusion.refs_2_
  2.1 206.9 %block.1 = (bf16[2,80,1536]{2,1,0:T(8,128)(2,1)}, f32[2,80,1536]{2,1,0:T(8,128)}, f32[192,1024]{1,0:T(8,128)}, f32[192,1024]{1,0:T(8,128)}, f32[192,1024]{1,0:T(...) custom-call(bf16[2,80,1536]{2,1,0:T(8,128)(2,1)} %refs_0_.1, bf16[2,80,1536]{2,1,0:T(8,128)(2,1)} %refs_1_.1, ...), custom_call_target="tpu_custom_call" | custom-call | tf_op jit(solution)/shard_map/block/pallas_call | solution.py:1304
  209.0 4.7 %finish.1 = (f32[1,192]{1,0:T(1,128)}, f32[1,192]{1,0:T(1,128)}, f32[192,384]{1,0:T(8,128)}, f32[192,192]{1,0:T(8,128)}, f32[192,192]{1,0:T(8,128)}, /*index=5*/...) custom-call(f32[8,384]{1,0:T(8,128)} %get-tuple-element.30.refs_0_, ...), custom_call_target="tpu_custom_call" | custom-call | tf_op jit(solution)/shard_map/finish/pallas_call | solution.py:1337
  (1 shorter events, 0.0 us)
Async XLA Ops:
  0.7 0.7 copy-start
  0.7 0.7 copy-start.1

commit v6 on v5

--- a/solution.py
+++ b/solution.py
@@ -248,11 +248,11 @@
 
 def block_kernel(dims, *refs):
     (rows, seq, width, shard, qp, kp, ff, groups) = dims
-    (tok, cot, wg_h, wq_h, wk_h, wv_h, wo_h, wa_h, wb_h, wd_h, ordr, lens) = refs[:12]
-    (out_h, gtok_h, gdown_h, ggate_h, gup_h, gout_h, gin_h, ggain_h) = refs[12:20]
-    (wgn, wi, wo, wu, wd, xf, n1, n2, gf, qkv, ob, dob, act, dq3, dgu, pr, hb, dh, pa, pb, ra, rb,
-     gb, xb, hop, fin, stage, acc, gains, gpart, gsum, gex, ybuf, tbuf,
-     wsend, wrecv, zsend, zrecv, rsend, rrecv, gsend, grecv, esend, erecv, lsem, osem, credit, psem, rq, rk, rv, ro, cols, cosr, sinr) = refs[20:]
+    (tok, cot, ga_h, gf_h, wq_h, wk_h, wv_h, wo_h, wa_h, wb_h, wd_h, ordr, lens) = refs[:13]
+    (out_v, gtok_v, gdown_v, ggate_v, gup_v, gout_v, gq_v, gk_v, gv_v, gone_v, gtwo_v) = refs[13:24]
+    (wgn, wi, wo, wu, wd, xf, n1, n2, gf, qkv, ob, act, dq3, dgu, pr, hb, pa, pb, ra, rb,
+     gb, xb, hop, fin, stage, acc, gains, gpart, gsum, gex, tbuf, rga, rgf, rq, rk, rv, ro, cols, cosr, sinr,
+     wsend, wrecv, zsend, zrecv, rsend, rrecv, gsend, grecv, esend, erecv, lsem, psem, credit) = refs[24:]
     ghf = xf
     heads = qp // LANES
     per_group = heads // groups
@@ -270,7 +270,8 @@
     pp = d + flip
     chip_own, chip_a, chip_b, chip_d = d // 2, aa // 2, bb // 2, dd // 2
     chip_x, chip_y = near_x // 2, near_y // 2
-    own = 1 * z * rows
+    own = z * rows
+    half = width
     zdev = {"tensor": z + 1}, {"tensor": z - 1}
 
     def rcopy(src, dst, ssem, rsem, dev):
@@ -279,12 +280,12 @@
         )
 
     barrier = pltpu.get_barrier_semaphore()
-    for step in range(1, 8):
-        pl.semaphore_signal(barrier, inc=1, device_id={"dp": (d + step) % 8}, device_id_type=MESH)
-    for step in (1, 2, 3):
-        pl.semaphore_signal(
-            barrier, inc=1, device_id={"tensor": (z + step) % 4}, device_id_type=MESH
-        )
+    for dev in (pp, aa, bb):
+        pl.semaphore_signal(barrier, inc=1, device_id={"dp": dev}, device_id_type=MESH)
+    for way in (0, 1):
+        @pl.when((z < 3) if way == 0 else (z > 0))
+        def _():
+            pl.semaphore_signal(barrier, inc=1, device_id=zdev[way], device_id_type=MESH)
 
     def raw_copy(i):
         src, dst = (
@@ -295,6 +296,8 @@
             (wd_h, wd.at[pl.ds(al(shard * d, 16), shard), :]),
             (wa_h, wu.at[pl.ds(al(shard * d, 16), shard), pl.ds(0, ff)]),
             (wb_h, wu.at[pl.ds(al(shard * d, 16), shard), pl.ds(ff, ff)]),
+            (ga_h, rga),
+            (gf_h, rgf),
         )[i]
         return pltpu.make_async_copy(src, dst, psem.at[i])
 
@@ -304,6 +307,20 @@
         lane = col % 64
         want = (col // 64) * (HEAD // 2) + lane
         return jnp.where((lane < HEAD // 2) & (row == want), 1.0, 0.0).astype(BF)
+
+    head_pick = head_map
+
+    def prep_gain():
+        raw_copy(7).wait()
+        raw_copy(8).wait()
+        line = lax.broadcasted_iota(jnp.int32, (16, shard), 0)
+        one = jnp.broadcast_to(rga[...].reshape(1, shard).astype(F32), (16, shard))
+        two = jnp.broadcast_to(rgf[...].reshape(1, shard).astype(F32), (16, shard))
+        row = lax.broadcasted_iota(jnp.int32, (shard, pair), 0)
+        col = lax.broadcasted_iota(jnp.int32, (shard, pair), 1)
+        place = jnp.where(col == row + shard * c, 1.0, 0.0).astype(BF)
+        both = jnp.where(line == 0, one, two).astype(BF)
+        wgn[pl.ds(al(16 * d, 16), 16), :] = nn(both, place).astype(BF)
 
     def prep_in():
         at = pl.ds(al(shard * d, 16), shard)
@@ -359,163 +376,162 @@
 
     def w_start(u):
         src = wblk(u, d)
-        if u == 0:
-            src = wg_h
-            pltpu.make_async_copy(src, wblk(u, d), lsem.at[u]).start()
         if u >= 3:
             raw_copy((5, 6, 4)[u - 3]).wait()
-        rcopy(src, wblk(u, d), wsend.at[u, 0], wrecv.at[u, 0], {"dp": aa}).start()
-        rcopy(src, wblk(u, d), wsend.at[u, 1], wrecv.at[u, 1], {"dp": bb}).start()
-        rcopy(src, wblk(u, d), wsend.at[u, 2], wrecv.at[u, 3], {"dp": pp}).start()
+        rcopy(src, src, wsend.at[u], wrecv.at[u, 0], {"dp": aa}).start()
+        rcopy(src, src, wsend.at[u], wrecv.at[u, 1], {"dp": bb}).start()
+        rcopy(src, src, wsend.at[u], wrecv.at[u, 3], {"dp": pp}).start()
+
+    def w_many(u, count):
+        ref, n, at, cut = wunits[u]
+        part = ref.at[pl.ds(0, count * n), pl.ds(at, cut)]
+        return rcopy(part, part, wsend.at[u], wrecv.at[u, 3], {"dp": pp})
 
     def w_wait(u, slot, i):
-        rcopy(wblk(u, i), wblk(u, i), wsend.at[u, 0], wrecv.at[u, slot], {"dp": aa}).wait_recv()
+        rcopy(wblk(u, i), wblk(u, i), wsend.at[u], wrecv.at[u, slot], {"dp": aa}).wait_recv()
 
     def w_relayb(u):
         w_wait(u, 1, bb)
-        rcopy(wblk(u, bb), wblk(u, bb), wsend.at[u, 3], wrecv.at[u, 2], {"dp": aa}).start()
-        rcopy(wblk(u, bb), wblk(u, bb), wsend.at[u, 4], wrecv.at[u, 5], {"dp": pp}).start()
+        rcopy(wblk(u, bb), wblk(u, bb), wsend.at[u], wrecv.at[u, 2], {"dp": aa}).start()
+        rcopy(wblk(u, bb), wblk(u, bb), wsend.at[u], wrecv.at[u, 3], {"dp": pp}).start()
 
     def w_relaya(u):
         w_wait(u, 0, aa)
-        rcopy(wblk(u, aa), wblk(u, aa), wsend.at[u, 5], wrecv.at[u, 4], {"dp": pp}).start()
+        rcopy(wblk(u, aa), wblk(u, aa), wsend.at[u], wrecv.at[u, 3], {"dp": pp}).start()
 
     def w_diag(u):
         w_wait(u, 2, dd)
-        rcopy(wblk(u, dd), wblk(u, dd), wsend.at[u, 6], wrecv.at[u, 6], {"dp": pp}).start()
+        rcopy(wblk(u, dd), wblk(u, dd), wsend.at[u], wrecv.at[u, 3], {"dp": pp}).start()
 
     def w_done(u):
-        w_wait(u, 3, pp)
-        w_wait(u, 4, bb + flip)
-        w_wait(u, 5, aa + flip)
-        w_wait(u, 6, dd + flip)
-        if u == 0:
-            pltpu.make_async_copy(wg_h, wblk(u, d), lsem.at[u]).wait()
+        w_many(u, 4).wait_recv()
 
     def w_sent(u):
-        for slot in range(7):
-            rcopy(wblk(u, d), wblk(u, d), wsend.at[u, slot], wrecv.at[u, 0], {"dp": aa}).wait_send()
+        w_many(u, 7).wait_send()
 
     zfull = (xf, gf, n2, ghf)
     zhbm = (tok, cot, None, None)
 
-    def zblk(u, s, i):
-        return zfull[u].at[pl.ds(al(s * seq + i * rows, 16), rows)]
-
-    def zag_send(u, s, k, way):
+    def zblk(u, s, i, h=None):
+        at = pl.ds(al(s * seq + i * rows, 16), rows)
+        return zfull[u].at[at] if h is None else zfull[u].at[at, pl.ds(h * half, half)]
+
+    def zcopy(u, s, k, way, h, i, src=None):
+        blk = zblk(u, s, i, h)
+        return rcopy(
+            blk if src is None else src, blk, zsend.at[u, s], zrecv.at[u % 3, s, way, k], zdev[way]
+        )
+
+    def zag_send(u, s, k, way, h):
         i = z - k if way == 0 else z + k
         go = (z < 3) & (i >= 0) if way == 0 else (z > 0) & (i <= 3)
 
         @pl.when(go)
         def _():
-            src = zhbm[u].at[s] if k == 0 and zhbm[u] is not None else zblk(u, s, i)
-            rcopy(src, zblk(u, s, i), zsend.at[u, s, way, k], zrecv.at[u, s, way, k], zdev[way]).start()
-
-    def zag_recv(u, s, k, way):
-        i = z - 1 - k if way == 0 else z + 1 + k
+            src = zhbm[u].at[s, :, pl.ds(h * half, half)] if k == 0 and zhbm[u] is not None else None
+            zcopy(u, s, k, way, h, i, src).start()
+
+    def own_copy(u, s):
+        return pltpu.make_async_copy(zhbm[u].at[s], zblk(u, s, z), lsem.at[2 + 2 * u + s])
+
+    def ag(u, s, t, way=None, h=0):
+        if t == 0:
+            if zhbm[u] is not None:
+                own_copy(u, s).start()
+            for part in (0,):
+                for side in (0, 1):
+                    zag_send(u, s, 0, side, part)
+            return
+        i = z - t if way == 0 else z + t
         go = (i >= 0) if way == 0 else (i <= 3)
 
         @pl.when(go)
         def _():
-            rcopy(
-                zblk(u, s, i), zblk(u, s, i), zsend.at[u, s, way, k], zrecv.at[u, s, way, k], zdev[way]
-            ).wait_recv()
-
-    def zag_start(u, s):
-        if zhbm[u] is not None:
-            pltpu.make_async_copy(zhbm[u].at[s], zblk(u, s, z), lsem.at[8 + 2 * u + s]).start()
-        for way in (0, 1):
-            zag_send(u, s, 0, way)
-
-    def ag(u, s, t, way=None):
-        if t == 0:
-            zag_start(u, s)
-            return
-        zag_recv(u, s, t - 1, way)
+            zcopy(u, s, t - 1, way, h, i).wait_recv()
+
         if t < 3:
-            zag_send(u, s, t, way)
+            zag_send(u, s, t, way, h)
 
     def own_here(u, s):
-        pltpu.make_async_copy(zhbm[u].at[s], zblk(u, s, z), lsem.at[8 + 2 * u + s]).wait()
+        own_copy(u, s).wait()
 
     def zag_sent(u, s):
-        for k in range(3):
-            for way in (0, 1):
-                i = z - k if way == 0 else z + k
-                go = (z < 3) & (i >= 0) if way == 0 else (z > 0) & (i <= 3)
-
-                @pl.when(go)
-                def _():
-                    rcopy(
-                        zblk(u, s, i), zblk(u, s, i), zsend.at[u, s, way, k], zrecv.at[u, s, way, k], zdev[way]
-                    ).wait_send()
+        def sent(count):
+            part = zfull[u].at[pl.ds(0, count * rows)]
+            rcopy(part, part, zsend.at[u, s], zrecv.at[u % 3, s, 0, 0], zdev[0]).wait_send()
+
+        @pl.when((z == 0) | (z == 3))
+        def _():
+            sent(1)
+
+        @pl.when((z > 0) & (z < 3))
+        def _():
+            sent(5)
 
     zpart = (pa, pb, pa, pa)
     zgot = (ra, rb, ra, ra)
 
-    def rs_copy(u, s, way, t, dest):
+    def rs_copy(u, s, way, t, dest, h):
+        cut = pl.ds(h * half, half)
         return rcopy(
-            zpart[u].at[pl.ds(al(s * seq + dest * rows, 16), rows)],
-            zgot[u].at[s, way, t],
-            rsend.at[u, s, way, t],
-            rrecv.at[u, s, way, t],
+            zpart[u].at[pl.ds(al(s * seq + dest * rows, 16), rows), cut],
+            zgot[u].at[s, way, t, :, cut],
+            rsend.at[u, s],
+            rrecv.at[1 if u == 1 else 0, s, way, t],
             zdev[way],
         )
 
-    def rs(u, s, t, ways=(0, 1)):
-        for way in ways:
-            from_end = z if way == 0 else 3 - z
-
-            def wait_and(target, base):
-                rs_copy(u, s, way, t - 1, z).wait_recv()
-
-                def body(i, carry):
-                    at = pl.ds(al(base + i * 16, 16), 16)
-                    got = zgot[u][s, way, t - 1, pl.ds(al(i * 16, 16), 16), :].astype(F32)
-                    target[at, :] = (target[at, :].astype(F32) + got).astype(target.dtype)
-                    return carry
-
-                lax.fori_loop(0, rows // 16, body, 0)
-
-            if t == 3:
-                if way == 0:
-                    def first(i, carry):
-                        at = pl.ds(al(i * 16, 16), 16)
-                        acc[at, :] = zpart[u][pl.ds(al(s * seq + own + i * 16, 16), 16), :].astype(F32)
-                        return carry
-
-                    lax.fori_loop(0, rows // 16, first, 0)
-
+    def rs_add(u, s, way, t, target, base, cut):
+        def body(i, carry):
+            at = pl.ds(al(base + i * 16, 16), 16)
+            got = zgot[u][s, way, t, pl.ds(al(i * 16, 16), 16), cut].astype(F32)
+            target[at, cut] = (target[at, cut].astype(F32) + got).astype(target.dtype)
+            return carry
+
+        lax.fori_loop(0, rows // 16, body, 0)
+
+    def rs(u, s, t, way, h=0):
+        from_end = z if way == 0 else 3 - z
+        dest = 3 + z - t if way == 0 else t - from_end
+
+        @pl.when(from_end <= t)
+        def _():
+            if t > 0:
                 @pl.when(from_end > 0)
                 def _():
-                    wait_and(acc, 0)
-            else:
-                dest = 3 + z - t if way == 0 else t - from_end
-
-                @pl.when(from_end <= t)
-                def _():
-                    if t > 0:
-                        @pl.when(from_end > 0)
-                        def _():
-                            wait_and(zpart[u], s * seq + dest * rows)
-
-                    rs_copy(u, s, way, t, dest).start()
-
-    def rs_sent(u, s):
+                    rs_copy(u, s, way, t - 1, z, h).wait_recv()
+                    rs_add(u, s, way, t - 1, zpart[u], s * seq + dest * rows, pl.ds(h * half, half))
+
+            rs_copy(u, s, way, t, dest, h).start()
+
+    def rs_final(u, s):
+        def first(i, carry):
+            at = pl.ds(al(i * 16, 16), 16)
+            acc[at, :] = zpart[u][pl.ds(al(s * seq + own + i * 16, 16), 16), :].astype(F32)
+            return carry
+
+        lax.fori_loop(0, rows // 16, first, 0)
         for way in (0, 1):
             from_end = z if way == 0 else 3 - z
-            for t in range(3):
-                @pl.when(from_end <= t)
-                def _():
-                    rs_copy(u, s, way, t, z).wait_send()
+
+            @pl.when(from_end > 0)
+            def _():
+                for h in (0,):
+                    rs_copy(u, s, way, 2, z, h).wait_recv()
+                rs_add(u, s, way, 2, acc, 0, pl.ds(0, width))
+
+    def rs_sent(u, s):
+        part = zpart[u].at[pl.ds(0, 3 * rows)]
+        rcopy(part, part, rsend.at[u, s], rrecv.at[0, s, 0, 0], zdev[0]).wait_send()
 
     gunits = (
-        (gf, act, 0, ff, gdown_h),
-        (n2, dgu, 0, ff, ggate_h),
-        (n2, dgu, ff, ff, gup_h),
-        (ghf, ob, 0, qp, gout_h),
-        (n1, dq3, 0, inw, gin_h),
-    )
+        (gf, act, 0, ff),
+        (n2, dgu, 0, ff),
+        (n2, dgu, ff, ff),
+        (ghf, ob, 0, qp),
+        (n1, dq3, 0, inw),
+    )
+
     def xslot(u, chip):
         b, n = u % 2, gunits[u][3]
         return xb.at[b, pl.ds(al(chip * shard, 16), shard), pl.ds(0, n)]
@@ -525,12 +541,12 @@
         return gb.at[b, pl.ds(al(chip * pair + core * shard, 16), shard), pl.ds(0, n)]
 
     def g_exchange(u, chip, i):
-        return rcopy(gslot(u, chip, 1 - c), xslot(u, chip), gsend.at[u, i], grecv.at[u, i], {"dp": pp})
+        return rcopy(gslot(u, chip, 1 - c), xslot(u, chip), gsend.at[u % 2], grecv.at[u % 2, i], {"dp": pp})
 
     chips = (chip_d, chip_x, chip_y, chip_own)
 
     def g_compute(u, i):
-        left, right, at, n, _ = gunits[u]
+        left, right, at, n = gunits[u]
         chip = chips[i]
         if u >= 2 and i == 0:
             pl.semaphore_wait(credit.at[0], 1)
@@ -561,13 +577,13 @@
 
     def g_hop(u):
         b, n = u % 2, gunits[u][3]
-        return rcopy(xslot(u, chip_d), hop.at[b, :, pl.ds(0, n)], gsend.at[u, 4], grecv.at[u, 4], {"dp": aa})
+        return rcopy(xslot(u, chip_d), hop.at[b, :, pl.ds(0, n)], gsend.at[b], grecv.at[b, 4], {"dp": aa})
 
     def g_last(u, way):
         b, n = u % 2, gunits[u][3]
         chip, dev = (chip_a, aa) if way == 0 else (chip_b, bb)
         return rcopy(
-            xslot(u, chip), fin.at[b, way, :, pl.ds(0, n)], gsend.at[u, 5 + way], grecv.at[u, 5 + way], {"dp": dev}
+            xslot(u, chip), fin.at[b, way, :, pl.ds(0, n)], gsend.at[b], grecv.at[b, 5 + way], {"dp": dev}
         )
 
     def g_first(u):
@@ -590,37 +606,43 @@
             pl.semaphore_wait(credit.at[2], 1)
         g_last(u, 1).start()
 
+    def picked(at, cut, which):
+        value = stage[at, cut]
+        high = value.astype(BF)
+        rest = value - high.astype(F32)
+        mid = rest.astype(BF)
+        low = (rest - mid.astype(F32)).astype(BF)
+        return nt(high, which) + (nt(mid, which) + nt(low, which))
+
     def g_finish(u):
-        b, n, out = u % 2, gunits[u][3], gunits[u][4]
+        b, n = u % 2, gunits[u][3]
         g_exchange(u, chip_own, 3).wait_recv()
         g_last(u, 0).wait_recv()
         g_last(u, 1).wait_recv()
+        out = (gdown_v, ggate_v, gup_v, stage, stage)[u]
 
         def body(i, carry):
             at = pl.ds(al(i * 16, 16), 16)
             total = gb[b, pl.ds(al(chip_own * pair + c * shard + i * 16, 16), 16), pl.ds(0, n)].astype(F32)
             total = total + xb[b, pl.ds(al(chip_own * shard + i * 16, 16), 16), pl.ds(0, n)].astype(F32)
             total = total + fin[b, 0, at, pl.ds(0, n)].astype(F32)
-            stage[b, at, pl.ds(0, n)] = total + fin[b, 1, at, pl.ds(0, n)].astype(F32)
+            out[at, pl.ds(0, n)] = total + fin[b, 1, at, pl.ds(0, n)].astype(F32)
             return carry
 
-        if u >= 2:
-            g_out(u - 2).wait()
         lax.fori_loop(0, shard // 16, body, 0)
-        g_out(u).start()
-        for i in range(4):
-            g_exchange(u, chips[i], i).wait_send()
-        g_hop(u).wait_send()
-        g_last(u, 0).wait_send()
-        g_last(u, 1).wait_send()
+        rows_all = pl.ds(0, shard)
+        if u == 3:
+            gout_v[...] = picked(rows_all, pl.ds(0, qp), head_pick(gout_v.shape[1]))
+        if u == 4:
+            gq_v[...] = picked(rows_all, pl.ds(0, qp), head_pick(gq_v.shape[1]))
+            gk_v[...] = picked(rows_all, pl.ds(qp, kp), head_pick(gk_v.shape[1]))
+            gv_v[...] = picked(rows_all, pl.ds(qp + kp, kp), head_pick(gv_v.shape[1]))
+        part = gb.at[b, pl.ds(0, 7 * shard), pl.ds(0, n)]
+        rcopy(part, part, gsend.at[b], grecv.at[b, 0], {"dp": pp}).wait_send()
         if u < 3:
             pl.semaphore_signal(credit.at[0], inc=1, device_id={"dp": pp}, device_id_type=MESH)
             pl.semaphore_signal(credit.at[1], inc=1, device_id={"dp": aa}, device_id_type=MESH)
             pl.semaphore_signal(credit.at[2], inc=1, device_id={"dp": bb}, device_id_type=MESH)
-
-    def g_out(u):
-        b, n, out = u % 2, gunits[u][3], gunits[u][4]
-        return pltpu.make_async_copy(stage.at[b, :, pl.ds(0, n)], out, osem.at[u])
 
     def gain_rows():
         for j in range(4):
@@ -684,8 +706,9 @@
             sc = jnp.where(mask, nt(q, k), -1e30)
             e = jnp.exp(sc - jnp.max(sc, axis=-1, keepdims=True))
             p = e * (1.0 / jnp.sum(e, axis=-1, keepdims=True))
+            p = p.astype(BF)
             pr[s * heads + h] = p
-            ob[at, pl.ds(al(h * LANES, LANES), LANES)] = nn(p.astype(BF), v).astype(BF)
+            ob[at, pl.ds(al(h * LANES, LANES), LANES)] = nn(p, v).astype(BF)
             return carry
 
         half = heads // 2
@@ -724,14 +747,14 @@
             h = tbuf[s, r, :].astype(F32) + acc[r, :]
             hb[pl.ds(al(base + i * 16, 16), 16), :] = h
             scale = lax.rsqrt(jnp.mean(h * h, axis=-1, keepdims=True) + eps)
-            n2[pl.ds(al(s * seq + own + i * 16, 16), 16), :] = (h * scale * gain).astype(BF)
+            real = cols[s, pl.ds(al(own + i * 16, 16), 16), 2:3]
+            n2[pl.ds(al(s * seq + own + i * 16, 16), 16), :] = (h * (scale * real) * gain).astype(BF)
             return carry
 
         lax.fori_loop(0, rows // 16, body, 0)
 
     def feed(s, part):
         at = pl.ds(s * seq, seq)
-        real = cols[s, :, 2:3]
         if part == 0:
             own_here(1, s)
 
@@ -739,10 +762,10 @@
             col = al(t * 256, 256)
             gate = nn(n2[at, :], wu[:, pl.ds(col, 256)])
             upper = nn(n2[at, :], wu[:, pl.ds(al(ff + t * 256, 256), 256)])
-            back = nn(gf[at, :], wd[:, pl.ds(col, 256)]) * real
+            back = nn(gf[at, :], wd[:, pl.ds(col, 256)])
             sigma = 1.0 / (1.0 + jnp.exp(-gate))
             swish = gate * sigma
-            act[at, pl.ds(col, 256)] = (swish * upper * real).astype(BF)
+            act[at, pl.ds(col, 256)] = (swish * upper).astype(BF)
             dgu[at, pl.ds(col, 256)] = (back * upper * sigma * (1.0 + gate * (1.0 - sigma))).astype(BF)
             dgu[at, pl.ds(al(ff + t * 256, 256), 256)] = (back * swish).astype(BF)
             return carry
@@ -755,11 +778,10 @@
             r = pl.ds(al(i * 16, 16), 16)
             real = cols[s, pl.ds(al(own + i * 16, 16), 16), 2:3]
             y = (hb[pl.ds(al(s * rows + i * 16, 16), 16), :] + acc[r, :]) * real
-            ybuf[s, r, :] = y.astype(BF)
+            out_v[s, r, :] = y.astype(BF)
             return carry
 
         lax.fori_loop(0, rows // 16, body, 0)
-        pltpu.make_async_copy(ybuf.at[s], out_h.at[s], osem.at[5 + s]).start()
 
     def norm2_back(s):
         gain = gains[1:2, :]
@@ -775,7 +797,7 @@
             dy = gf[pl.ds(al(s * seq + own + i * 16, 16), 16), :].astype(F32)
             dy = dy * cols[s, pl.ds(al(own + i * 16, 16), 16), 2:3]
             dhr = dy + scale * (inner - unit * jnp.mean(inner * unit, axis=-1, keepdims=True))
-            dh[ro, :] = dhr
+            gtok_v[s, r, :] = dhr
             ghf[pl.ds(al(s * seq + own + i * 16, 16), 16), :] = dhr.astype(BF)
             return carry + jnp.sum(grad * unit, axis=0, keepdims=True)
 
@@ -784,7 +806,7 @@
     def grad_heads(s):
         at = pl.ds(s * seq, seq)
         for j in range(qp // 256):
-            dob[at, pl.ds(j * 256, 256)] = nn(ghf[at, :], wo[:, pl.ds(j * 256, 256)]).astype(BF)
+            dq3[at, pl.ds(j * 256, 256)] = nn(ghf[at, :], wo[:, pl.ds(j * 256, 256)]).astype(BF)
 
     def attend_back(s):
         at = pl.ds(s * seq, seq)
@@ -799,11 +821,12 @@
                 h = g * per_group + m
                 hat = pl.ds(al(h * LANES, LANES), LANES)
                 q = qkv[at, hat]
-                do = dob[at, hat]
-                p = pr[s * heads + h]
+                do = dq3[at, hat]
+                low = pr[s * heads + h]
+                p = low.astype(F32)
                 dp = nt(do, v)
                 ds = (p * (dp - jnp.sum(p * dp, axis=-1, keepdims=True))).astype(BF)
-                dv = dv + tn(p.astype(BF), do)
+                dv = dv + tn(low, do)
                 dk = dk + tn(ds, q)
                 dq = nn(ds, k) * head_scale
                 dq3[at, hat] = (dq * cosine - pltpu.roll(dq, LANES // 2, 1) * sine).astype(BF)
@@ -820,378 +843,369 @@
 
         def body(i, carry):
             r = pl.ds(al(i * 16, 16), 16)
-            ro = pl.ds(al(s * rows + i * 16, 16), 16)
             x = tbuf[s, r, :].astype(F32)
             scale = lax.rsqrt(jnp.mean(x * x, axis=-1, keepdims=True) + eps)
             unit = x * scale
             grad = acc[r, :]
             inner = grad * gain
-            dh[ro, :] = dh[ro, :] + scale * (inner - unit * jnp.mean(inner * unit, axis=-1, keepdims=True))
+            gtok_v[s, r, :] += scale * (inner - unit * jnp.mean(inner * unit, axis=-1, keepdims=True))
             return carry
 
         lax.fori_loop(0, rows // 16, body, 0)
-        pltpu.make_async_copy(
-            dh.at[pl.ds(s * rows, rows)], gtok_h.at[s], osem.at[7 + s]
-        ).start()
 
     X, COT, N2, GH = 0, 1, 2, 3
     BR, FFN, DN2, DN1 = 0, 1, 2, 3
 
     def tok_copy(s):
-        return pltpu.make_async_copy(tok.at[s], tbuf.at[s], lsem.at[5 + s])
+        return pltpu.make_async_copy(tok.at[s], tbuf.at[s], lsem.at[s])
 
     def fin_br(s):
-        rs(BR, s, 3)
+        rs_final(BR, s)
         tok_copy(s).wait()
         norm2(s)
         ag(N2, s, 0)
 
     def fin_dn2(s):
-        rs(DN2, s, 3)
+        rs_final(DN2, s)
         norm2_back(s)
         ag(GH, s, 0)
 
     def fin_ffn(s):
-        rs(FFN, s, 3)
+        rs_final(FFN, s)
         finish_out(s)
 
     def fin_dn1(s):
-        rs(DN1, s, 3)
+        rs_final(DN1, s)
         norm1_back(s)
 
-    def e_copy(i):
-        dev = {"tensor": (z + i + 1) % 4} if i < 3 else {"dp": (d + i - 2) % 8}
-        return rcopy(gsum if i < 3 else gex.at[10], gex.at[i], esend.at[i], erecv.at[i], dev)
-
-    def e1s():
-        for j in range(4):
-            at = pl.ds(j * pair, pair)
-            gsum[j : j + 1, :] = gpart[0:1, at] / gains[0:1, at]
-            gsum[4 + j : 5 + j, :] = gpart[1:2, j * pair : (j + 1) * pair]
-        for i in range(3):
-            e_copy(i).start()
-
-    def e1w():
-        for i in range(3):
-            e_copy(i).wait()
-        gex[10] = gsum[...] + gex[0] + gex[1] + gex[2]
-        for i in range(3, 10):
-            e_copy(i).start()
-
-    def e2w():
-        for i in range(3, 10):
-            e_copy(i).wait()
-        total = gex[10]
-        for i in range(3, 10):
-            total = total + gex[i]
-        gsum[...] = total
-
-    for i in range(7):
+    def e_copy(i, src, dev):
+        line = i < 6
+        return rcopy(src, gex.at[i], esend.at[0 if line else 1], erecv.at[i if line else i // 2 + 3], dev)
+
+    def e_line(t):
+        if t == 0:
+            for j in range(4):
+                at = pl.ds(j * pair, pair)
+                gsum[j : j + 1, :] = gpart[0:1, at] / gains[0:1, at]
+                gsum[4 + j : 5 + j, :] = gpart[1:2, at]
+        for way in (0, 1):
+            here = (z - t >= 0) if way == 0 else (z + t <= 3)
+            on = (z < 3) if way == 0 else (z > 0)
+            slot = 3 * way + t
+
+            @pl.when(here)
+            def _():
+                if t > 0:
+                    e_copy(slot - 1, gsum, zdev[way]).wait_recv()
+                if t < 3:
+                    @pl.when(on)
+                    def _():
+                        e_copy(slot, gsum if t == 0 else gex.at[slot - 1], zdev[way]).start()
+
+        if t == 3:
+            gex[6] = gsum[...]
+            for way in (0, 1):
+                for k in (1, 2, 3):
+                    @pl.when((z - k >= 0) if way == 0 else (z + k <= 3))
+                    def _():
+                        gex[6] += gex[3 * way + k - 1]
+
+            e_copy(7, gex.at[6], {"dp": pp}).start()
+
+    def e_plane(t):
+        i = 7 + 2 * t
+        dev = (pp, aa, bb)[t]
+        e_copy(i, gex.at[i - 1], {"dp": dev}).wait()
+        total = gex[i - 1] + gex[i]
+        if t < 2:
+            gex[i + 1] = total
+            e_copy(i + 2, gex.at[i + 1], {"dp": (aa, bb)[t]}).start()
+        else:
+            gex[12] = total
+            for at, out in ((0, gone_v), (4, gtwo_v)):
+                line = gex[12, pl.ds(at + d // 2, 1), :]
+                out[...] = jnp.where(c == 0, line[:, :shard], line[:, shard:])
+
+    def e_sent():
+        def sent(count):
+            part = gex.at[pl.ds(0, count)]
+            rcopy(part, part, esend.at[0], erecv.at[0], zdev[0]).wait_send()
+
+        @pl.when((z == 0) | (z == 3))
+        def _():
+            sent(1)
+
+        @pl.when((z > 0) & (z < 3))
+        def _():
+            sent(5)
+
+    def clean(i):
+        if i == 0:
+            for u in range(6):
+                w_sent(u)
+        elif i < 4:
+            for s in (0, 1):
+                zag_sent((COT, N2, GH)[i - 1], s)
+        else:
+            rs_sent(FFN, i - 4)
+
+    for i in (7, 8, 0, 1, 2, 3, 5, 6, 4):
         raw_copy(i).start()
     gpart[...] = jnp.zeros_like(gpart)
     for s in (0, 1):
         tok_copy(s).start()
-    pl.semaphore_wait(barrier, 10)
+    pl.semaphore_wait(barrier, 3 + (z + 3) // 4 + (6 - z) // 4)
     ag(X, 0, 0)
+    prep_in()
     ag(X, 1, 0)
     prep_out()
-    prep_in()
+    prep_rows(0)
+    prep_gain()
     w_start(0)
     w_start(1)
+    w_relayb(0)
     w_start(2)
     ag(X, 0, 1, 1)
-    w_relayb(0)
-    prep_rows(0)
     ag(X, 0, 1, 0)
+    w_relaya(1)
+    w_diag(0)
+    ag(X, 1, 1, 0)
+    ag(X, 0, 2, 0)
+    w_relayb(1)
     ag(COT, 0, 0)
-    w_relaya(1)
-    w_relayb(2)
-    ag(X, 0, 2, 0)
-    prep_rows(1)
-    ag(X, 1, 1, 0)
-    w_relaya(2)
-    w_relayb(1)
-    w_diag(0)
-    w_diag(2)
     w_relaya(0)
-    ag(X, 0, 2, 1)
     w_done(0)
     gain_rows()
+    norm1(0, 1)
+    norm1(0, 0)
+    w_relayb(2)
+    ag(X, 0, 2, 1)
+    ag(COT, 1, 0)
     ag(X, 1, 1, 1)
-    norm1(0, 0)
+    norm1(1, 1)
     w_start(3)
-    ag(COT, 0, 1, 0)
     norm1(1, 0)
+    prep_rows(1)
+    w_start(4)
     norm1(0, 2)
-    norm1(0, 1)
-    ag(COT, 1, 0)
     w_diag(1)
+    ag(COT, 0, 1, 1)
+    ag(X, 0, 3, 1)
+    w_relaya(2)
+    w_diag(2)
     ag(X, 0, 3, 0)
-    ag(X, 0, 3, 1)
+    norm1(0, 3)
     w_done(1)
-    norm1(0, 3)
     project(0)
     attend(0, 0)
     attend(0, 1)
-    w_start(4)
-    ag(COT, 0, 1, 1)
+    w_done(2)
+    spread(0, pa, ob, wo, 512)
+    rs(BR, 0, 0, 1)
+    ag(COT, 0, 1, 0)
+    rs(BR, 0, 1, 1)
+    ag(X, 1, 2, 0)
+    rs(BR, 0, 0, 0)
+    rs(BR, 0, 1, 0)
     w_start(5)
     ag(X, 1, 2, 1)
-    w_done(2)
-    spread(0, pa, ob, wo, 512)
-    rs(BR, 0, 0, (0,))
-    rs(BR, 0, 1, (0,))
-    ag(X, 1, 2, 0)
-    rs(BR, 0, 0, (1,))
-    rs(BR, 0, 1, (1,))
-    rs(BR, 0, 2, (1,))
+    w_relaya(4)
+    rs(BR, 0, 2, 1)
+    rs(BR, 0, 2, 0)
+    ag(COT, 0, 2, 0)
     norm1(1, 2)
-    rs(BR, 0, 2, (0,))
-    ag(COT, 0, 2, 0)
-    ag(COT, 0, 2, 1)
     ag(X, 1, 3, 0)
     ag(X, 1, 3, 1)
+    w_relayb(3)
     norm1(1, 3)
-    w_relayb(3)
-    norm1(1, 1)
+    project(1)
+    attend(1, 0)
+    w_relaya(3)
+    fin_br(0)
     w_relayb(4)
-    fin_br(0)
-    project(1)
+    zag_sent(X, 0)
+    ag(COT, 0, 2, 1)
+    w_diag(3)
+    attend(1, 1)
+    spread(1, pa, ob, wo, 512)
+    rs_sent(BR, 0)
+    ag(N2, 0, 1, 1)
+    rs(BR, 1, 0, 1)
+    ag(N2, 0, 1, 0)
     w_relayb(5)
-    w_relaya(4)
-    rs_sent(BR, 0)
-    attend(1, 0)
-    attend(1, 1)
-    w_relaya(3)
-    spread(1, pa, ob, wo, 512)
-    rs(BR, 1, 0, (1,))
-    rs(BR, 1, 0, (0,))
-    w_diag(3)
-    zag_sent(X, 0)
+    rs(BR, 1, 0, 0)
+    rs(BR, 1, 1, 1)
+    w_done(3)
+    ag(N2, 0, 2, 0)
+    rs(BR, 1, 1, 0)
+    ag(N2, 0, 2, 1)
+    w_relaya(5)
+    rs(BR, 1, 2, 0)
+    w_diag(4)
+    rs(BR, 1, 2, 1)
+    w_diag(5)
+    w_done(5)
     ag(COT, 0, 3, 0)
-    w_relaya(5)
-    ag(N2, 0, 1, 1)
-    w_done(3)
-    ag(N2, 0, 1, 0)
-    w_diag(5)
-    rs(BR, 1, 1, (1,))
-    rs(BR, 1, 1, (0,))
-    ag(N2, 0, 2, 1)
-    ag(N2, 0, 2, 0)
-    w_diag(4)
+    ag(COT, 1, 1, 1)
     w_done(4)
+    ag(COT, 1, 1, 0)
+    ag(N2, 0, 3, 1)
+    ag(N2, 0, 3, 0)
     ag(COT, 0, 3, 1)
-    rs(BR, 1, 2, (1,))
-    ag(N2, 0, 3, 1)
-    w_done(5)
-    rs(BR, 1, 2, (0,))
-    ag(N2, 0, 3, 0)
-    ag(COT, 1, 1, 0)
     feed(0, 0)
     feed(0, 1)
     feed(0, 2)
-    ag(COT, 1, 1, 1)
     fin_br(1)
     feed(0, 3)
     spread(0, pa, dgu, wu, 256, 0, 2)
     spread(0, pa, dgu, wu, 256, 1, 2)
-    rs(DN2, 0, 0, (1,))
+    ag(COT, 1, 2, 1)
+    rs(DN2, 0, 0, 1)
+    rs(DN2, 0, 0, 0)
+    spread(0, pb, act, wd, 512)
+    ag(N2, 1, 1, 0)
+    rs(DN2, 0, 1, 0)
+    ag(COT, 1, 3, 1)
+    rs(FFN, 0, 0, 0)
+    ag(N2, 1, 1, 1)
+    ag(N2, 1, 2, 1)
+    rs_sent(BR, 1)
     ag(COT, 1, 2, 0)
-    rs(DN2, 0, 0, (0,))
-    spread(0, pb, act, wd, 512)
-    rs_sent(BR, 1)
-    ag(N2, 1, 1, 1)
-    ag(N2, 1, 1, 0)
-    rs(DN2, 0, 1, (0,))
-    ag(N2, 1, 2, 1)
-    rs(DN2, 0, 1, (1,))
-    rs(FFN, 0, 0, (1,))
-    rs(FFN, 0, 0, (0,))
-    ag(COT, 1, 2, 1)
-    rs(DN2, 0, 2, (1,))
+    rs(DN2, 0, 1, 1)
+    ag(N2, 1, 2, 0)
+    rs(FFN, 0, 0, 1)
+    rs(DN2, 0, 2, 0)
+    rs(DN2, 0, 2, 1)
+    ag(N2, 1, 3, 0)
     zag_sent(X, 1)
-    ag(N2, 1, 2, 0)
-    rs(DN2, 0, 2, (0,))
+    rs(FFN, 0, 1, 1)
+    rs(FFN, 0, 1, 0)
+    ag(N2, 1, 3, 1)
     ag(COT, 1, 3, 0)
-    rs(FFN, 0, 1, (1,))
-    ag(COT, 1, 3, 1)
-    ag(N2, 1, 3, 1)
-    ag(N2, 1, 3, 0)
     feed(1, 0)
-    rs(FFN, 0, 1, (0,))
     feed(1, 1)
     feed(1, 2)
     feed(1, 3)
     fin_dn2(0)
     spread(1, pa, dgu, wu, 256, 0, 2)
     spread(1, pa, dgu, wu, 256, 1, 2)
-    rs(DN2, 1, 0, (1,))
+    rs(DN2, 1, 0, 0)
     g_compute(0, 0)
-    rs(DN2, 1, 0, (0,))
+    rs(DN2, 1, 0, 1)
     g_compute(0, 1)
+    ag(GH, 0, 1, 0)
+    ag(GH, 0, 1, 1)
+    g_first(0)
     g_compute(0, 2)
-    ag(GH, 0, 1, 0)
-    g_first(0)
-    ag(GH, 0, 1, 1)
     g_compute(0, 3)
-    rs(DN2, 1, 1, (0,))
-    rs(DN2, 1, 1, (1,))
-    g_firstb(0)
+    rs(DN2, 1, 1, 1)
+    rs(DN2, 1, 1, 0)
     ag(GH, 0, 2, 1)
     ag(GH, 0, 2, 0)
     g_compute(1, 0)
-    rs(DN2, 1, 2, (0,))
-    rs(DN2, 1, 2, (1,))
+    g_firstb(0)
+    rs(DN2, 1, 2, 0)
+    rs(DN2, 1, 2, 1)
+    spread(1, pb, act, wd, 512)
+    rs(FFN, 1, 0, 1)
+    rs(FFN, 1, 0, 0)
+    rs_sent(DN2, 0)
+    g_second(0)
+    g_first(1)
     g_compute(1, 1)
-    spread(1, pb, act, wd, 512)
-    rs(FFN, 1, 0, (0,))
+    g_compute(1, 2)
+    ag(GH, 0, 3, 1)
     ag(GH, 0, 3, 0)
-    g_second(0)
-    rs(FFN, 1, 0, (1,))
-    ag(GH, 0, 3, 1)
-    g_compute(1, 2)
-    g_first(1)
     fin_dn2(1)
-    rs_sent(DN2, 0)
     g_firstb(1)
     grad_heads(0)
     attend_back(0)
+    rs_sent(DN2, 1)
     spread_gain(0)
+    rs(DN1, 0, 0, 0)
+    ag(GH, 1, 1, 1)
+    rs(DN1, 0, 0, 1)
+    ag(GH, 1, 1, 0)
+    g_second(1)
+    rs(FFN, 1, 1, 0)
     g_finish(0)
-    rs(DN1, 0, 0, (1,))
-    rs(DN1, 0, 0, (0,))
-    ag(GH, 1, 1, 0)
-    ag(GH, 1, 1, 1)
-    rs(FFN, 1, 1, (0,))
     g_compute(1, 3)
-    g_second(1)
     g_compute(2, 0)
+    ag(GH, 1, 2, 1)
+    rs(FFN, 1, 1, 1)
+    g_first(2)
+    rs(FFN, 0, 2, 1)
+    ag(GH, 1, 2, 0)
+    rs(FFN, 0, 2, 0)
     g_compute(2, 1)
-    rs(FFN, 1, 1, (1,))
-    ag(GH, 1, 2, 0)
-    rs(DN1, 0, 1, (1,))
-    ag(GH, 1, 2, 1)
-    g_first(2)
-    rs(DN1, 0, 1, (0,))
-    rs_sent(DN2, 1)
     g_compute(2, 2)
     g_compute(2, 3)
-    rs(FFN, 1, 2, (0,))
-    g_finish(1)
+    rs(DN1, 0, 1, 1)
     g_firstb(2)
-    rs(FFN, 0, 2, (1,))
     ag(GH, 1, 3, 0)
+    rs(FFN, 1, 2, 0)
+    ag(GH, 1, 3, 1)
+    grad_heads(1)
     g_second(2)
-    ag(GH, 1, 3, 1)
-    g_compute(3, 0)
-    grad_heads(1)
+    clean(3)
     attend_back(1)
     spread_gain(1)
-    rs(DN1, 1, 0, (0,))
+    rs(DN1, 1, 0, 0)
+    e_line(0)
+    g_finish(1)
+    g_compute(3, 0)
+    rs(DN1, 1, 0, 1)
+    rs(FFN, 1, 2, 1)
+    rs(DN1, 0, 1, 0)
     g_compute(3, 1)
-    g_first(3)
-    rs(DN1, 1, 0, (1,))
     g_compute(3, 2)
     g_compute(3, 3)
-    rs(FFN, 1, 2, (1,))
-    e1s()
+    g_first(3)
+    clean(4)
+    fin_ffn(0)
     g_firstb(3)
-    rs(FFN, 0, 2, (0,))
+    clean(0)
+    clean(1)
+    clean(2)
     g_finish(2)
     g_compute(4, 0)
+    g_compute(4, 1)
+    e_line(1)
     g_second(3)
-    rs(DN1, 1, 1, (1,))
-    g_compute(4, 1)
-    rs(DN1, 1, 1, (0,))
-    rs(DN1, 0, 2, (0,))
-    rs(DN1, 0, 2, (1,))
+    g_compute(4, 2)
+    rs(DN1, 1, 1, 1)
+    rs(DN1, 1, 1, 0)
+    e_line(2)
     g_first(4)
-    g_compute(4, 2)
+    e_line(3)
+    rs(DN1, 0, 2, 1)
+    g_finish(3)
+    rs(DN1, 0, 2, 0)
+    e_plane(0)
+    g_firstb(4)
     g_compute(4, 3)
+    rs(DN1, 1, 2, 1)
+    g_second(4)
+    rs(DN1, 1, 2, 0)
+    fin_dn1(0)
+    e_plane(1)
+    clean(5)
     fin_ffn(1)
-    g_firstb(4)
-    g_second(4)
-    fin_ffn(0)
-    rs(DN1, 1, 2, (1,))
-    rs(DN1, 1, 2, (0,))
-    g_finish(3)
-    fin_dn1(0)
-    e1w()
+    e_plane(2)
     g_finish(4)
-    e2w()
     fin_dn1(1)
-    last = pltpu.make_async_copy(gsum, ggain_h, osem.at[9])
-    last.start()
-    for u in range(6):
-        w_sent(u)
-    for u in (COT, N2, GH):
-        for s in (0, 1):
-            zag_sent(u, s)
     for s in (0, 1):
-        rs_sent(FFN, s)
         rs_sent(DN1, s)
-    g_out(3).wait()
-    g_out(4).wait()
-    for s in (0, 1):
-        pltpu.make_async_copy(ybuf.at[s], out_h.at[s], osem.at[5 + s]).wait()
-        pltpu.make_async_copy(dh.at[pl.ds(s * rows, rows)], gtok_h.at[s], osem.at[7 + s]).wait()
-    last.wait()
-
-
-def finish_kernel(dims, *refs):
-    (qp, kp, shard) = dims
-    ins, outs, bufs, (sem_in, sem_out) = refs[:8], refs[8:19], refs[19:33], refs[33:]
-    given, made = bufs[:8], bufs[8:]
-    d = lax.axis_index("dp")
-
-    def load(i):
-        return pltpu.make_async_copy(ins[i], given[i], sem_in.at[i])
-
-    def save(i, src):
-        return pltpu.make_async_copy(src, outs[i], sem_out.at[i])
-
-    def head_map(n):
-        row = lax.broadcasted_iota(jnp.int32, (n, n // HEAD * LANES), 0)
-        col = lax.broadcasted_iota(jnp.int32, (n, n // HEAD * LANES), 1)
-        lane = col % 64
-        want = (col // 64) * (HEAD // 2) + lane
-        return jnp.where((lane < HEAD // 2) & (row == want), 1.0, 0.0).astype(BF)
-
-    def picked(value, which):
-        high = value.astype(BF)
-        rest = value - high.astype(F32)
-        mid = rest.astype(BF)
-        low = (rest - mid.astype(F32)).astype(BF)
-        return nt(high, which) + (nt(mid, which) + nt(low, which))
-
-    order = (1, 2, 0, 3, 4, 5, 6, 7)
-    for i in order:
-        load(i).start()
-    ggain, gin, gout = given[:3]
-    tone, ttwo, tq, tk, tv, tout = made
-    wide, narrow = head_map(tq.shape[1]), head_map(tk.shape[1])
-    load(1).wait()
-    tq[...] = picked(gin[:, :qp], wide)
-    save(2, tq).start()
-    tk[...] = picked(gin[:, qp : qp + kp], narrow)
-    save(3, tk).start()
-    tv[...] = picked(gin[:, qp + kp :], narrow)
-    save(4, tv).start()
-    load(2).wait()
-    tout[...] = picked(gout[...], wide)
-    save(5, tout).start()
-    load(0).wait()
-    for i, ref in enumerate((tone, ttwo)):
-        line = ggain[pl.ds(4 * i + d // 2, 1), :]
-        ref[...] = jnp.where(d % 2 == 0, line[:, :shard], line[:, shard:])
-        save(i, ref).start()
-    for i in range(3, 8):
-        load(i).wait()
-        save(i + 3, given[i]).start()
-    for i, ref in enumerate(made):
-        save(i, ref).wait()
-    for i in range(3, 8):
-        save(i + 3, given[i]).wait()
+    e_sent()
+
+
+def put_out(*refs):
+    ins, outs, sem = refs[:11], refs[11:22], refs[22]
+    copies = [pltpu.make_async_copy(src, dst, sem.at[i]) for i, (src, dst) in enumerate(zip(ins, outs))]
+    for copy in copies:
+        copy.start()
+    for copy in copies:
+        copy.wait()
 
 
 def fused(
@@ -1218,14 +1232,6 @@
     qp = q_cols // HEAD * LANES
     kp = groups * LANES
     inw = qp + 2 * kp
-    even = lax.axis_index("dp") % 2 == 0
-
-    def placed(gain):
-        return jnp.where(even, jnp.pad(gain, (0, shard)), jnp.pad(gain, (shard, 0)))[None, :]
-
-    line = lax.broadcasted_iota(jnp.int32, (16, 2 * shard), 0)
-    gain = jnp.where(line == 0, placed(gain_attn), placed(gain_ffn))
-
     total = micro * seq
     vm = pltpu.VMEM
     dma = pltpu.SemaphoreType.DMA
@@ -1241,12 +1247,10 @@
         vm((total, width), BF),
         vm((total, inw), BF),
         vm((total, qp), BF),
-        vm((total, qp), BF),
         vm((total, ff), BF),
         vm((total, inw), BF),
         vm((total, 2 * ff), BF),
-        vm((micro * qp // LANES, seq, seq), F32),
-        vm((micro * rows, width), F32),
+        vm((micro * qp // LANES, seq, seq), BF),
         vm((micro * rows, width), F32),
         vm((total, width), BF),
         vm((total, width), BF),
@@ -1256,28 +1260,15 @@
         vm((2, width // 2, ff), BF),
         vm((2, shard, ff), BF),
         vm((2, 2, shard, ff), BF),
-        vm((2, shard, ff), F32),
+        vm((shard, ff), F32),
         vm((rows, width), F32),
         vm((16, width), F32),
         vm((8, width), F32),
         vm((8, width // 4), F32),
-        vm((11, 8, width // 4), F32),
+        vm((13, 8, width // 4), F32),
         vm((micro, rows, width), BF),
-        vm((micro, rows, width), BF),
-        dma((6, 7)),
-        dma((6, 7)),
-        dma((4, 2, 2, 3)),
-        dma((4, 2, 2, 3)),
-        dma((4, 2, 2, 3)),
-        dma((4, 2, 2, 3)),
-        dma((5, 7)),
-        dma((5, 7)),
-        dma((10,)),
-        dma((10,)),
-        dma((12,)),
-        dma((10,)),
-        pltpu.SemaphoreType.REGULAR((3,)),
-        dma((7,)),
+        vm(gain_attn.shape, BF),
+        vm(gain_ffn.shape, BF),
         vm(w_query.shape, BF),
         vm(w_key.shape, BF),
         vm(w_value.shape, BF),
@@ -1285,36 +1276,53 @@
         vm((micro, seq, LANES), F32),
         vm((micro, seq, LANES), F32),
         vm((micro, seq, LANES), F32),
+        dma((6,)),
+        dma((6, 4)),
+        dma((4, 2)),
+        dma((3, 2, 2, 3)),
+        dma((4, 2)),
+        dma((2, 2, 2, 3)),
+        dma((2,)),
+        dma((2, 7)),
+        dma((2,)),
+        dma((9,)),
+        dma((6,)),
+        dma((9,)),
+        pltpu.SemaphoreType.REGULAR((3,)),
     ]
     hbm = pl.BlockSpec(memory_space=pl.ANY)
     vmem = pl.BlockSpec(memory_space=pltpu.VMEM)
     smem = pl.BlockSpec(memory_space=pltpu.SMEM)
     shape = jax.ShapeDtypeStruct
     shapes = [
-        shape((micro, rows, width), BF),
-        shape((micro, rows, width), F32),
-        shape((shard, ff), F32),
-        shape((shard, ff), F32),
-        shape((shard, ff), F32),
-        shape((shard, qp), F32),
-        shape((shard, inw), F32),
-        shape((8, width // 4), F32),
+        vm((micro, rows, width), BF),
+        vm((micro, rows, width), F32),
+        vm((shard, ff), F32),
+        vm((shard, ff), F32),
+        vm((shard, ff), F32),
+        vm((shard, q_cols), F32),
+        vm((shard, q_cols), F32),
+        vm((shard, k_cols), F32),
+        vm((shard, k_cols), F32),
+        vm((1, shard), F32),
+        vm((1, shard), F32),
     ]
     dims = (rows, seq, width, shard, qp, kp, ff, groups)
-    out, gtok, gdown, ggate, gup, gout, gin, ggain = pl.pallas_call(
+    out, gtok, gdown, ggate, gup, gout, gq, gk, gv, one, two = pl.pallas_call(
         functools.partial(block_kernel, dims),
         out_shape=shapes,
-        in_specs=[hbm] * 10 + [vmem, smem],
-        out_specs=[hbm] * 8,
+        in_specs=[hbm] * 11 + [vmem, smem],
+        out_specs=[vmem] * 11,
         scratch_shapes=scratch,
         compiler_params=pltpu.CompilerParams(
-            collective_id=0, has_side_effects=True, vmem_limit_bytes=67_043_328
+            collective_id=0, has_side_effects=True, vmem_limit_bytes=61_600_000
         ),
         name="block",
     )(
         tokens,
         cotangent,
-        gain,
+        gain_attn,
+        gain_ffn,
         w_query,
         w_key,
         w_value,
@@ -1325,23 +1333,16 @@
         order,
         lengths,
     )
-    made = [
-        shape((1, shard), F32),
-        shape((1, shard), F32),
-        shape((shard, q_cols), F32),
-        shape((shard, k_cols), F32),
-        shape((shard, k_cols), F32),
-        shape((shard, q_cols), F32),
-    ]
-    given = [ggain, gin, gout, out, gtok, ggate, gup, gdown]
-    one, two, gq, gk, gv, gout, out, gtok, ggate, gup, gdown = pl.pallas_call(
-        functools.partial(finish_kernel, (qp, kp, shard)),
-        out_shape=made + [shape(x.shape, x.dtype) for x in given[3:]],
-        in_specs=[hbm] * 8,
+    results = [out, gtok, gdown, ggate, gup, gout, gq, gk, gv, one, two]
+    out, gtok, gdown, ggate, gup, gout, gq, gk, gv, one, two = pl.pallas_call(
+        put_out,
+        out_shape=[shape(x.shape, x.dtype) for x in results],
+        in_specs=[vmem] * 11,
         out_specs=[hbm] * 11,
-        scratch_shapes=[vm(x.shape, x.dtype) for x in given + made] + [dma((8,)), dma((11,))],
-        name="finish",
-    )(*given)
+        scratch_shapes=[dma((11,))],
+        compiler_params=pltpu.CompilerParams(vmem_limit_bytes=2**18),
+        name="put_out",
+    )(*results)
     return out, gtok, one[0], gq, gk, gv, gout.T, two[0], ggate, gup, gdown.T
 
 

time: 216 us -> 208 us (0.963)
  Pallas kernels: 212 us -> 206 us
    pallas_call x1, Pallas kernels: 207 us -> 204 us  [fused(): pl.pallas_call(functools.partial(block_kernel, dims), out_shape=shapes, i...]
    pallas_call x1, Pallas kernels: 4.66 us -> 2.3 us  [fused(): pl.pallas_call(put_out, out_shape=[shape(x.shape, x.dtype) for x in resul...]
where the time goes in v6:
time: 208 us; the launch traced here: 207 us
  Pallas kernels  206 us (99%)
    pallas_call x1, Pallas kernels, fused(): pl.pallas_call(functools.partial(block_kernel, dims), out_shape=shapes, i...  204 us

profile of v6, /device:TPU:0, one launch (start us, length us, event | category | flops | bytes accessed | tf_op | source)
XLA Modules:
  0.0 206.8 jit_solution(6515008464050494685)
XLA Ops:
  0.6 203.7 %block.1 = (bf16[2,80,1536]{2,1,0:T(8,128)(2,1)S(1)}, f32[2,80,1536]{2,1,0:T(8,128)S(1)}, f32[192,1024]{1,0:T(8,128)S(1)}, f32[192,1024]{1,0:T(8,128)S(1)}, f32[...) custom-call(bf16[2,80,1536]{2,1,0:T(8,128)(2,1)} %refs_0_.1, ...), custom_call_target="tpu_custom_call" | custom-call | tf_op jit(solution)/shard_map/block/pallas_call | solution.py:1311
  204.4 2.3 %put_out.1 = (bf16[2,80,1536]{2,1,0:T(8,128)(2,1)}, f32[2,80,1536]{2,1,0:T(8,128)}, f32[192,1024]{1,0:T(8,128)}, f32[192,1024]{1,0:T(8,128)}, f32[192,1024]{1,0:...) custom-call(bf16[2,80,1536]{2,1,0:T(8,128)(2,1)S(1)} %get-tuple-elem, ...), custom_call_target="tpu_custom_call" | custom-call | tf_op jit(solution)/shard_map/put_out/pallas_call | solution.py:1337

commit v7 on v6

--- a/solution.py
+++ b/solution.py
@@ -753,25 +753,25 @@
 
         lax.fori_loop(0, rows // 16, body, 0)
 
-    def feed(s, part):
+    def feed_forward(s, part):
         at = pl.ds(s * seq, seq)
+        one, two = pl.ds(part * 256, 256), pl.ds(ff + part * 256, 256)
+        gate = nn(n2[at, :], wu[:, one])
+        upper = nn(n2[at, :], wu[:, two])
+        sigma = 1.0 / (1.0 + jnp.exp(-gate))
+        swish = gate * sigma
+        act[at, one] = (swish * upper).astype(BF)
+        dgu[at, one] = (upper * sigma * (1.0 + gate * (1.0 - sigma))).astype(BF)
+        dgu[at, two] = swish.astype(BF)
+
+    def feed_back(s, part):
         if part == 0:
             own_here(1, s)
-
-        def body(t, carry):
-            col = al(t * 256, 256)
-            gate = nn(n2[at, :], wu[:, pl.ds(col, 256)])
-            upper = nn(n2[at, :], wu[:, pl.ds(al(ff + t * 256, 256), 256)])
-            back = nn(gf[at, :], wd[:, pl.ds(col, 256)])
-            sigma = 1.0 / (1.0 + jnp.exp(-gate))
-            swish = gate * sigma
-            act[at, pl.ds(col, 256)] = (swish * upper).astype(BF)
-            dgu[at, pl.ds(col, 256)] = (back * upper * sigma * (1.0 + gate * (1.0 - sigma))).astype(BF)
-            dgu[at, pl.ds(al(ff + t * 256, 256), 256)] = (back * swish).astype(BF)
-            return carry
-
-        count = ff // 256 // 4
-        lax.fori_loop(part * count, (part + 1) * count, body, 0)
+        at = pl.ds(s * seq, seq)
+        one, two = pl.ds(part * 256, 256), pl.ds(ff + part * 256, 256)
+        back = nn(gf[at, :], wd[:, one])
+        dgu[at, one] = (back * dgu[at, one].astype(F32)).astype(BF)
+        dgu[at, two] = (back * dgu[at, two].astype(F32)).astype(BF)
 
     def finish_out(s):
         def body(i, carry):
@@ -956,243 +956,251 @@
         tok_copy(s).start()
     pl.semaphore_wait(barrier, 3 + (z + 3) // 4 + (6 - z) // 4)
     ag(X, 0, 0)
-    prep_in()
-    ag(X, 1, 0)
-    prep_out()
-    prep_rows(0)
     prep_gain()
     w_start(0)
+    prep_in()
     w_start(1)
-    w_relayb(0)
+    prep_out()
     w_start(2)
     ag(X, 0, 1, 1)
+    w_relayb(0)
     ag(X, 0, 1, 0)
+    ag(X, 1, 0)
+    prep_rows(0)
+    w_relayb(1)
     w_relaya(1)
+    ag(X, 0, 2, 0)
     w_diag(0)
-    ag(X, 1, 1, 0)
-    ag(X, 0, 2, 0)
-    w_relayb(1)
+    w_relaya(0)
+    ag(X, 0, 2, 1)
     ag(COT, 0, 0)
-    w_relaya(0)
+    ag(X, 1, 1, 1)
+    prep_rows(1)
     w_done(0)
     gain_rows()
     norm1(0, 1)
+    w_relayb(2)
     norm1(0, 0)
-    w_relayb(2)
-    ag(X, 0, 2, 1)
-    ag(COT, 1, 0)
-    ag(X, 1, 1, 1)
-    norm1(1, 1)
-    w_start(3)
-    norm1(1, 0)
-    prep_rows(1)
-    w_start(4)
+    w_diag(1)
     norm1(0, 2)
-    w_diag(1)
-    ag(COT, 0, 1, 1)
     ag(X, 0, 3, 1)
-    w_relaya(2)
-    w_diag(2)
     ag(X, 0, 3, 0)
     norm1(0, 3)
+    w_relaya(2)
+    ag(X, 1, 1, 0)
     w_done(1)
     project(0)
+    w_diag(2)
+    w_start(3)
     attend(0, 0)
     attend(0, 1)
     w_done(2)
     spread(0, pa, ob, wo, 512)
     rs(BR, 0, 0, 1)
+    rs(BR, 0, 0, 0)
     ag(COT, 0, 1, 0)
+    ag(X, 1, 2, 1)
+    w_start(4)
+    ag(COT, 0, 1, 1)
     rs(BR, 0, 1, 1)
+    norm1(1, 0)
     ag(X, 1, 2, 0)
-    rs(BR, 0, 0, 0)
+    ag(COT, 0, 2, 0)
     rs(BR, 0, 1, 0)
-    w_start(5)
-    ag(X, 1, 2, 1)
-    w_relaya(4)
+    norm1(1, 2)
+    norm1(1, 1)
     rs(BR, 0, 2, 1)
+    ag(X, 1, 3, 1)
+    ag(X, 1, 3, 0)
+    norm1(1, 3)
     rs(BR, 0, 2, 0)
-    ag(COT, 0, 2, 0)
-    norm1(1, 2)
-    ag(X, 1, 3, 0)
-    ag(X, 1, 3, 1)
     w_relayb(3)
-    norm1(1, 3)
     project(1)
     attend(1, 0)
+    w_start(5)
+    attend(1, 1)
+    ag(COT, 0, 2, 1)
+    spread(1, pa, ob, wo, 512)
+    rs(BR, 1, 0, 0)
+    rs(BR, 1, 0, 1)
+    fin_br(0)
+    rs_sent(BR, 0)
+    rs(BR, 1, 1, 0)
+    ag(N2, 0, 1, 0)
     w_relaya(3)
-    fin_br(0)
+    w_relaya(4)
+    rs(BR, 1, 1, 1)
     w_relayb(4)
-    zag_sent(X, 0)
-    ag(COT, 0, 2, 1)
+    ag(N2, 0, 1, 1)
+    ag(COT, 0, 3, 1)
+    rs(BR, 1, 2, 0)
+    rs(BR, 1, 2, 1)
+    w_relayb(5)
+    ag(N2, 0, 2, 1)
     w_diag(3)
-    attend(1, 1)
-    spread(1, pa, ob, wo, 512)
-    rs_sent(BR, 0)
-    ag(N2, 0, 1, 1)
-    rs(BR, 1, 0, 1)
-    ag(N2, 0, 1, 0)
-    w_relayb(5)
-    rs(BR, 1, 0, 0)
-    rs(BR, 1, 1, 1)
+    ag(N2, 0, 2, 0)
+    ag(COT, 1, 0)
+    w_diag(4)
+    fin_br(1)
+    ag(N2, 0, 3, 0)
+    w_done(4)
+    w_relaya(5)
+    ag(N2, 0, 3, 1)
     w_done(3)
-    ag(N2, 0, 2, 0)
-    rs(BR, 1, 1, 0)
-    ag(N2, 0, 2, 1)
-    w_relaya(5)
-    rs(BR, 1, 2, 0)
-    w_diag(4)
-    rs(BR, 1, 2, 1)
+    feed_forward(0, 0)
     w_diag(5)
+    rs_sent(BR, 1)
+    feed_forward(0, 1)
+    feed_forward(0, 2)
+    feed_forward(0, 3)
     w_done(5)
+    spread(0, pb, act, wd, 512)
+    rs(FFN, 0, 0, 1)
+    ag(COT, 1, 1, 1)
+    ag(COT, 1, 1, 0)
+    rs(FFN, 0, 0, 0)
     ag(COT, 0, 3, 0)
-    ag(COT, 1, 1, 1)
-    w_done(4)
-    ag(COT, 1, 1, 0)
-    ag(N2, 0, 3, 1)
-    ag(N2, 0, 3, 0)
-    ag(COT, 0, 3, 1)
-    feed(0, 0)
-    feed(0, 1)
-    feed(0, 2)
-    fin_br(1)
-    feed(0, 3)
+    feed_back(0, 0)
+    feed_back(0, 1)
+    feed_back(0, 2)
+    feed_back(0, 3)
     spread(0, pa, dgu, wu, 256, 0, 2)
     spread(0, pa, dgu, wu, 256, 1, 2)
-    ag(COT, 1, 2, 1)
+    rs(DN2, 0, 0, 0)
+    zag_sent(X, 1)
+    ag(N2, 1, 1, 1)
+    ag(N2, 1, 1, 0)
     rs(DN2, 0, 0, 1)
-    rs(DN2, 0, 0, 0)
-    spread(0, pb, act, wd, 512)
-    ag(N2, 1, 1, 0)
+    clean(0)
+    rs(DN2, 0, 1, 1)
+    rs(FFN, 0, 1, 1)
     rs(DN2, 0, 1, 0)
-    ag(COT, 1, 3, 1)
-    rs(FFN, 0, 0, 0)
-    ag(N2, 1, 1, 1)
     ag(N2, 1, 2, 1)
-    rs_sent(BR, 1)
-    ag(COT, 1, 2, 0)
-    rs(DN2, 0, 1, 1)
-    ag(N2, 1, 2, 0)
-    rs(FFN, 0, 0, 1)
-    rs(DN2, 0, 2, 0)
-    rs(DN2, 0, 2, 1)
-    ag(N2, 1, 3, 0)
-    zag_sent(X, 1)
-    rs(FFN, 0, 1, 1)
     rs(FFN, 0, 1, 0)
     ag(N2, 1, 3, 1)
+    ag(N2, 1, 2, 0)
+    ag(N2, 1, 3, 0)
+    ag(COT, 1, 2, 1)
+    feed_forward(1, 0)
+    feed_forward(1, 1)
+    feed_forward(1, 2)
+    ag(COT, 1, 2, 0)
+    zag_sent(X, 0)
+    rs(DN2, 0, 2, 0)
+    feed_forward(1, 3)
+    rs(DN2, 0, 2, 1)
     ag(COT, 1, 3, 0)
-    feed(1, 0)
-    feed(1, 1)
-    feed(1, 2)
-    feed(1, 3)
-    fin_dn2(0)
+    ag(COT, 1, 3, 1)
+    feed_back(1, 0)
+    feed_back(1, 1)
+    feed_back(1, 2)
+    feed_back(1, 3)
     spread(1, pa, dgu, wu, 256, 0, 2)
     spread(1, pa, dgu, wu, 256, 1, 2)
+    rs(DN2, 1, 0, 1)
     rs(DN2, 1, 0, 0)
     g_compute(0, 0)
-    rs(DN2, 1, 0, 1)
     g_compute(0, 1)
-    ag(GH, 0, 1, 0)
-    ag(GH, 0, 1, 1)
+    fin_dn2(0)
     g_first(0)
     g_compute(0, 2)
     g_compute(0, 3)
+    g_firstb(0)
+    rs(DN2, 1, 1, 0)
     rs(DN2, 1, 1, 1)
-    rs(DN2, 1, 1, 0)
-    ag(GH, 0, 2, 1)
-    ag(GH, 0, 2, 0)
     g_compute(1, 0)
-    g_firstb(0)
+    g_compute(1, 1)
+    g_second(0)
+    ag(GH, 0, 1, 0)
+    ag(GH, 0, 1, 1)
+    g_compute(1, 2)
     rs(DN2, 1, 2, 0)
     rs(DN2, 1, 2, 1)
     spread(1, pb, act, wd, 512)
     rs(FFN, 1, 0, 1)
+    ag(GH, 0, 2, 0)
     rs(FFN, 1, 0, 0)
+    ag(GH, 0, 2, 1)
+    g_first(1)
+    g_firstb(1)
+    fin_dn2(1)
+    g_finish(0)
     rs_sent(DN2, 0)
-    g_second(0)
-    g_first(1)
-    g_compute(1, 1)
-    g_compute(1, 2)
+    g_compute(1, 3)
+    g_compute(2, 0)
+    ag(GH, 0, 3, 0)
+    g_second(1)
     ag(GH, 0, 3, 1)
-    ag(GH, 0, 3, 0)
-    fin_dn2(1)
-    g_firstb(1)
     grad_heads(0)
     attend_back(0)
-    rs_sent(DN2, 1)
+    ag(GH, 1, 1, 0)
+    rs(FFN, 1, 1, 0)
+    g_first(2)
+    ag(GH, 1, 1, 1)
+    rs(FFN, 1, 1, 1)
+    g_compute(2, 1)
     spread_gain(0)
     rs(DN1, 0, 0, 0)
-    ag(GH, 1, 1, 1)
+    g_compute(2, 2)
+    ag(GH, 1, 2, 1)
     rs(DN1, 0, 0, 1)
-    ag(GH, 1, 1, 0)
-    g_second(1)
-    rs(FFN, 1, 1, 0)
-    g_finish(0)
-    g_compute(1, 3)
-    g_compute(2, 0)
-    ag(GH, 1, 2, 1)
-    rs(FFN, 1, 1, 1)
-    g_first(2)
-    rs(FFN, 0, 2, 1)
+    g_firstb(2)
     ag(GH, 1, 2, 0)
     rs(FFN, 0, 2, 0)
-    g_compute(2, 1)
-    g_compute(2, 2)
+    g_finish(1)
     g_compute(2, 3)
+    rs(FFN, 1, 2, 1)
+    g_second(2)
+    ag(GH, 1, 3, 0)
+    ag(GH, 1, 3, 1)
+    rs(FFN, 0, 2, 1)
+    g_compute(3, 0)
+    g_compute(3, 1)
+    rs(FFN, 1, 2, 0)
+    grad_heads(1)
+    attend_back(1)
+    g_first(3)
+    rs_sent(DN2, 1)
+    spread_gain(1)
+    rs(DN1, 1, 0, 1)
+    e_line(0)
+    rs(DN1, 1, 0, 0)
+    rs(DN1, 0, 1, 0)
+    g_compute(3, 2)
     rs(DN1, 0, 1, 1)
-    g_firstb(2)
-    ag(GH, 1, 3, 0)
-    rs(FFN, 1, 2, 0)
-    ag(GH, 1, 3, 1)
-    grad_heads(1)
-    g_second(2)
-    clean(3)
-    attend_back(1)
-    spread_gain(1)
-    rs(DN1, 1, 0, 0)
-    e_line(0)
-    g_finish(1)
-    g_compute(3, 0)
-    rs(DN1, 1, 0, 1)
-    rs(FFN, 1, 2, 1)
-    rs(DN1, 0, 1, 0)
-    g_compute(3, 1)
-    g_compute(3, 2)
     g_compute(3, 3)
-    g_first(3)
-    clean(4)
-    fin_ffn(0)
     g_firstb(3)
-    clean(0)
-    clean(1)
-    clean(2)
     g_finish(2)
     g_compute(4, 0)
+    g_second(3)
+    g_first(4)
+    rs(DN1, 1, 1, 1)
     g_compute(4, 1)
     e_line(1)
-    g_second(3)
     g_compute(4, 2)
-    rs(DN1, 1, 1, 1)
     rs(DN1, 1, 1, 0)
+    clean(2)
+    clean(5)
+    g_firstb(4)
+    fin_ffn(0)
     e_line(2)
-    g_first(4)
+    clean(3)
+    rs(DN1, 0, 2, 0)
+    g_finish(3)
+    rs(DN1, 0, 2, 1)
     e_line(3)
-    rs(DN1, 0, 2, 1)
-    g_finish(3)
-    rs(DN1, 0, 2, 0)
     e_plane(0)
-    g_firstb(4)
+    rs(DN1, 1, 2, 0)
+    g_second(4)
     g_compute(4, 3)
+    fin_ffn(1)
     rs(DN1, 1, 2, 1)
-    g_second(4)
-    rs(DN1, 1, 2, 0)
     fin_dn1(0)
+    clean(1)
+    clean(4)
     e_plane(1)
-    clean(5)
-    fin_ffn(1)
+    g_finish(4)
     e_plane(2)
-    g_finish(4)
     fin_dn1(1)
     for s in (0, 1):
         rs_sent(DN1, s)

time: 208 us -> 207 us (level)
  no operation moved by 1% of the time
where the time goes in v7:
time: 207 us
  Pallas kernels  206 us (100%)
    pallas_call x1, Pallas kernels, fused(): pl.pallas_call(functools.partial(block_kernel, dims), out_shape=shapes, i...  204 us

profile of v7, /device:TPU:0, one launch (start us, length us, event | category | flops | bytes accessed | tf_op | source)
XLA Modules:
  0.0 206.8 jit_solution(4781664481120191493)
XLA Ops:
  0.6 203.7 %block.1 = (bf16[2,80,1536]{2,1,0:T(8,128)(2,1)S(1)}, f32[2,80,1536]{2,1,0:T(8,128)S(1)}, f32[192,1024]{1,0:T(8,128)S(1)}, f32[192,1024]{1,0:T(8,128)S(1)}, f32[...) custom-call(bf16[2,80,1536]{2,1,0:T(8,128)(2,1)} %refs_0_.1, ...), custom_call_target="tpu_custom_call" | custom-call | tf_op jit(solution)/shard_map/block/pallas_call | solution.py:1319
  204.4 2.3 %put_out.1 = (bf16[2,80,1536]{2,1,0:T(8,128)(2,1)}, f32[2,80,1536]{2,1,0:T(8,128)}, f32[192,1024]{1,0:T(8,128)}, f32[192,1024]{1,0:T(8,128)}, f32[192,1024]{1,0:...) custom-call(bf16[2,80,1536]{2,1,0:T(8,128)(2,1)S(1)} %get-tuple-elem, ...), custom_call_target="tpu_custom_call" | custom-call | tf_op jit(solution)/shard_map/put_out/pallas_call | solution.py:1345

commit v8 on v7

--- a/solution.py
+++ b/solution.py
@@ -271,7 +271,7 @@
     chip_own, chip_a, chip_b, chip_d = d // 2, aa // 2, bb // 2, dd // 2
     chip_x, chip_y = near_x // 2, near_y // 2
     own = z * rows
-    half = width
+    half = width // 2
     zdev = {"tensor": z + 1}, {"tensor": z - 1}
 
     def rcopy(src, dst, ssem, rsem, dev):
@@ -419,7 +419,7 @@
     def zcopy(u, s, k, way, h, i, src=None):
         blk = zblk(u, s, i, h)
         return rcopy(
-            blk if src is None else src, blk, zsend.at[u, s], zrecv.at[u % 3, s, way, k], zdev[way]
+            blk if src is None else src, blk, zsend.at[u, s], zrecv.at[u % 3, s, way, k, h], zdev[way]
         )
 
     def zag_send(u, s, k, way, h):
@@ -434,23 +434,24 @@
     def own_copy(u, s):
         return pltpu.make_async_copy(zhbm[u].at[s], zblk(u, s, z), lsem.at[2 + 2 * u + s])
 
-    def ag(u, s, t, way=None, h=0):
+    def ag(u, s, t, way=None):
         if t == 0:
             if zhbm[u] is not None:
                 own_copy(u, s).start()
-            for part in (0,):
+            for part in (0, 1):
                 for side in (0, 1):
                     zag_send(u, s, 0, side, part)
             return
         i = z - t if way == 0 else z + t
         go = (i >= 0) if way == 0 else (i <= 3)
 
-        @pl.when(go)
-        def _():
-            zcopy(u, s, t - 1, way, h, i).wait_recv()
-
-        if t < 3:
-            zag_send(u, s, t, way, h)
+        for h in (0, 1):
+            @pl.when(go)
+            def _():
+                zcopy(u, s, t - 1, way, h, i).wait_recv()
+
+            if t < 3:
+                zag_send(u, s, t, way, h)
 
     def own_here(u, s):
         own_copy(u, s).wait()
@@ -458,7 +459,7 @@
     def zag_sent(u, s):
         def sent(count):
             part = zfull[u].at[pl.ds(0, count * rows)]
-            rcopy(part, part, zsend.at[u, s], zrecv.at[u % 3, s, 0, 0], zdev[0]).wait_send()
+            rcopy(part, part, zsend.at[u, s], zrecv.at[u % 3, s, 0, 0, 0], zdev[0]).wait_send()
 
         @pl.when((z == 0) | (z == 3))
         def _():
@@ -477,7 +478,7 @@
             zpart[u].at[pl.ds(al(s * seq + dest * rows, 16), rows), cut],
             zgot[u].at[s, way, t, :, cut],
             rsend.at[u, s],
-            rrecv.at[1 if u == 1 else 0, s, way, t],
+            rrecv.at[1 if u == 1 else 0, s, way, t, h],
             zdev[way],
         )
 
@@ -490,19 +491,20 @@
 
         lax.fori_loop(0, rows // 16, body, 0)
 
-    def rs(u, s, t, way, h=0):
+    def rs(u, s, t, way):
         from_end = z if way == 0 else 3 - z
         dest = 3 + z - t if way == 0 else t - from_end
 
         @pl.when(from_end <= t)
         def _():
-            if t > 0:
-                @pl.when(from_end > 0)
-                def _():
-                    rs_copy(u, s, way, t - 1, z, h).wait_recv()
-                    rs_add(u, s, way, t - 1, zpart[u], s * seq + dest * rows, pl.ds(h * half, half))
-
-            rs_copy(u, s, way, t, dest, h).start()
+            for h in (0, 1):
+                if t > 0:
+                    @pl.when(from_end > 0)
+                    def _():
+                        rs_copy(u, s, way, t - 1, z, h).wait_recv()
+                        rs_add(u, s, way, t - 1, zpart[u], s * seq + dest * rows, pl.ds(h * half, half))
+
+                rs_copy(u, s, way, t, dest, h).start()
 
     def rs_final(u, s):
         def first(i, carry):
@@ -516,13 +518,13 @@
 
             @pl.when(from_end > 0)
             def _():
-                for h in (0,):
+                for h in (0, 1):
                     rs_copy(u, s, way, 2, z, h).wait_recv()
                 rs_add(u, s, way, 2, acc, 0, pl.ds(0, width))
 
     def rs_sent(u, s):
         part = zpart[u].at[pl.ds(0, 3 * rows)]
-        rcopy(part, part, rsend.at[u, s], rrecv.at[0, s, 0, 0], zdev[0]).wait_send()
+        rcopy(part, part, rsend.at[u, s], rrecv.at[0, s, 0, 0, 0], zdev[0]).wait_send()
 
     gunits = (
         (gf, act, 0, ff),
@@ -1287,9 +1289,9 @@
         dma((6,)),
         dma((6, 4)),
         dma((4, 2)),
-        dma((3, 2, 2, 3)),
+        dma((3, 2, 2, 3, 2)),
         dma((4, 2)),
-        dma((2, 2, 2, 3)),
+        dma((2, 2, 2, 3, 2)),
         dma((2,)),
         dma((2, 7)),
         dma((2,)),

time: 207 us -> 205 us (level)
  Pallas kernels: 206 us -> 203 us
    pallas_call x1, Pallas kernels: 204 us -> 201 us  [fused(): pl.pallas_call(functools.partial(block_kernel, dims), out_shape=shapes, i...]
where the time goes in v8:
time: 205 us; the launch traced here: 204 us
  Pallas kernels  203 us (99%)
    pallas_call x1, Pallas kernels, fused(): pl.pallas_call(functools.partial(block_kernel, dims), out_shape=shapes, i...  201 us

profile of v8, /device:TPU:0, one launch (start us, length us, event | category | flops | bytes accessed | tf_op | source)
XLA Modules:
  0.0 204.1 jit_solution(7450162640085051360)
XLA Ops:
  0.6 201.0 %block.1 = (bf16[2,80,1536]{2,1,0:T(8,128)(2,1)S(1)}, f32[2,80,1536]{2,1,0:T(8,128)S(1)}, f32[192,1024]{1,0:T(8,128)S(1)}, f32[192,1024]{1,0:T(8,128)S(1)}, f32[...) custom-call(bf16[2,80,1536]{2,1,0:T(8,128)(2,1)} %refs_0_.1, ...), custom_call_target="tpu_custom_call" | custom-call | tf_op jit(solution)/shard_map/block/pallas_call | solution.py:1321
  201.6 2.3 %put_out.1 = (bf16[2,80,1536]{2,1,0:T(8,128)(2,1)}, f32[2,80,1536]{2,1,0:T(8,128)}, f32[192,1024]{1,0:T(8,128)}, f32[192,1024]{1,0:T(8,128)}, f32[192,1024]{1,0:...) custom-call(bf16[2,80,1536]{2,1,0:T(8,128)(2,1)S(1)} %get-tuple-elem, ...), custom_call_target="tpu_custom_call" | custom-call | tf_op jit(solution)/shard_map/put_out/pallas_call | solution.py:1347

commit v9 on v8

--- a/solution.py
+++ b/solution.py
@@ -419,7 +419,7 @@
     def zcopy(u, s, k, way, h, i, src=None):
         blk = zblk(u, s, i, h)
         return rcopy(
-            blk if src is None else src, blk, zsend.at[u, s], zrecv.at[u % 3, s, way, k, h], zdev[way]
+            blk if src is None else src, blk, zsend.at[u, s], zrecv.at[1 if u == 1 else 0, s, way, k, h], zdev[way]
         )
 
     def zag_send(u, s, k, way, h):
@@ -459,7 +459,7 @@
     def zag_sent(u, s):
         def sent(count):
             part = zfull[u].at[pl.ds(0, count * rows)]
-            rcopy(part, part, zsend.at[u, s], zrecv.at[u % 3, s, 0, 0, 0], zdev[0]).wait_send()
+            rcopy(part, part, zsend.at[u, s], zrecv.at[1 if u == 1 else 0, s, 0, 0, 0], zdev[0]).wait_send()
 
         @pl.when((z == 0) | (z == 3))
         def _():
@@ -1289,7 +1289,7 @@
         dma((6,)),
         dma((6, 4)),
         dma((4, 2)),
-        dma((3, 2, 2, 3, 2)),
+        dma((2, 2, 2, 3, 2)),
         dma((4, 2)),
         dma((2, 2, 2, 3, 2)),
         dma((2,)),

time: 205 us -> 204 us (level)
  no operation moved by 1% of the time
where the time goes in v9:
time: 204 us
  Pallas kernels  203 us (100%)
    pallas_call x1, Pallas kernels, fused(): pl.pallas_call(functools.partial(block_kernel, dims), out_shape=shapes, i...  201 us

profile of v9, /device:TPU:0, one launch (start us, length us, event | category | flops | bytes accessed | tf_op | source)
XLA Modules:
  0.0 203.9 jit_solution(7952523667249768766)
XLA Ops:
  0.6 200.8 %block.1 = (bf16[2,80,1536]{2,1,0:T(8,128)(2,1)S(1)}, f32[2,80,1536]{2,1,0:T(8,128)S(1)}, f32[192,1024]{1,0:T(8,128)S(1)}, f32[192,1024]{1,0:T(8,128)S(1)}, f32[...) custom-call(bf16[2,80,1536]{2,1,0:T(8,128)(2,1)} %refs_0_.1, ...), custom_call_target="tpu_custom_call" | custom-call | tf_op jit(solution)/shard_map/block/pallas_call | solution.py:1321
  201.4 2.3 %put_out.1 = (bf16[2,80,1536]{2,1,0:T(8,128)(2,1)}, f32[2,80,1536]{2,1,0:T(8,128)}, f32[192,1024]{1,0:T(8,128)}, f32[192,1024]{1,0:T(8,128)}, f32[192,1024]{1,0:...) custom-call(bf16[2,80,1536]{2,1,0:T(8,128)(2,1)S(1)} %get-tuple-elem, ...), custom_call_target="tpu_custom_call" | custom-call | tf_op jit(solution)/shard_map/put_out/pallas_call | solution.py:1347
